TPU v7x, 32 devices: a whole 2x2x4 slice. The times are simulated.
32 devices in a mesh: blk: 4 (over x, core), fsdp: 8 (over z, y).
Axes of the slice: x: 2, y: 2, z: 4, core: 2. Of those that a mesh axis runs over, the one named last changes fastest.
Arguments:
- normed: bfloat16 [8, 1024, 2048], P('fsdp', 'blk'), may hold values from -128 to 128
- picked: int32 [8, 64], P('fsdp', 'blk'), may hold values from 0 to 255, as said below
- queries: bfloat16 [8, 64, 2048], P('fsdp', 'blk'), may hold values from -9 to 9
- key_states: bfloat16 [8, 1024, 512], P('fsdp', 'blk'), may hold values from -4 to 4
- values: bfloat16 [8, 1024, 512], P('fsdp', 'blk'), may hold values from -6 to 6
- cotangent: bfloat16 [8, 64, 2048], P('fsdp', 'blk'), may hold values from -16 to 16
- hessian: float32 [2048, 512], P(('blk', 'fsdp')), may hold values from 0.1 to 1
Outputs:
- hessian_next: float32 [2048, 512], P(('blk', 'fsdp'))
Inputs may be any that keep to these rules, and one draw needn't show every extreme that they name: `picked`: ascending and distinct within each block of 16 rows.
All inputs are finite; a program needn't handle non-finite values.
Results may differ from a plain program's by a relative error of at most 0.007.
Values may be sent and summed in bfloat16 or wider, within the bound.
No kernel may reach another device: no remote copies, remote signals or barrier semaphores. Data moves between devices by JAX's collectives and lax.ppermute only.
A program may use at most 64 MiB of HBM per device.

v0:
```python
import jax
import jax.numpy as jnp
from jax import lax
from jax.sharding import PartitionSpec as P

HEADS = 16
KV_HEADS = 4
HEAD_DIM = 128


decay_rate = 0.99
rope_base = 500000.0
neg_large = -1e30


def shifted(block, axis, distance):
    devices = range(lax.axis_size(axis))
    route = [((i - distance) % len(devices), i) for i in devices]
    return lax.ppermute(block, axis, route)


def rotate_back(gradient, positions):
    half_dim = gradient.shape[-1] // 2
    exponent = jnp.arange(half_dim, dtype=jnp.float32) * (2.0 / gradient.shape[-1])
    frequency = jnp.power(jnp.float32(rope_base), -exponent)
    angles = positions.astype(jnp.float32)[:, None] * frequency[None, :]
    cosine = jnp.cos(angles)[:, None, :]
    sine_part = jnp.sin(angles)[:, None, :]
    leading = gradient[..., :half_dim]
    trailing = gradient[..., half_dim:]
    return jnp.concatenate(
        [leading * cosine + trailing * sine_part, trailing * cosine - leading * sine_part], axis=-1
    )


def attend(running, query_part, key_block, value_block, visible):
    running_max, running_sum, weighted = running
    scores = jnp.einsum(
        "qgrd,kgd->grqk", query_part, key_block, preferred_element_type=jnp.float32
    ) * HEAD_DIM ** (-0.5)
    scores = jnp.where(visible[None, None], scores, neg_large)
    new_max = jnp.maximum(running_max, jnp.max(scores, axis=-1))
    shrink = jnp.exp(running_max - new_max)
    exponent = jnp.exp(scores - new_max[..., None])
    running_sum = running_sum * shrink + jnp.sum(exponent, axis=-1)
    update = jnp.einsum(
        "grqk,kgd->grqd",
        exponent.astype(jnp.bfloat16),
        value_block,
        preferred_element_type=jnp.float32,
    )
    return (new_max, running_sum, weighted * shrink[..., None] + update)


def key_gradient(query_part, cot_part, log_norm, row_dot, key_block, value_block, visible):
    scaling = HEAD_DIM ** (-0.5)
    scores = (
        jnp.einsum("qgrd,kgd->grqk", query_part, key_block, preferred_element_type=jnp.float32)
        * scaling
    )
    scores = jnp.where(visible[None, None], scores, neg_large)
    attention = jnp.exp(scores - log_norm[..., None])
    grad_weights = jnp.einsum(
        "qgrd,kgd->grqk", cot_part, value_block, preferred_element_type=jnp.float32
    )
    grad_scores = (attention * (grad_weights - row_dot[..., None])).astype(jnp.bfloat16)
    return (
        jnp.einsum("grqk,qgrd->kgd", grad_scores, query_part, preferred_element_type=jnp.float32)
        * scaling
    )


def pass_queries(blocks):
    return tuple(shifted((blocks[0], blocks[1]), "blk", 1))


def pass_state(state):
    return tuple(shifted((state[0], state[1], state[2]), "blk", 1))


def local(normed, picked, queries, key_states, values, cotangent, hessian):
    rows = queries.shape[1]
    tokens = key_states.shape[1]
    groups = key_states.shape[2] // HEAD_DIM
    repeat_count = HEADS // KV_HEADS
    cycle_size = lax.axis_size("blk")
    cycle_place = lax.axis_index("blk")
    query_all = queries[0].reshape(rows, groups, repeat_count, HEAD_DIM)
    cot_all = cotangent[0].reshape(rows, groups, repeat_count, HEAD_DIM)
    key_all = key_states[0].reshape(tokens, groups, HEAD_DIM)
    value_all = values[0].reshape(tokens, groups, HEAD_DIM)
    own_offsets = picked[0]
    key_ids = lax.broadcasted_iota(jnp.int32, (tokens,), 0)

    def visible_mask(held):
        reach = (held - cycle_place) * tokens + own_offsets
        return key_ids[None, :] <= reach[:, None]

    halves = [(1, 0, groups)]
    first_blocks, first_states, first_stores = ([], [], [])
    step_dir, first_group, end_group = halves[0]
    group_span = end_group - first_group
    starting = (
        jnp.full((group_span, repeat_count, rows), neg_large, jnp.float32),
        jnp.zeros((group_span, repeat_count, rows), jnp.float32),
        jnp.zeros((group_span, repeat_count, rows, HEAD_DIM), jnp.float32),
    )
    first_states.append(attend(starting, query_all, key_all, value_all, visible_mask(cycle_place)))
    first_blocks.append((query_all, cot_all))
    empty_store = jnp.zeros((cycle_size,) + query_all.shape, jnp.bfloat16)
    first_stores.append(
        (
            lax.dynamic_update_index_in_dim(empty_store, query_all, cycle_place, 0),
            lax.dynamic_update_index_in_dim(empty_store, cot_all, cycle_place, 0),
        )
    )

    def forward_step(cycle_step, loop_state):
        blocks, states, stores = loop_state
        next_blocks, next_states, next_stores = ([], [], [])
        for number, (step_dir, first_group, end_group) in enumerate(halves):
            moved = pass_queries(blocks[number])
            arrived = pass_state(states[number])
            held = (cycle_place - step_dir * cycle_step) % cycle_size
            key_part = key_all
            value_part = value_all

            def forward_compute(
                running, moved=moved, held=held, key_part=key_part, value_part=value_part
            ):
                return attend(running, moved[0], key_part, value_part, visible_mask(held))

            next_states.append(
                lax.cond(held >= cycle_place, forward_compute, lambda running: running, arrived)
            )
            next_blocks.append(moved)
            next_stores.append(
                (
                    lax.dynamic_update_index_in_dim(stores[number][0], moved[0], held, 0),
                    lax.dynamic_update_index_in_dim(stores[number][1], moved[1], held, 0),
                )
            )
        return (tuple(next_blocks), tuple(next_states), tuple(next_stores))

    blocks, states, stores = lax.fori_loop(
        1, cycle_size, forward_step, (tuple(first_blocks), tuple(first_states), tuple(first_stores))
    )
    stats = []
    for number, (step_dir, first_group, end_group) in enumerate(halves):
        running_max, running_sum, weighted = states[number]
        attended = weighted / running_sum[..., None]
        log_norm = running_max + jnp.log(running_sum)
        row_dot = jnp.einsum("qgrd,grqd->grq", blocks[number][1].astype(jnp.float32), attended)
        stats.append(log_norm[None])
        stats.append(row_dot[None])
    gathered = lax.all_gather(tuple(stats), "blk", axis=0, tiled=True)
    key_grads = []
    for number, (step_dir, first_group, end_group) in enumerate(halves):
        key_part = key_all
        value_part = value_all
        norms_all = gathered[2 * number]
        dots_all = gathered[2 * number + 1]
        query_store, cot_store = stores[number]

        def backward_step(
            slot,
            total,
            step_dir=step_dir,
            key_part=key_part,
            value_part=value_part,
            norms_all=norms_all,
            dots_all=dots_all,
            query_store=query_store,
            cot_store=cot_store,
        ):

            def backward_compute():
                source = (slot - step_dir) % cycle_size
                return key_gradient(
                    lax.dynamic_index_in_dim(query_store, slot, 0, keepdims=False),
                    lax.dynamic_index_in_dim(cot_store, slot, 0, keepdims=False),
                    lax.dynamic_index_in_dim(norms_all, source, 0, keepdims=False),
                    lax.dynamic_index_in_dim(dots_all, source, 0, keepdims=False),
                    key_part,
                    value_part,
                    visible_mask(slot),
                )

            def nothing():
                return jnp.zeros_like(total)

            return total + lax.cond(slot >= cycle_place, backward_compute, nothing)

        zeros_grad = jnp.zeros((tokens, end_group - first_group, HEAD_DIM), jnp.float32)
        key_grads.append(lax.fori_loop(0, cycle_size, backward_step, zeros_grad))
    gradient = key_grads[0]
    unrotated = (
        rotate_back(gradient, cycle_place * tokens + key_ids)
        .astype(jnp.bfloat16)
        .reshape(tokens, groups * HEAD_DIM)
    )
    features = normed[0]
    local_grad = lax.dot_general(
        features, unrotated, (((0,), (0,)), ((), ())), preferred_element_type=jnp.float32
    )
    summed_rows = lax.psum_scatter(local_grad, ("blk", "fsdp"), scatter_dimension=0, tiled=True)
    batch_count = lax.axis_size("fsdp")
    return decay_rate * hessian + (1.0 - decay_rate) * summed_rows * summed_rows / batch_count


def solution(mesh):
    placed = (
        P("fsdp", "blk", None),
        P("fsdp", "blk"),
        P("fsdp", "blk", None),
        P("fsdp", "blk", None),
        P("fsdp", "blk", None),
        P("fsdp", "blk", None),
        P(("blk", "fsdp"), None),
    )
    return jax.shard_map(
        local, mesh=mesh, in_specs=placed, out_specs=P(("blk", "fsdp"), None), check_vma=False
    )
```

profile of v0, /device:TPU:0, one launch (start us, length us, event | category | flops | bytes accessed | tf_op | source)
XLA Modules:
  0.0 216.7 jit_solution(174343914285545888)
XLA Ops:
  6.6 1.0 reshape_squeeze.12
  7.5 0.9 broadcast_in_dim.95
  8.4 0.9 broadcast_in_dim.96
  9.3 0.9 reshape_squeeze.13
  10.2 0.7 iota_compare_fusion
  10.9 1.1 copy.44
  12.0 0.3 fusion.48
  12.7 1.1 copy.47
  14.6 24.6 %while.42 = (s32[]{:T(128)}, bf16[16,4,4,128]{3,0,2,1:T(8,128)(2,1)S(1)}, bf16[16,4,4,128]{3,2,1,0:T(4,128)(2,1)S(1)}, f32[4,4,16]{2,1,0:T(4,128)S(1)}, f32[4,4,...) while((s32[]{:T(128)}, ...), condition=%wide.region_7.8_spmd.clone, body=%wide.region_2.7_spmd.clone.sunk | while | flops 34083360 | bytes 3513202 | solution.py:145
  14.6 0.5 collective-permute-start.1
  15.1 2.6 %collective-permute-start.3 = (f32[4,4,16]{2,1,0:T(4,128)S(1)}, f32[4,4,16]{2,1,0:T(4,128)S(1)}, u32[]{:S(2)}, u32[]{:S(2)}) collective-permute-start(f32[4,4,16]{2,1,0:T(4,128)S(1)} %get-tuple-element.981), channel_id=1, source_target_pairs={{24,0},{0,8},{8,16},{16,24},{25,1},{1,9},{9,17},{17,25},{26,2},{2,... | collective-permute-start | bytes 3080 | tf_op jit(solution)/shard_map/while/body/eval_jaxpr/ppermute | solution.py:19
  17.9 1.1 collective-permute-done.1
  19.0 2.5 %collective-permute-done = bf16[16,4,4,128]{3,0,2,1:T(8,128)(2,1)S(1)} collective-permute-done((bf16[16,4,4,128]{3,0,2,1:T(8,128)(2,1)S(1)}, bf16[16,4,4,128]{3,0,2,1:T(8,128)(2,1)S(1)}, u32[]{:S(2)}, u32[]{:S(2)}) %collective-permute-start) | collective-permute-done | bytes 65568 | tf_op jit(solution)/shard_map/while/body/eval_jaxpr/ppermute | solution.py:19
  21.6 1.3 collective-permute-done.4
  22.9 0.9 conditional.6
  23.0 0.3 fusion.47
  23.5 0.3 convolution_add_fusion
  23.9 0.5 collective-permute-start.3
  24.5 1.6 collective-permute-start
  26.2 1.4 collective-permute-done.1
  27.6 0.8 collective-permute-done
  28.5 2.0 collective-permute-done.4
  30.6 0.9 conditional.6
  30.6 0.3 fusion.47
  31.2 0.3 convolution_add_fusion
  31.7 2.1 collective-permute-start
  33.9 1.4 collective-permute-done.1
  35.3 0.8 collective-permute-done
  36.2 2.0 collective-permute-done.4
  38.2 0.9 conditional.6
  38.3 0.3 fusion.47
  38.8 0.3 convolution_add_fusion
  39.2 5.2 %all-gather = f32[16,4,16]{2,1,0:T(4,128)S(1)} all-gather(f32[4,4,16]{2,1,0:T(4,128)S(1)} %bitcast.127), channel_id=2, replica_groups=mesh['blk'=4,'fsdp'=8] {'blk'}, dimensions={0}, use_global_device_ids=true | all-gather | bytes 5120 | tf_op jit(solution)/shard_map/all_gather | solution.py:156
  44.6 5.2 %all-gather.1 = f32[16,4,16]{2,1,0:T(4,128)S(1)} all-gather(f32[4,4,16]{2,1,0:T(4,128)S(1)} %multiply_reduce_fusion), channel_id=3, replica_groups=mesh['blk'=4,'fsdp'=8] {'blk'}, dimensions={0}, use_global_device_ids=true | all-gather | bytes 5120 | tf_op jit(solution)/shard_map/all_gather | solution.py:156
  49.8 3.8 %while.43 = (s32[]{:T(128)}, f32[256,4,128]{0,2,1:T(8,128)S(1)}, s32[]{:T(128)}, bf16[4,16,4,4,128]{4,1,3,2,0:T(8,128)(2,1)S(1)}, s32[16]{0:T(128)S(1)}, /*index...) while((s32[]{:T(128)}, f32[256,4,128]{0,2,1:T(8,128)S(1)}, ...), condition=%wide.region_11.12_spmd.clone, body=%wide.region_8.11_spmd.clone.sunk | while | flops 51122216 | bytes 3374734 | solution.py:195
  49.9 0.8 conditional.7
  50.3 0.4 fusion.13
  50.8 0.8 conditional.7
  51.2 0.4 fusion.13
  51.8 0.8 conditional.7
  52.2 0.4 fusion.13
  52.7 0.8 conditional.7
  53.1 0.4 fusion.13
  53.7 0.3 multiply_cosine_fusion
  54.1 2.7 %convolution_bitcast_fusion.2 = f32[2048,512]{0,1:T(8,128)} fusion(bf16[256,512]{0,1:T(8,128)(2,1)S(1)} %bitcast.118, bf16[1,256,2048]{2,1,0:T(8,128)(2,1)S(1)} %copy-done), kind=kOutput, calls=%fused_computation.46 | convolution fusion | flops 536870912 | bytes 5505024 | tf_op jit(solution)/shard_map/dot_general | solution.py:203
  56.8 5.4 %copy.74 = f32[2048,512]{1,0:T(8,128)} copy(f32[2048,512]{0,1:T(8,128)} %convolution_bitcast_fusion.2) | data formatting | bytes 8388608
  62.2 146.1 %reduce-scatter.4.cloned.1.call-done = f32[64,512]{1,0:T(8,128)} async-done(((f32[2048,512]{1,0:T(8,128)}), f32[64,512]{1,0:T(8,128)}) %reduce-scatter.4.cloned.1.call-update) | async-done | bytes 131088 | tf_op jit(solution)/shard_map/reduce_scatter | solution.py:206
  208.2 1.6 fusion.42
  (111 shorter events, 5.2 us)
Async XLA Ops:
  6.5 47.6 %copy-start = (bf16[1,256,2048]{2,1,0:T(8,128)(2,1)S(1)}, bf16[1,256,2048]{2,1,0:T(8,128)(2,1)}, u32[]{:S(2)}) copy-start(bf16[1,256,2048]{2,1,0:T(8,128)(2,1)} %param.15) | copy-start | bytes 3145732
  6.5 8.0 %copy-start.2 = (s32[1,16]{1,0:T(1,128)S(1)}, s32[1,16]{1,0:T(1,128)}, u32[]{:S(2)}) copy-start(s32[1,16]{1,0:T(1,128)} %param.16) | copy-start | bytes 196
  6.5 201.7 %reduce-scatter.4.cloned.1.call-start = ((), (), s32[]{:S(2)}) async-start(), calls=%async_computation.1 | async-start | bytes 4325376 | tf_op jit(solution)/shard_map/reduce_scatter | solution.py:206
  14.6 4.4 %collective-permute-start.1 = (bf16[16,4,4,128]{3,2,1,0:T(4,128)(2,1)S(1)}, bf16[16,4,4,128]{3,2,1,0:T(4,128)(2,1)S(1)}, u32[]{:S(2)}, u32[]{:S(2)}) collective-permute-start(bf16[16,4,4,128]{3,2,1,0:T(4,128)(2,1)S(1)} %get-tuple-element.979), channel_id=1, source_target_pairs={{24,0},{0,8},{8,16},{16,24},{25,1},{1,9},{9,17},{17,25},{26,2},{2,... | collective-permute-start | bytes 196616 | tf_op jit(solution)/shard_map/while/body/eval_jaxpr/ppermute | solution.py:19
  15.1 6.4 %collective-permute-start.3 = (f32[4,4,16]{2,1,0:T(4,128)S(1)}, f32[4,4,16]{2,1,0:T(4,128)S(1)}, u32[]{:S(2)}, u32[]{:S(2)}) collective-permute-start(f32[4,4,16]{2,1,0:T(4,128)S(1)} %get-tuple-element.981), channel_id=1, source_target_pairs={{24,0},{0,8},{8,16},{16,24},{25,1},{1,9},{9,17},{17,25},{26,2},{2,... | collective-permute-start | bytes 3080 | tf_op jit(solution)/shard_map/while/body/eval_jaxpr/ppermute | solution.py:19
  17.7 3.9 %collective-permute-start.2 = (f32[4,4,16]{2,1,0:T(4,128)S(1)}, f32[4,4,16]{2,1,0:T(4,128)S(1)}, u32[]{:S(2)}, u32[]{:S(2)}) collective-permute-start(f32[4,4,16]{2,1,0:T(4,128)S(1)} %get-tuple-element.980), channel_id=1, source_target_pairs={{24,0},{0,8},{8,16},{16,24},{25,1},{1,9},{9,17},{17,25},{26,2},{2,... | collective-permute-start | bytes 3080 | tf_op jit(solution)/shard_map/while/body/eval_jaxpr/ppermute | solution.py:19
  17.8 3.7 %collective-permute-start = (bf16[16,4,4,128]{3,0,2,1:T(8,128)(2,1)S(1)}, bf16[16,4,4,128]{3,0,2,1:T(8,128)(2,1)S(1)}, u32[]{:S(2)}, u32[]{:S(2)}) collective-permute-start(bf16[16,4,4,128]{3,0,2,1:T(8,128)(2,1)S(1)} %get-tuple-element.978), channel_id=1, source_target_pairs={{24,0},{0,8},{8,16},{16,24},{25,1},{1,9},{9,17},{17,25},{26,2},{2,... | collective-permute-start | bytes 196616 | tf_op jit(solution)/shard_map/while/body/eval_jaxpr/ppermute | solution.py:19
  17.8 5.1 %collective-permute-start.4 = (f32[4,4,16,128]{3,2,1,0:T(8,128)S(1)}, f32[4,4,16,128]{3,2,1,0:T(8,128)S(1)}, u32[]{:S(2)}, u32[]{:S(2)}) collective-permute-start(f32[4,4,16,128]{3,2,1,0:T(8,128)S(1)} %get-tuple-element.982), channel_id=1, source_target_pairs={{24,0},{0,8},{8,16},{16,24},{25,1},{1,9},{9,17},{17,25},{26,2},{2,... | collective-permute-start | bytes 393224 | tf_op jit(solution)/shard_map/while/body/eval_jaxpr/ppermute | solution.py:19
  23.8 3.7 %collective-permute-start.1 = (bf16[16,4,4,128]{3,2,1,0:T(4,128)(2,1)S(1)}, bf16[16,4,4,128]{3,2,1,0:T(4,128)(2,1)S(1)}, u32[]{:S(2)}, u32[]{:S(2)}) collective-permute-start(bf16[16,4,4,128]{3,2,1,0:T(4,128)(2,1)S(1)} %get-tuple-element.979), channel_id=1, source_target_pairs={{24,0},{0,8},{8,16},{16,24},{25,1},{1,9},{9,17},{17,25},{26,2},{2,... | collective-permute-start | bytes 196616 | tf_op jit(solution)/shard_map/while/body/eval_jaxpr/ppermute | solution.py:19
  23.9 4.6 %collective-permute-start.3 = (f32[4,4,16]{2,1,0:T(4,128)S(1)}, f32[4,4,16]{2,1,0:T(4,128)S(1)}, u32[]{:S(2)}, u32[]{:S(2)}) collective-permute-start(f32[4,4,16]{2,1,0:T(4,128)S(1)} %get-tuple-element.981), channel_id=1, source_target_pairs={{24,0},{0,8},{8,16},{16,24},{25,1},{1,9},{9,17},{17,25},{26,2},{2,... | collective-permute-start | bytes 3080 | tf_op jit(solution)/shard_map/while/body/eval_jaxpr/ppermute | solution.py:19
  24.4 4.1 %collective-permute-start.2 = (f32[4,4,16]{2,1,0:T(4,128)S(1)}, f32[4,4,16]{2,1,0:T(4,128)S(1)}, u32[]{:S(2)}, u32[]{:S(2)}) collective-permute-start(f32[4,4,16]{2,1,0:T(4,128)S(1)} %get-tuple-element.980), channel_id=1, source_target_pairs={{24,0},{0,8},{8,16},{16,24},{25,1},{1,9},{9,17},{17,25},{26,2},{2,... | collective-permute-start | bytes 3080 | tf_op jit(solution)/shard_map/while/body/eval_jaxpr/ppermute | solution.py:19
  24.5 4.0 %collective-permute-start = (bf16[16,4,4,128]{3,0,2,1:T(8,128)(2,1)S(1)}, bf16[16,4,4,128]{3,0,2,1:T(8,128)(2,1)S(1)}, u32[]{:S(2)}, u32[]{:S(2)}) collective-permute-start(bf16[16,4,4,128]{3,0,2,1:T(8,128)(2,1)S(1)} %get-tuple-element.978), channel_id=1, source_target_pairs={{24,0},{0,8},{8,16},{16,24},{25,1},{1,9},{9,17},{17,25},{26,2},{2,... | collective-permute-start | bytes 196616 | tf_op jit(solution)/shard_map/while/body/eval_jaxpr/ppermute | solution.py:19
  26.2 4.4 %collective-permute-start.4 = (f32[4,4,16,128]{3,2,1,0:T(8,128)S(1)}, f32[4,4,16,128]{3,2,1,0:T(8,128)S(1)}, u32[]{:S(2)}, u32[]{:S(2)}) collective-permute-start(f32[4,4,16,128]{3,2,1,0:T(8,128)S(1)} %get-tuple-element.982), channel_id=1, source_target_pairs={{24,0},{0,8},{8,16},{16,24},{25,1},{1,9},{9,17},{17,25},{26,2},{2,... | collective-permute-start | bytes 393224 | tf_op jit(solution)/shard_map/while/body/eval_jaxpr/ppermute | solution.py:19
  31.5 3.7 %collective-permute-start.1 = (bf16[16,4,4,128]{3,2,1,0:T(4,128)(2,1)S(1)}, bf16[16,4,4,128]{3,2,1,0:T(4,128)(2,1)S(1)}, u32[]{:S(2)}, u32[]{:S(2)}) collective-permute-start(bf16[16,4,4,128]{3,2,1,0:T(4,128)(2,1)S(1)} %get-tuple-element.979), channel_id=1, source_target_pairs={{24,0},{0,8},{8,16},{16,24},{25,1},{1,9},{9,17},{17,25},{26,2},{2,... | collective-permute-start | bytes 196616 | tf_op jit(solution)/shard_map/while/body/eval_jaxpr/ppermute | solution.py:19
  31.6 4.6 %collective-permute-start.3 = (f32[4,4,16]{2,1,0:T(4,128)S(1)}, f32[4,4,16]{2,1,0:T(4,128)S(1)}, u32[]{:S(2)}, u32[]{:S(2)}) collective-permute-start(f32[4,4,16]{2,1,0:T(4,128)S(1)} %get-tuple-element.981), channel_id=1, source_target_pairs={{24,0},{0,8},{8,16},{16,24},{25,1},{1,9},{9,17},{17,25},{26,2},{2,... | collective-permute-start | bytes 3080 | tf_op jit(solution)/shard_map/while/body/eval_jaxpr/ppermute | solution.py:19
  31.6 4.6 %collective-permute-start.2 = (f32[4,4,16]{2,1,0:T(4,128)S(1)}, f32[4,4,16]{2,1,0:T(4,128)S(1)}, u32[]{:S(2)}, u32[]{:S(2)}) collective-permute-start(f32[4,4,16]{2,1,0:T(4,128)S(1)} %get-tuple-element.980), channel_id=1, source_target_pairs={{24,0},{0,8},{8,16},{16,24},{25,1},{1,9},{9,17},{17,25},{26,2},{2,... | collective-permute-start | bytes 3080 | tf_op jit(solution)/shard_map/while/body/eval_jaxpr/ppermute | solution.py:19
  31.7 4.4 %collective-permute-start = (bf16[16,4,4,128]{3,0,2,1:T(8,128)(2,1)S(1)}, bf16[16,4,4,128]{3,0,2,1:T(8,128)(2,1)S(1)}, u32[]{:S(2)}, u32[]{:S(2)}) collective-permute-start(bf16[16,4,4,128]{3,0,2,1:T(8,128)(2,1)S(1)} %get-tuple-element.978), channel_id=1, source_target_pairs={{24,0},{0,8},{8,16},{16,24},{25,1},{1,9},{9,17},{17,25},{26,2},{2,... | collective-permute-start | bytes 196616 | tf_op jit(solution)/shard_map/while/body/eval_jaxpr/ppermute | solution.py:19
  33.8 4.4 %collective-permute-start.4 = (f32[4,4,16,128]{3,2,1,0:T(8,128)S(1)}, f32[4,4,16,128]{3,2,1,0:T(8,128)S(1)}, u32[]{:S(2)}, u32[]{:S(2)}) collective-permute-start(f32[4,4,16,128]{3,2,1,0:T(8,128)S(1)} %get-tuple-element.982), channel_id=1, source_target_pairs={{24,0},{0,8},{8,16},{16,24},{25,1},{1,9},{9,17},{17,25},{26,2},{2,... | collective-permute-start | bytes 393224 | tf_op jit(solution)/shard_map/while/body/eval_jaxpr/ppermute | solution.py:19
  62.2 146.1 %copy-start.1 = (f32[64,512]{1,0:T(8,128)S(1)}, f32[64,512]{1,0:T(8,128)}, u32[]{:S(2)}) copy-start(f32[64,512]{1,0:T(8,128)} %param.21) | copy-start | bytes 393220
Sparse Core Ops, SparseCore 0:
  62.3 145.8 reduce-scatter.3
where the time goes:
time: 217 us
  waiting for transfers between devices  159 us (73%)
  between operations  13.6 us (6%)
  local copies, waits for them, and re-layouts  12.1 us (6%)
  blocking collectives  10.4 us (5%)
  starting transfers between devices  8.04 us (4%)
  matrix products  7.28 us (3%)
  other arithmetic  5.04 us (2%)
    reduce_scatter x1, waiting for transfers between devices, local(): lax.psum_scatter(local_grad, ('blk', 'fsdp'), scatter_dimension=0, tiled=...  146 us
    ppermute x15, waiting for transfers between devices, shifted(): return lax.ppermute(block, axis, route)  13.3 us
    all_gather x2, blocking collectives, local(): gathered = lax.all_gather(tuple(stats), 'blk', axis=0, tiled=True)  10.4 us
    ppermute x15, starting transfers between devices, shifted(): return lax.ppermute(block, axis, route)  8.04 us
    unnamed x14, local copies, waits for them, and re-layouts  8.03 us
  transfers between devices with their start and end apart: 16, of which 10 were waited for; matrix products, arithmetic and copies ran while one was open for 0% of the time, Pallas kernels for 0%

commit v1 on v0

v1 whole, which is shorter than its diff:
```python
import functools

import jax
import jax.numpy as jnp
from jax import lax
from jax.experimental import pallas as pl
from jax.experimental.pallas import tpu as pltpu
from jax.sharding import PartitionSpec as P

HEADS = 16
KV_HEADS = 4
HEAD_DIM = 128
REPEAT = HEADS // KV_HEADS

decay_rate = 0.99
rope_base = 500000.0
neg_large = -1e30

VMEM = pl.BlockSpec(memory_space=pltpu.VMEM)
SMEM = pl.BlockSpec(memory_space=pltpu.SMEM)
NT_DIMS = (((1,), (1,)), ((), ()))


def swapped(block, axis, bits):
    route = [(i, i ^ bits) for i in range(lax.axis_size(axis))]
    return lax.ppermute(block, axis, route)


def call(kernel, out_shape, in_specs, flops, scratch=()):
    return pl.pallas_call(
        kernel,
        out_shape=out_shape,
        in_specs=in_specs,
        out_specs=jax.tree.map(lambda _: VMEM, out_shape),
        scratch_shapes=scratch,
        cost_estimate=pl.CostEstimate(flops=flops, bytes_accessed=1 << 20, transcendentals=0),
    )


def rotation_tables(first, tokens):
    half = HEAD_DIM // 2
    exponent = jnp.arange(half, dtype=jnp.float32) * (2.0 / HEAD_DIM)
    frequency = jnp.power(jnp.float32(rope_base), -exponent)
    positions = first + lax.broadcasted_iota(jnp.int32, (tokens,), 0)
    angles = positions.astype(jnp.float32)[:, None] * frequency[None, :]
    cosine, sine = jnp.cos(angles), jnp.sin(angles)
    return jnp.concatenate([cosine, cosine], -1), jnp.concatenate([sine, -sine], -1)


def chunks(rows):
    per = max(1, min(REPEAT, 256 // rows))
    return per, REPEAT // per


def collect(order_ref, refs, held):
    rows = refs[0].shape[0]
    for number, ref in enumerate(refs):
        held[pl.ds(pl.multiple_of(order_ref[number] * rows, rows), rows), :] = ref[...]


def heads_of(held, first, count):
    parts = [held[:, pl.ds((first + r) * HEAD_DIM, HEAD_DIM)] for r in range(count)]
    return parts[0] if count == 1 else jnp.concatenate(parts, axis=0)


def stats_kernel(blocks, order_ref, *refs):
    query_refs, cot_refs = refs[:blocks], refs[blocks : 2 * blocks]
    key_ref, value_ref, reach_ref, stats_ref, query_held, cot_held = refs[2 * blocks :]
    collect(order_ref, query_refs, query_held)
    collect(order_ref, cot_refs, cot_held)
    per, count = chunks(query_held.shape[0])
    width = per * query_held.shape[0]
    groups = key_ref.shape[1] // HEAD_DIM
    for group in range(groups):
        columns = pl.ds(group * HEAD_DIM, HEAD_DIM)
        for chunk in range(count):
            first = group * REPEAT + chunk * per
            query = heads_of(query_held, first, per)
            cot = heads_of(cot_held, first, per)
            scores = lax.dot_general(
                key_ref[:, columns], query, NT_DIMS, preferred_element_type=jnp.float32
            ) * (HEAD_DIM**-0.5)
            grads = lax.dot_general(
                value_ref[:, columns], cot, NT_DIMS, preferred_element_type=jnp.float32
            )
            key_ids = lax.broadcasted_iota(jnp.int32, scores.shape, 0)
            scores = jnp.where(key_ids <= reach_ref[...], scores, neg_large)
            top = jnp.max(scores, axis=0, keepdims=True)
            expo = jnp.exp(scores - top)
            total = jnp.sum(expo, axis=0, keepdims=True)
            weights = expo.astype(jnp.bfloat16).astype(jnp.float32)
            dot = jnp.sum(weights * grads, axis=0, keepdims=True)
            place = pl.ds(chunk * width, width)
            stats_ref[0, group : group + 1, place] = top
            stats_ref[1, group : group + 1, place] = total
            stats_ref[2, group : group + 1, place] = dot


def grad_kernel(blocks, order_ref, *refs):
    query_refs, cot_refs = refs[:blocks], refs[blocks : 2 * blocks]
    key_ref, value_ref, reach_ref, norm_ref, dot_ref, cosine_ref, sine_ref = refs[
        2 * blocks : 2 * blocks + 7
    ]
    out_ref, query_held, cot_held = refs[2 * blocks + 7 :]
    collect(order_ref, query_refs, query_held)
    collect(order_ref, cot_refs, cot_held)
    per, count = chunks(query_held.shape[0])
    width = per * query_held.shape[0]
    groups = key_ref.shape[1] // HEAD_DIM
    for group in range(groups):
        columns = pl.ds(group * HEAD_DIM, HEAD_DIM)
        gradient = None
        for chunk in range(count):
            first = group * REPEAT + chunk * per
            query = heads_of(query_held, first, per)
            cot = heads_of(cot_held, first, per)
            place = pl.ds(chunk * width, width)
            scores = lax.dot_general(
                key_ref[:, columns], query, NT_DIMS, preferred_element_type=jnp.float32
            ) * (HEAD_DIM**-0.5)
            grads = lax.dot_general(
                value_ref[:, columns], cot, NT_DIMS, preferred_element_type=jnp.float32
            )
            key_ids = lax.broadcasted_iota(jnp.int32, scores.shape, 0)
            scores = jnp.where(key_ids <= reach_ref[...], scores, neg_large)
            prob = jnp.exp(scores - norm_ref[group : group + 1, place])
            pulled = (prob * (grads - dot_ref[group : group + 1, place])).astype(jnp.bfloat16)
            term = jnp.dot(pulled, query, preferred_element_type=jnp.float32)
            gradient = term if gradient is None else gradient + term
        gradient = gradient * (HEAD_DIM**-0.5)
        turned = pltpu.roll(gradient, HEAD_DIM // 2, 1)
        out_ref[:, columns] = (gradient * cosine_ref[...] + turned * sine_ref[...]).astype(
            jnp.bfloat16
        )


def split_kernel(place_ref, features_ref, keep_ref, send_ref):
    core = place_ref[0]
    rows = keep_ref.shape[0] // 16
    for side in range(2):
        for target, out_ref in ((core, keep_ref), (1 - core, send_ref)):
            start = pl.multiple_of((side * 2 + target) * 8 * rows, 128)
            part = features_ref[:, pl.ds(start, 8 * rows)].T
            for z in range(4):
                for y in range(2):
                    out_ref[pl.ds((side * 8 + y * 4 + z) * rows, rows), :] = part[
                        (z * 2 + y) * rows : (z * 2 + y + 1) * rows
                    ]


def product_kernel(
    place_ref, own_ref, far_ref, own_unrot, far_unrot, a_keep, a_send, b_keep, b_send
):
    side, y = place_ref[1], place_ref[2]
    half = own_ref.shape[0] // 2
    quarter = half // 2
    left = own_unrot.shape[1] // 2

    def product(start, size, columns):
        at = pl.ds(pl.multiple_of(start, quarter), size)
        return jnp.dot(
            own_ref[at, :], own_unrot[:, columns], preferred_element_type=jnp.float32
        ) + jnp.dot(far_ref[at, :], far_unrot[:, columns], preferred_element_type=jnp.float32)

    first, second = pl.ds(0, left), pl.ds(left, left)
    a_send[...] = product((1 - side) * half, half, first).astype(jnp.bfloat16)
    for x in range(2):
        at = pl.ds(x * quarter, quarter)
        b_send[at, :] = product(x * half + (1 - y) * quarter, quarter, second).astype(jnp.bfloat16)
    a_keep[...] = product(side * half, half, first)
    for x in range(2):
        at = pl.ds(x * quarter, quarter)
        b_keep[at, :] = product(x * half + y * quarter, quarter, second)


def gathered_over_blk(query, cot):
    size = lax.axis_size("blk")
    held = {0: (query, cot)}
    bit = size // 2
    while bit:
        for number in sorted(held):
            block = held[number]
            held[number | bit] = tuple(swapped(part, "blk", bit) for part in block)
        bit //= 2
    return [held[number][0] for number in range(size)], [held[number][1] for number in range(size)]


def combined(stats):
    bit = lax.axis_size("blk") // 2
    while bit:
        other = swapped(stats, "blk", bit)
        top = jnp.maximum(stats[0], other[0])
        mine, theirs = jnp.exp(stats[0] - top), jnp.exp(other[0] - top)
        stats = jnp.stack(
            [top, stats[1] * mine + other[1] * theirs, stats[2] * mine + other[2] * theirs]
        )
        bit //= 2
    return stats[0] + jnp.log(stats[1]), stats[2] / stats[1]


def pick(array, index):
    return lax.dynamic_index_in_dim(array, index, 0, keepdims=False)


def reduced_by_halves(unrotated, own, far, place):
    _, side, y = place
    z = lax.axis_index("fsdp") // 2
    far_unrotated = swapped(unrotated, "blk", 1)
    total, width = own.shape[0], unrotated.shape[1]
    half, quarter, left = total // 2, total // 4, width // 2
    shapes = [
        jax.ShapeDtypeStruct((half, left), dtype)
        for dtype in (jnp.float32, jnp.bfloat16, jnp.float32, jnp.bfloat16)
    ]
    a_keep, a_send, b_keep, b_send = call(
        product_kernel, shapes, [SMEM] + [VMEM] * 4, 4 * total * width * own.shape[1]
    )(jnp.stack(place), own, far, unrotated, far_unrotated)
    a_come = swapped(a_send, "blk", 2)
    b_come = swapped(b_send, "fsdp", 1)
    a_sum = (a_keep + a_come.astype(jnp.float32)).reshape(2, quarter, left)
    a_come = swapped(pick(a_sum, 1 - y).astype(jnp.bfloat16), "fsdp", 1)
    b_sum = (b_keep + b_come.astype(jnp.float32)).reshape(2, quarter, left)
    b_come = swapped(pick(b_sum, 1 - side).astype(jnp.bfloat16), "blk", 2)
    a_sum = pick(a_sum, y) + a_come.astype(jnp.float32)
    b_sum = pick(b_sum, side) + b_come.astype(jnp.float32)
    rows = quarter // 4
    both = jnp.concatenate([a_sum, b_sum], axis=-1).reshape(4, rows, width)
    result = pick(both, z)
    for distance in (1, 2, 3):
        route = [(i, (i + 2 * distance) % 8) for i in range(8)]
        piece = pick(both, (z + distance) % 4).astype(jnp.bfloat16)
        result = result + lax.ppermute(piece, "fsdp", route).astype(jnp.float32)
    return result


def local(normed, picked, queries, key_states, values, cotangent, hessian):
    rows = queries.shape[1]
    tokens = key_states.shape[1]
    width = key_states.shape[2]
    groups = width // HEAD_DIM
    blocks, sequences = lax.axis_size("blk"), lax.axis_size("fsdp")
    place_blk = lax.axis_index("blk")
    features = normed[0]
    halves = blocks == 4 and sequences == 8 and hessian.shape[0] == 64 and tokens % 128 == 0

    if blocks & (blocks - 1) == 0:
        query_blocks, cot_blocks = gathered_over_blk(queries[0], cotangent[0])
        order = jnp.arange(blocks, dtype=jnp.int32) ^ place_blk
    else:
        all_queries = lax.all_gather(queries[0], "blk", axis=0)
        all_cots = lax.all_gather(cotangent[0], "blk", axis=0)
        query_blocks = [all_queries[i] for i in range(blocks)]
        cot_blocks = [all_cots[i] for i in range(blocks)]
        order = jnp.arange(blocks, dtype=jnp.int32)

    ids = jnp.arange(blocks, dtype=jnp.int32)[:, None]
    reach = jnp.where(
        ids == place_blk, picked, jnp.where(ids > place_blk, jnp.int32(tokens), jnp.int32(-1))
    ).reshape(1, blocks * rows)
    per, count = chunks(blocks * rows)
    reach = jnp.tile(reach, (1, per))
    cosine, sine = rotation_tables(place_blk * tokens, tokens)

    if halves:
        place = (place_blk % 2, place_blk // 2, lax.axis_index("fsdp") % 2)
        half = jax.ShapeDtypeStruct((features.shape[1] // 2, tokens), jnp.bfloat16)
        own, far = call(split_kernel, [half, half], [SMEM, VMEM], 1 << 27)(
            jnp.stack(place), features
        )
        far = swapped(far, "blk", 1)

    held = pltpu.VMEM((blocks * rows, HEADS * HEAD_DIM), jnp.bfloat16)
    operands = (order, *query_blocks, *cot_blocks, key_states[0], values[0], reach)
    specs = [SMEM] + [VMEM] * (2 * blocks + 3)
    work = 4 * HEADS * blocks * rows * tokens * HEAD_DIM
    stats = call(
        functools.partial(stats_kernel, blocks),
        jax.ShapeDtypeStruct((3, groups, REPEAT * blocks * rows), jnp.float32),
        specs,
        work,
        [held, held],
    )(*operands)
    log_norm, row_dot = combined(stats) if blocks & (blocks - 1) == 0 else gathered_stats(stats)
    unrotated = call(
        functools.partial(grad_kernel, blocks),
        jax.ShapeDtypeStruct((tokens, width), jnp.bfloat16),
        specs + [VMEM] * 4,
        work + work // 2,
        [held, held],
    )(*operands, log_norm, row_dot, cosine, sine)

    if halves:
        summed = reduced_by_halves(unrotated, own, far, place)
    else:
        term = lax.dot_general(
            features, unrotated, (((0,), (0,)), ((), ())), preferred_element_type=jnp.float32
        )
        summed = lax.psum_scatter(term, ("blk", "fsdp"), scatter_dimension=0, tiled=True)
    return decay_rate * hessian + (1.0 - decay_rate) * summed * summed / sequences


def gathered_stats(stats):
    every = lax.all_gather(stats, "blk", axis=0)
    top = jnp.max(every[:, 0], axis=0)
    shrink = jnp.exp(every[:, 0] - top)
    total = jnp.sum(every[:, 1] * shrink, axis=0)
    dot = jnp.sum(every[:, 2] * shrink, axis=0)
    return top + jnp.log(total), dot / total


def solution(mesh):
    placed = (
        P("fsdp", "blk", None),
        P("fsdp", "blk"),
        P("fsdp", "blk", None),
        P("fsdp", "blk", None),
        P("fsdp", "blk", None),
        P("fsdp", "blk", None),
        P(("blk", "fsdp"), None),
    )
    return jax.shard_map(
        local, mesh=mesh, in_specs=placed, out_specs=P(("blk", "fsdp"), None), check_vma=False
    )
```

time: 217 us -> 54.6 us (0.25)
  waiting for transfers between devices: 159 us -> 16.4 us
  between operations: 13.6 us -> 0.17 us
  Pallas kernels: 0 us -> 11.3 us
  blocking collectives: 10.4 us -> 0 us
  starting transfers between devices: 8.04 us -> 18.3 us
  local copies, waits for them, and re-layouts: 12.1 us -> 3 us
  matrix products: 7.28 us -> 0 us
    reduce_scatter x1 -> x0, waiting for transfers between devices: 146 us -> none  [local(): lax.psum_scatter(local_grad, ('blk', 'fsdp'), scatter_dimension=0, tiled=...]
    pallas_call x0 -> x4, Pallas kernels: none -> 11.3 us  [the longest x1 3.15 us: local(): call(functools.partial(grad_kernel, blocks), jax.ShapeDtypeStruct((tokens...]
    all_gather x2 -> x0, blocking collectives: 10.4 us -> none  [local(): gathered = lax.all_gather(tuple(stats), 'blk', axis=0, tiled=True)]
    ppermute x15 -> x17, starting transfers between devices: 8.04 us -> 18.3 us  [the longest x14 12.7 us: swapped(): return lax.ppermute(block, axis, route)]
    dot_general x17 -> x0, matrix products: 7.28 us -> none  [the longest x1 2.7 us: local(): lax.dot_general(features, unrotated, (((0,), (0,)), ((), ())), preferred_...]
    unnamed x14 -> x24, local copies, waits for them, and re-layouts: 8.03 us -> 2.16 us
    ppermute x15 -> x17, waiting for transfers between devices: 13.3 us -> 16.4 us  [the longest x14 13.5 us: swapped(): return lax.ppermute(block, axis, route)]
  transfers between devices with their start and end apart: 16 -> 17, of which waited for: 10 -> 11; matrix products, arithmetic and copies ran while one was open for 0% -> 10% of each run, Pallas kernels for 0% -> 15%
where the time goes in v1:
time: 54.6 us; the launch traced here: 54.3 us
  starting transfers between devices  18.3 us (34%)
  waiting for transfers between devices  16.4 us (30%)
  Pallas kernels  11.3 us (21%)
  other arithmetic  5.25 us (10%)
  local copies, waits for them, and re-layouts  3 us (5%)
    ppermute x14, waiting for transfers between devices, swapped(): return lax.ppermute(block, axis, route)  13.5 us
    ppermute x14, starting transfers between devices, swapped(): return lax.ppermute(block, axis, route)  12.7 us
    ppermute x3, starting transfers between devices, reduced_by_halves(): result = result + lax.ppermute(piece, 'fsdp', route).astype(jnp.float32)  5.57 us
    pallas_call x1, Pallas kernels, local(): call(functools.partial(grad_kernel, blocks), jax.ShapeDtypeStruct((tokens...  3.15 us
    pallas_call x1, Pallas kernels, reduced_by_halves(): call(product_kernel, shapes, [SMEM] + [VMEM] * 4, 4 * total * width * own...  3.08 us
    ppermute x3, waiting for transfers between devices, reduced_by_halves(): result = result + lax.ppermute(piece, 'fsdp', route).astype(jnp.float32)  2.91 us
    pallas_call x1, Pallas kernels, local(): call(functools.partial(stats_kernel, blocks), jax.ShapeDtypeStruct((3, gr...  2.57 us
    pallas_call x1, Pallas kernels, local(): call(split_kernel, [half, half], [SMEM, VMEM], 1 << 27)  2.48 us
  transfers between devices with their start and end apart: 17, of which 11 were waited for; matrix products, arithmetic and copies ran while one was open for 10% of the time, Pallas kernels for 15%

profile of v1, /device:TPU:0, one launch (start us, length us, event | category | flops | bytes accessed | tf_op | source)
XLA Modules:
  0.0 54.3 jit_solution(16063895150256165713)
XLA Ops:
  0.0 3.0 %collective-permute-start.2 = (bf16[16,2048]{1,0:T(8,128)(2,1)}, bf16[16,2048]{1,0:T(8,128)(2,1)S(1)}, u32[]{:S(2)}, u32[]{:S(2)}) collective-permute-start(bf16[16,2048]{1,0:T(8,128)(2,1)} %bitcast.137), channel_id=1, source_target_pairs={{0,16},{8,24},{16,0},{24,8},{1,17},{9,25},{17,1},{25,9},{2,18},{10... | collective-permute-start | bytes 196616 | tf_op jit(solution)/shard_map/ppermute | solution.py:26
  3.0 0.1 collective-permute-start.5
  3.0 0.4 collective-permute-start.4
  3.5 0.6 %pad_add_fusion.place_ref = s32[3]{0:T(128)} fusion(s32[1]{0:T(128)} %bitcast.2, s32[1]{0:T(128)} %bitcast.1, s32[1]{0:T(128)} %bitcast), kind=kLoop, calls=%fused_computation.60 | loop fusion | flops 6 | bytes 24 | tf_op jit(solution)/shard_map/stack | solution.py:217
  4.0 2.5 %shard_map.73 = (bf16[1024,256]{1,0:T(8,128)(2,1)}, bf16[1024,256]{1,0:T(8,128)(2,1)}) custom-call(s32[3]{0:T(128)} %pad_add_fusion.place_ref, bf16[256,2048]{1,0:T(8,128)(2,1)} %bitcast.136), custom_call_target="tpu_custom_call" | custom-call | flops 134217728 | bytes 1048576 | tf_op jit(solution)/shard_map/pallas_call | solution.py:267
  6.5 0.1 collective-permute-start
  6.6 0.6 %copy-done.9 = s32[1,16]{1,0:T(1,128)S(1)} copy-done((s32[1,16]{1,0:T(1,128)S(1)}, s32[1,16]{1,0:T(1,128)}, u32[]{:S(2)}) %copy-start.9) | copy-done | bytes 88
  7.3 0.1 broadcast_select_fusion
  7.3 0.1 select_n.81
  7.4 0.7 %tile.9.refs_10_ = s32[1,256]{1,0:T(1,128)} reshape(s32[4,64]{1,0:T(4,128)S(1)} %tile.8) | data formatting | bytes 2048 | tf_op jit(solution)/shard_map/tile | solution.py:261
  8.1 0.6 %iota_xor_fusion.order_ref = s32[4]{0:T(128)} fusion(s32[]{:T(128)S(6)} %axis_index.27), kind=kLoop, calls=%fused_computation.63 | loop fusion | flops 4 | bytes 20 | tf_op jit(solution)/shard_map/xor | solution.py:248
  8.7 0.4 collective-permute-start.3
  9.1 0.1 collective-permute-start.6
  9.3 0.8 %collective-permute-done.3.refs_3_ = bf16[16,2048]{1,0:T(8,128)(2,1)S(1)} collective-permute-done((bf16[16,2048]{1,0:T(8,128)(2,1)S(1)}, bf16[16,2048]{1,0:T(8,128)(2,1)S(1)}, u32[]{:S(2)}, u32[]{:S(2)}) %collective-permute-start.3) | collective-permute-done | bytes 65568 | tf_op jit(solution)/shard_map/ppermute | solution.py:26
  10.0 0.4 collective-permute-done.6.refs_7_
  10.4 0.2 copy-done.5
  10.6 0.4 copy-done.6
  11.0 2.6 %shard_map.74 = f32[3,4,256]{2,1,0:T(4,128)} custom-call(s32[4]{0:T(128)} %iota_xor_fusion.order_ref, bf16[16,2048]{1,0:T(8,128)(2,1)} %bitcast.139, bf16[16,2048]{1,0:T(8,128)(2,1)} %copy-done.2, bf16[16,2048]{1,0:T(8,128)(2,1)} %copy-done.1, bf16[16,2048]{1,0:T(8,128)(2,1)} %copy-done.5, bf16[16,2048]{1,0:T(8,128)(2,1)} %bitcast.143, ...), custom_call_target="tpu_custom_call" | custom-call | flops 134217728 | bytes 1048576 | tf_op jit(solution)/shard_map/pallas_call | solution.py:276
  13.6 1.7 %collective-permute-start.7 = (f32[3,4,256]{2,1,0:T(4,128)}, f32[3,4,256]{2,1,0:T(4,128)S(1)}, u32[]{:S(2)}, u32[]{:S(2)}) collective-permute-start(f32[3,4,256]{2,1,0:T(4,128)} %shard_map.74), channel_id=1, source_target_pairs={{0,16},{8,24},{16,0},{24,8},{1,17},{9,25},{17,1},{25,9},{2,18},{10... | collective-permute-start | bytes 36872 | tf_op jit(solution)/shard_map/ppermute | solution.py:26
  15.3 0.5 multiply_sine_fusion
  15.9 1.6 %collective-permute-done.7 = f32[3,4,256]{2,1,0:T(4,128)S(1)} collective-permute-done((f32[3,4,256]{2,1,0:T(4,128)}, f32[3,4,256]{2,1,0:T(4,128)S(1)}, u32[]{:S(2)}, u32[]{:S(2)}) %collective-permute-start.7) | collective-permute-done | bytes 12320 | tf_op jit(solution)/shard_map/ppermute | solution.py:26
  17.5 0.1 collective-permute-start.8
  17.6 0.8 %pad_maximum_fusion.1 = (f32[256,128]{1,0:T(8,128)}, f32[256,128]{1,0:T(8,128)}) fusion(f32[256,64]{1,0:T(8,128)S(1)} %get-tuple-element.26, f32[256,64]{1,0:T(8,128)S(1)} %get-tuple-element.25, f32[256,64]{1,0:T(8,128)S(1)} %get-tuple-element.24), kind=kLoop, calls=%fused_computation.14 | loop fusion | flops 65536 | bytes 458752 | tf_op jit(solution)/shard_map/concatenate | solution.py:47
  18.4 0.3 collective-permute-done.8
  18.8 0.6 %fusion.12 = (f32[4,256]{1,0:T(4,128)}, f32[4,256]{1,0:T(4,128)}) fusion(f32[3,4,256]{2,1,0:T(4,128)S(1)} %collective-permute-done.8, f32[3,4,256]{2,1,0:T(4,128)S(1)} %collective-permute-done.7, f32[3,4,256]{2,1,0:T(4,128)S(1)} %copy-done.7), kind=kLoop, calls=%fused_computation.30 | loop fusion | flops 20480 | bytes 45056 | tf_op jit(solution)/shard_map/div | solution.py:198
  19.4 3.1 %shard_map.75.own_unrot = bf16[256,512]{1,0:T(8,128)(2,1)} custom-call(s32[4]{0:T(128)} %iota_xor_fusion.order_ref, bf16[16,2048]{1,0:T(8,128)(2,1)} %bitcast.140, bf16[16,2048]{1,0:T(8,128)(2,1)} %copy-done.2, bf16[16,2048]{1,0:T(8,128)(2,1)} %copy-done.1, bf16[16,2048]{1,0:T(8,128)(2,1)} %copy-done.5, bf16[16,2048]{1,0:T(8,128)(2,1)} %bitcast.144, ...), custom_call_target="tpu_custom_call" | custom-call | flops 201326592 | bytes 1048576 | tf_op jit(solution)/shard_map/pallas_call | solution.py:284
  22.5 0.2 collective-permute-start.9
  22.7 1.6 %collective-permute-done.9.far_unrot = bf16[256,512]{1,0:T(8,128)(2,1)S(1)} collective-permute-done((bf16[256,512]{1,0:T(8,128)(2,1)}, bf16[256,512]{1,0:T(8,128)(2,1)S(1)}, u32[]{:S(2)}, u32[]{:S(2)}) %collective-permute-start.9) | collective-permute-done | bytes 262176 | tf_op jit(solution)/shard_map/ppermute | solution.py:26
  24.3 0.7 %copy-done.11 = bf16[256,512]{1,0:T(8,128)(2,1)} copy-done((bf16[256,512]{1,0:T(8,128)(2,1)}, bf16[256,512]{1,0:T(8,128)(2,1)S(1)}, u32[]{:S(2)}) %copy-start.11) | copy-done | bytes 262168
  25.0 0.2 copy-done.10
  25.2 3.1 %shard_map.76 = (f32[512,256]{1,0:T(8,128)}, bf16[512,256]{1,0:T(8,128)(2,1)}, f32[512,256]{1,0:T(8,128)}, bf16[512,256]{1,0:T(8,128)(2,1)}) custom-call(s32[3]{0:T(128)} %pad_add_fusion.place_ref, bf16[1024,256]{1,0:T(8,128)(2,1)} %get-tuple-element.11.own_ref, bf16[1024,256]{1,0:T(8,128)(2,1)} %copy-done.10, bf16[256,512]{1,0:T(8,128)(2,1)} %shard_map.75.own_unrot, ...), custom_call_target="tpu_custom_call" | custom-call | flops 536870912 | bytes 1048576 | tf_op jit(solution)/shard_map/pallas_call | solution.py:215
  28.3 1.7 %collective-permute-start.10 = (bf16[512,256]{1,0:T(8,128)(2,1)}, bf16[512,256]{1,0:T(8,128)(2,1)S(1)}, u32[]{:S(2)}, u32[]{:S(2)}) collective-permute-start(bf16[512,256]{1,0:T(8,128)(2,1)} %get-tuple-element.14), channel_id=1, source_target_pairs={{0,16},{8,24},{16,0},{24,8},{1,17},{9,25},{17,1},{25,9},{2,18},{10... | collective-permute-start | bytes 786440 | tf_op jit(solution)/shard_map/ppermute | solution.py:26
  30.0 1.5 %collective-permute-start.12 = (bf16[512,256]{1,0:T(8,128)(2,1)}, bf16[512,256]{1,0:T(8,128)(2,1)S(1)}, u32[]{:S(2)}, u32[]{:S(2)}) collective-permute-start(bf16[512,256]{1,0:T(8,128)(2,1)} %get-tuple-element.16), channel_id=1, source_target_pairs={{0,1},{1,0},{2,3},{3,2},{4,5},{5,4},{6,7},{7,6},{8,9},{9,8},{10,11... | collective-permute-start | bytes 786440 | tf_op jit(solution)/shard_map/ppermute | solution.py:26
  31.5 5.3 %collective-permute-done.10 = bf16[512,256]{1,0:T(8,128)(2,1)S(1)} collective-permute-done((bf16[512,256]{1,0:T(8,128)(2,1)}, bf16[512,256]{1,0:T(8,128)(2,1)S(1)}, u32[]{:S(2)}, u32[]{:S(2)}) %collective-permute-start.10) | collective-permute-done | bytes 262176 | tf_op jit(solution)/shard_map/ppermute | solution.py:26
  36.8 1.2 %convert_add_fusion.1 = f32[512,256]{1,0:T(8,128)S(1)} fusion(f32[512,256]{1,0:T(8,128)} %get-tuple-element.13, bf16[512,256]{1,0:T(8,128)(2,1)S(1)} %collective-permute-done.10), kind=kLoop, calls=%fused_computation.2 | loop fusion | flops 262144 | bytes 1310720 | tf_op jit(solution)/shard_map/add | solution.py:220
  38.0 1.8 %collective-permute-start.11 = (bf16[256,256]{1,0:T(8,128)(2,1)S(1)}, bf16[256,256]{1,0:T(8,128)(2,1)S(1)}, u32[]{:S(2)}, u32[]{:S(2)}) collective-permute-start(bf16[256,256]{1,0:T(8,128)(2,1)S(1)} %fusion.2), channel_id=1, source_target_pairs={{0,1},{1,0},{2,3},{3,2},{4,5},{5,4},{6,7},{7,6},{8,9},{9,8},{10,11... | collective-permute-start | bytes 393224 | tf_op jit(solution)/shard_map/ppermute | solution.py:26
  39.9 0.1 convert_add_fusion
  40.0 1.6 %collective-permute-start.13 = (bf16[256,256]{1,0:T(8,128)(2,1)S(1)}, bf16[256,256]{1,0:T(8,128)(2,1)S(1)}, u32[]{:S(2)}, u32[]{:S(2)}) collective-permute-start(bf16[256,256]{1,0:T(8,128)(2,1)S(1)} %fusion.3), channel_id=1, source_target_pairs={{0,16},{8,24},{16,0},{24,8},{1,17},{9,25},{17,1},{25,9},{2,18},{10... | collective-permute-start | bytes 393224 | tf_op jit(solution)/shard_map/ppermute | solution.py:26
  41.5 1.6 %collective-permute-done.11 = bf16[256,256]{1,0:T(8,128)(2,1)S(1)} collective-permute-done((bf16[256,256]{1,0:T(8,128)(2,1)S(1)}, bf16[256,256]{1,0:T(8,128)(2,1)S(1)}, u32[]{:S(2)}, u32[]{:S(2)}) %collective-permute-start.11) | collective-permute-done | bytes 131104 | tf_op jit(solution)/shard_map/ppermute | solution.py:26
  43.1 1.9 %collective-permute-done.13 = bf16[256,256]{1,0:T(8,128)(2,1)S(1)} collective-permute-done((bf16[256,256]{1,0:T(8,128)(2,1)S(1)}, bf16[256,256]{1,0:T(8,128)(2,1)S(1)}, u32[]{:S(2)}, u32[]{:S(2)}) %collective-permute-start.13) | collective-permute-done | bytes 131104 | tf_op jit(solution)/shard_map/ppermute | solution.py:26
  45.0 0.1 pad_maximum_fusion
  45.1 1.6 %collective-permute-start.14 = (bf16[64,512]{1,0:T(8,128)(2,1)S(1)}, bf16[64,512]{1,0:T(8,128)(2,1)S(1)}, u32[]{:S(2)}, u32[]{:S(2)}) collective-permute-start(bf16[64,512]{1,0:T(8,128)(2,1)S(1)} %get-tuple-element.19), channel_id=1, source_target_pairs={{0,2},{1,3},{2,4},{3,5},{4,6},{5,7},{6,0},{7,1},{8,10},{9,11},{10,... | collective-permute-start | bytes 196616 | tf_op jit(solution)/shard_map/ppermute | solution.py:232
  46.8 2.6 %collective-permute-start.15 = (bf16[64,512]{1,0:T(8,128)(2,1)S(1)}, bf16[64,512]{1,0:T(8,128)(2,1)S(1)}, u32[]{:S(2)}, u32[]{:S(2)}) collective-permute-start(bf16[64,512]{1,0:T(8,128)(2,1)S(1)} %get-tuple-element.21), channel_id=1, source_target_pairs={{0,4},{1,5},{2,6},{3,7},{4,0},{5,1},{6,2},{7,3},{8,12},{9,13},{10,... | collective-permute-start | bytes 196616 | tf_op jit(solution)/shard_map/ppermute | solution.py:232
  49.4 1.4 %collective-permute-start.16 = (bf16[64,512]{1,0:T(8,128)(2,1)S(1)}, bf16[64,512]{1,0:T(8,128)(2,1)S(1)}, u32[]{:S(2)}, u32[]{:S(2)}) collective-permute-start(bf16[64,512]{1,0:T(8,128)(2,1)S(1)} %get-tuple-element.20), channel_id=1, source_target_pairs={{0,6},{1,7},{2,0},{3,1},{4,2},{5,3},{6,4},{7,5},{8,14},{9,15},{10,... | collective-permute-start | bytes 196616 | tf_op jit(solution)/shard_map/ppermute | solution.py:232
  50.7 0.6 %collective-permute-done.14 = bf16[64,512]{1,0:T(8,128)(2,1)S(1)} collective-permute-done((bf16[64,512]{1,0:T(8,128)(2,1)S(1)}, bf16[64,512]{1,0:T(8,128)(2,1)S(1)}, u32[]{:S(2)}, u32[]{:S(2)}) %collective-permute-start.14) | collective-permute-done | bytes 65568 | tf_op jit(solution)/shard_map/ppermute | solution.py:232
  51.3 0.7 %collective-permute-done.15 = bf16[64,512]{1,0:T(8,128)(2,1)S(1)} collective-permute-done((bf16[64,512]{1,0:T(8,128)(2,1)S(1)}, bf16[64,512]{1,0:T(8,128)(2,1)S(1)}, u32[]{:S(2)}, u32[]{:S(2)}) %collective-permute-start.15) | collective-permute-done | bytes 65568 | tf_op jit(solution)/shard_map/ppermute | solution.py:232
  52.0 1.6 %collective-permute-done.16 = bf16[64,512]{1,0:T(8,128)(2,1)S(1)} collective-permute-done((bf16[64,512]{1,0:T(8,128)(2,1)S(1)}, bf16[64,512]{1,0:T(8,128)(2,1)S(1)}, u32[]{:S(2)}, u32[]{:S(2)}) %collective-permute-start.16) | collective-permute-done | bytes 65568 | tf_op jit(solution)/shard_map/ppermute | solution.py:232
  53.6 0.7 %fusion.1 = f32[64,512]{1,0:T(8,128)} fusion(bf16[64,512]{1,0:T(8,128)(2,1)S(1)} %collective-permute-done.16, bf16[64,512]{1,0:T(8,128)(2,1)S(1)} %collective-permute-done.15, bf16[64,512]{1,0:T(8,128)(2,1)S(1)} %collective-permute-done.14, f32[4,64,512]{2,1,0:T(8,128)S(1)} %bitcast.131, s32[]{:T(128)S(6)} %select_n.87, f32[64,512]{1,0:T(8,128)S(1)} %copy-done.8), kind=kLoop, calls=%fused_computation.11 | loop fusion | flops 360448 | bytes 589828 | tf_op jit(solution)/shard_map/add | solution.py:299
  (39 shorter events, 0.2 us)
Async XLA Ops:
  0.0 8.7 %collective-permute-start.2 = (bf16[16,2048]{1,0:T(8,128)(2,1)}, bf16[16,2048]{1,0:T(8,128)(2,1)S(1)}, u32[]{:S(2)}, u32[]{:S(2)}) collective-permute-start(bf16[16,2048]{1,0:T(8,128)(2,1)} %bitcast.137), channel_id=1, source_target_pairs={{0,16},{8,24},{16,0},{24,8},{1,17},{9,25},{17,1},{25,9},{2,18},{10... | collective-permute-start | bytes 196616 | tf_op jit(solution)/shard_map/ppermute | solution.py:26
  3.0 6.3 %collective-permute-start.1 = (bf16[16,2048]{1,0:T(8,128)(2,1)}, bf16[16,2048]{1,0:T(8,128)(2,1)S(1)}, u32[]{:S(2)}, u32[]{:S(2)}) collective-permute-start(bf16[16,2048]{1,0:T(8,128)(2,1)} %bitcast.138), channel_id=1, source_target_pairs={{0,8},{8,0},{16,24},{24,16},{1,9},{9,1},{17,25},{25,17},{2,10},{10... | collective-permute-start | bytes 196616 | tf_op jit(solution)/shard_map/ppermute | solution.py:26
  3.0 6.2 %collective-permute-start.5 = (bf16[16,2048]{1,0:T(8,128)(2,1)}, bf16[16,2048]{1,0:T(8,128)(2,1)S(1)}, u32[]{:S(2)}, u32[]{:S(2)}) collective-permute-start(bf16[16,2048]{1,0:T(8,128)(2,1)} %bitcast.141), channel_id=1, source_target_pairs={{0,16},{8,24},{16,0},{24,8},{1,17},{9,25},{17,1},{25,9},{2,18},{10... | collective-permute-start | bytes 196616 | tf_op jit(solution)/shard_map/ppermute | solution.py:26
  3.0 6.2 %collective-permute-start.4 = (bf16[16,2048]{1,0:T(8,128)(2,1)}, bf16[16,2048]{1,0:T(8,128)(2,1)S(1)}, u32[]{:S(2)}, u32[]{:S(2)}) collective-permute-start(bf16[16,2048]{1,0:T(8,128)(2,1)} %bitcast.142), channel_id=1, source_target_pairs={{0,8},{8,0},{16,24},{24,16},{1,9},{9,1},{17,25},{25,17},{2,10},{10... | collective-permute-start | bytes 196616 | tf_op jit(solution)/shard_map/ppermute | solution.py:26
  6.5 17.8 %collective-permute-start = (bf16[1024,256]{1,0:T(8,128)(2,1)}, bf16[1024,256]{1,0:T(8,128)(2,1)S(1)}, u32[]{:S(2)}, u32[]{:S(2)}) collective-permute-start(bf16[1024,256]{1,0:T(8,128)(2,1)} %get-tuple-element.12), channel_id=1, source_target_pairs={{0,8},{8,0},{16,24},{24,16},{1,9},{9,1},{17,25},{25,17},{2,10},{10... | collective-permute-start | bytes 1572872 | tf_op jit(solution)/shard_map/ppermute | solution.py:26
  6.6 0.7 %copy-start.9 = (s32[1,16]{1,0:T(1,128)S(1)}, s32[1,16]{1,0:T(1,128)}, u32[]{:S(2)}) copy-start(s32[1,16]{1,0:T(1,128)} %param.8) | copy-start | bytes 196
  8.7 1.7 %copy-start.1 = (bf16[16,2048]{1,0:T(8,128)(2,1)}, bf16[16,2048]{1,0:T(8,128)(2,1)S(1)}, u32[]{:S(2)}) copy-start(bf16[16,2048]{1,0:T(8,128)(2,1)S(1)} %collective-permute-done.2.refs_2_) | copy-start | bytes 196612
  8.7 1.3 %collective-permute-start.3 = (bf16[16,2048]{1,0:T(8,128)(2,1)S(1)}, bf16[16,2048]{1,0:T(8,128)(2,1)S(1)}, u32[]{:S(2)}, u32[]{:S(2)}) collective-permute-start(bf16[16,2048]{1,0:T(8,128)(2,1)S(1)} %collective-permute-done.2.refs_2_), channel_id=1, source_target_pairs={{0,8},{8,0},{16,24},{24,16},{1,9},{9,1},{17,25},{25,17},{2,10},{10... | collective-permute-start | bytes 196616 | tf_op jit(solution)/shard_map/ppermute | solution.py:26
  9.1 1.3 %copy-start.3 = (bf16[16,2048]{1,0:T(8,128)(2,1)}, bf16[16,2048]{1,0:T(8,128)(2,1)S(1)}, u32[]{:S(2)}) copy-start(bf16[16,2048]{1,0:T(8,128)(2,1)S(1)} %collective-permute-done.5.refs_6_) | copy-start | bytes 196612
  9.1 1.3 %collective-permute-start.6 = (bf16[16,2048]{1,0:T(8,128)(2,1)S(1)}, bf16[16,2048]{1,0:T(8,128)(2,1)S(1)}, u32[]{:S(2)}, u32[]{:S(2)}) collective-permute-start(bf16[16,2048]{1,0:T(8,128)(2,1)S(1)} %collective-permute-done.5.refs_6_), channel_id=1, source_target_pairs={{0,8},{8,0},{16,24},{24,16},{1,9},{9,1},{17,25},{25,17},{2,10},{10... | collective-permute-start | bytes 196616 | tf_op jit(solution)/shard_map/ppermute | solution.py:26
  9.2 1.2 %copy-start.2 = (bf16[16,2048]{1,0:T(8,128)(2,1)}, bf16[16,2048]{1,0:T(8,128)(2,1)S(1)}, u32[]{:S(2)}) copy-start(bf16[16,2048]{1,0:T(8,128)(2,1)S(1)} %collective-permute-done.1.refs_1_) | copy-start | bytes 196612
  9.2 1.2 %copy-start.4 = (bf16[16,2048]{1,0:T(8,128)(2,1)}, bf16[16,2048]{1,0:T(8,128)(2,1)S(1)}, u32[]{:S(2)}) copy-start(bf16[16,2048]{1,0:T(8,128)(2,1)S(1)} %collective-permute-done.4.refs_5_) | copy-start | bytes 196612
  10.0 0.6 %copy-start.5 = (bf16[16,2048]{1,0:T(8,128)(2,1)}, bf16[16,2048]{1,0:T(8,128)(2,1)S(1)}, u32[]{:S(2)}) copy-start(bf16[16,2048]{1,0:T(8,128)(2,1)S(1)} %collective-permute-done.3.refs_3_) | copy-start | bytes 196612
  10.4 0.6 %copy-start.6 = (bf16[16,2048]{1,0:T(8,128)(2,1)}, bf16[16,2048]{1,0:T(8,128)(2,1)S(1)}, u32[]{:S(2)}) copy-start(bf16[16,2048]{1,0:T(8,128)(2,1)S(1)} %collective-permute-done.6.refs_7_) | copy-start | bytes 196612
  13.6 3.9 %copy-start.7 = (f32[3,4,256]{2,1,0:T(4,128)S(1)}, f32[3,4,256]{2,1,0:T(4,128)}, u32[]{:S(2)}) copy-start(f32[3,4,256]{2,1,0:T(4,128)} %shard_map.74) | copy-start | bytes 36868
  13.6 3.9 %collective-permute-start.7 = (f32[3,4,256]{2,1,0:T(4,128)}, f32[3,4,256]{2,1,0:T(4,128)S(1)}, u32[]{:S(2)}, u32[]{:S(2)}) collective-permute-start(f32[3,4,256]{2,1,0:T(4,128)} %shard_map.74), channel_id=1, source_target_pairs={{0,16},{8,24},{16,0},{24,8},{1,17},{9,25},{17,1},{25,9},{2,18},{10... | collective-permute-start | bytes 36872 | tf_op jit(solution)/shard_map/ppermute | solution.py:26
  17.5 1.2 %collective-permute-start.8 = (f32[3,4,256]{2,1,0:T(4,128)S(1)}, f32[3,4,256]{2,1,0:T(4,128)S(1)}, u32[]{:S(2)}, u32[]{:S(2)}) collective-permute-start(f32[3,4,256]{2,1,0:T(4,128)S(1)} %pad_maximum_fusion.3), channel_id=1, source_target_pairs={{0,8},{8,0},{16,24},{24,16},{1,9},{9,1},{17,25},{25,17},{2,10},{10... | collective-permute-start | bytes 36872 | tf_op jit(solution)/shard_map/ppermute | solution.py:26
  22.5 1.7 %collective-permute-start.9 = (bf16[256,512]{1,0:T(8,128)(2,1)}, bf16[256,512]{1,0:T(8,128)(2,1)S(1)}, u32[]{:S(2)}, u32[]{:S(2)}) collective-permute-start(bf16[256,512]{1,0:T(8,128)(2,1)} %shard_map.75.own_unrot), channel_id=1, source_target_pairs={{0,8},{8,0},{16,24},{24,16},{1,9},{9,1},{17,25},{25,17},{2,10},{10... | collective-permute-start | bytes 786440 | tf_op jit(solution)/shard_map/ppermute | solution.py:26
  24.3 0.7 %copy-start.11 = (bf16[256,512]{1,0:T(8,128)(2,1)}, bf16[256,512]{1,0:T(8,128)(2,1)S(1)}, u32[]{:S(2)}) copy-start(bf16[256,512]{1,0:T(8,128)(2,1)S(1)} %collective-permute-done.9.far_unrot) | copy-start | bytes 786436
  24.3 0.9 %copy-start.10 = (bf16[1024,256]{1,0:T(8,128)(2,1)}, bf16[1024,256]{1,0:T(8,128)(2,1)S(1)}, u32[]{:S(2)}) copy-start(bf16[1024,256]{1,0:T(8,128)(2,1)S(1)} %collective-permute-done.far_ref) | copy-start | bytes 1572868
  28.3 8.6 %collective-permute-start.10 = (bf16[512,256]{1,0:T(8,128)(2,1)}, bf16[512,256]{1,0:T(8,128)(2,1)S(1)}, u32[]{:S(2)}, u32[]{:S(2)}) collective-permute-start(bf16[512,256]{1,0:T(8,128)(2,1)} %get-tuple-element.14), channel_id=1, source_target_pairs={{0,16},{8,24},{16,0},{24,8},{1,17},{9,25},{17,1},{25,9},{2,18},{10... | collective-permute-start | bytes 786440 | tf_op jit(solution)/shard_map/ppermute | solution.py:26
  30.0 9.9 %collective-permute-start.12 = (bf16[512,256]{1,0:T(8,128)(2,1)}, bf16[512,256]{1,0:T(8,128)(2,1)S(1)}, u32[]{:S(2)}, u32[]{:S(2)}) collective-permute-start(bf16[512,256]{1,0:T(8,128)(2,1)} %get-tuple-element.16), channel_id=1, source_target_pairs={{0,1},{1,0},{2,3},{3,2},{4,5},{5,4},{6,7},{7,6},{8,9},{9,8},{10,11... | collective-permute-start | bytes 786440 | tf_op jit(solution)/shard_map/ppermute | solution.py:26
  36.8 3.0 %copy-start = (f32[512,256]{1,0:T(8,128)S(1)}, f32[512,256]{1,0:T(8,128)}, u32[]{:S(2)}) copy-start(f32[512,256]{1,0:T(8,128)} %get-tuple-element.15) | copy-start | bytes 1572868
  38.0 5.0 %collective-permute-start.11 = (bf16[256,256]{1,0:T(8,128)(2,1)S(1)}, bf16[256,256]{1,0:T(8,128)(2,1)S(1)}, u32[]{:S(2)}, u32[]{:S(2)}) collective-permute-start(bf16[256,256]{1,0:T(8,128)(2,1)S(1)} %fusion.2), channel_id=1, source_target_pairs={{0,1},{1,0},{2,3},{3,2},{4,5},{5,4},{6,7},{7,6},{8,9},{9,8},{10,11... | collective-permute-start | bytes 393224 | tf_op jit(solution)/shard_map/ppermute | solution.py:26
  40.0 5.0 %collective-permute-start.13 = (bf16[256,256]{1,0:T(8,128)(2,1)S(1)}, bf16[256,256]{1,0:T(8,128)(2,1)S(1)}, u32[]{:S(2)}, u32[]{:S(2)}) collective-permute-start(bf16[256,256]{1,0:T(8,128)(2,1)S(1)} %fusion.3), channel_id=1, source_target_pairs={{0,16},{8,24},{16,0},{24,8},{1,17},{9,25},{17,1},{25,9},{2,18},{10... | collective-permute-start | bytes 393224 | tf_op jit(solution)/shard_map/ppermute | solution.py:26
  45.1 8.5 %copy-start.8 = (f32[64,512]{1,0:T(8,128)S(1)}, f32[64,512]{1,0:T(8,128)}, u32[]{:S(2)}) copy-start(f32[64,512]{1,0:T(8,128)} %param.13) | copy-start | bytes 393220
  45.1 6.2 %collective-permute-start.14 = (bf16[64,512]{1,0:T(8,128)(2,1)S(1)}, bf16[64,512]{1,0:T(8,128)(2,1)S(1)}, u32[]{:S(2)}, u32[]{:S(2)}) collective-permute-start(bf16[64,512]{1,0:T(8,128)(2,1)S(1)} %get-tuple-element.19), channel_id=1, source_target_pairs={{0,2},{1,3},{2,4},{3,5},{4,6},{5,7},{6,0},{7,1},{8,10},{9,11},{10,... | collective-permute-start | bytes 196616 | tf_op jit(solution)/shard_map/ppermute | solution.py:232
  46.8 5.3 %collective-permute-start.15 = (bf16[64,512]{1,0:T(8,128)(2,1)S(1)}, bf16[64,512]{1,0:T(8,128)(2,1)S(1)}, u32[]{:S(2)}, u32[]{:S(2)}) collective-permute-start(bf16[64,512]{1,0:T(8,128)(2,1)S(1)} %get-tuple-element.21), channel_id=1, source_target_pairs={{0,4},{1,5},{2,6},{3,7},{4,0},{5,1},{6,2},{7,3},{8,12},{9,13},{10,... | collective-permute-start | bytes 196616 | tf_op jit(solution)/shard_map/ppermute | solution.py:232
  49.4 4.3 %collective-permute-start.16 = (bf16[64,512]{1,0:T(8,128)(2,1)S(1)}, bf16[64,512]{1,0:T(8,128)(2,1)S(1)}, u32[]{:S(2)}, u32[]{:S(2)}) collective-permute-start(bf16[64,512]{1,0:T(8,128)(2,1)S(1)} %get-tuple-element.20), channel_id=1, source_target_pairs={{0,6},{1,7},{2,0},{3,1},{4,2},{5,3},{6,4},{7,5},{8,14},{9,15},{10,... | collective-permute-start | bytes 196616 | tf_op jit(solution)/shard_map/ppermute | solution.py:232

commit v2 on v1

v2 whole, which is shorter than its diff:
```python
import functools

import jax
import jax.numpy as jnp
import numpy as np
from jax import lax
from jax.experimental import pallas as pl
from jax.experimental.pallas import tpu as pltpu
from jax.sharding import PartitionSpec as P


HEADS = 16
KV_HEADS = 4
HEAD_DIM = 128
REPEAT = HEADS // KV_HEADS

decay_rate = 0.99
rope_base = 500000.0
neg_large = -1e30

VMEM = pl.BlockSpec(memory_space=pltpu.VMEM)
HBM = pl.BlockSpec(memory_space=pltpu.HBM)
NT_DIMS = (((1,), (1,)), ((), ()))
BOTH = ("blk", "fsdp")


def swapped(block, axis, bits):
    route = [(i, i ^ bits) for i in range(lax.axis_size(axis))]
    return lax.ppermute(block, axis, route)


def call(kernel, out_shape, in_specs, flops, scratch=()):
    return pl.pallas_call(
        kernel,
        out_shape=out_shape,
        in_specs=in_specs,
        out_specs=jax.tree.map(lambda _: VMEM, out_shape),
        scratch_shapes=scratch,
        compiler_params=pltpu.CompilerParams(vmem_limit_bytes=16 << 20),
        cost_estimate=pl.CostEstimate(flops=flops, bytes_accessed=1 << 20, transcendentals=0),
    )


def shape(dims, dtype):
    return jax.ShapeDtypeStruct(dims, dtype)


def rotation_rows(positions):
    half = HEAD_DIM // 2
    frequency = rope_base ** (-2.0 * np.arange(half) / HEAD_DIM)
    angles = positions[:, None] * frequency[None, :]
    cosine, sine = np.cos(angles), np.sin(angles)
    pair = np.concatenate([cosine, cosine], -1), np.concatenate([sine, -sine], -1)
    return jnp.asarray(np.stack(pair).astype(np.float32))


def fill_rotation(starts, tokens, coarse_ref, fine_ref, cosine_ref, sine_ref):
    fine_cos, fine_sin = fine_ref[0], fine_ref[1]
    for part, start in enumerate(starts):
        for step in range(tokens // 16):
            row = pl.ds(start // 16 + step, 1)
            cosine, sine = coarse_ref[0, row, :], coarse_ref[1, row, :]
            at = pl.ds(part * tokens + step * 16, 16)
            cosine_ref[at, :] = cosine * fine_cos - sine * fine_sin
            sine_ref[at, :] = sine * fine_cos + cosine * fine_sin


def position():
    blk, fsdp = lax.axis_index("blk"), lax.axis_index("fsdp")
    return blk & 1, blk >> 1, fsdp & 1, fsdp >> 1


def first_second():
    core, side, y, _ = position()
    return jnp.where(core == 0, side, y), jnp.where(core == 0, y, side)


def chunks(rows):
    per = max(1, min(REPEAT, 256 // rows))
    return per, REPEAT // per


def heads_of(held, first, count):
    parts = [held[:, pl.ds((first + r) * HEAD_DIM, HEAD_DIM)] for r in range(count)]
    return parts[0] if count == 1 else jnp.concatenate(parts, axis=0)


def reach_of(picked, here, width, blocks, tokens):
    rows = picked.shape[1]
    square = (rows, rows)
    diagonal = lax.broadcasted_iota(jnp.int32, square, 0) == lax.broadcasted_iota(
        jnp.int32, square, 1
    )
    column = jnp.sum(jnp.where(diagonal, picked, 0), axis=1, keepdims=True)
    lane = lax.broadcasted_iota(jnp.int32, (rows, width), 1)
    chosen = lax.broadcasted_iota(jnp.int32, (rows, width), 0) == (lane & (rows - 1))
    own = jnp.sum(jnp.where(chosen, column, 0), axis=0, keepdims=True)
    lane = lax.broadcasted_iota(jnp.int32, (1, width), 1)
    block = (lane >> (rows.bit_length() - 1)) & (blocks - 1)
    return jnp.where(block == here, own, jnp.where(block > here, tokens, -1))


def stats_kernel(torus, blocks, parts, *refs):
    query_refs, cot_refs = refs[:blocks], refs[blocks : 2 * blocks]
    key_refs, value_refs = (
        refs[(2 * blocks + i * parts) : (2 * blocks + (i + 1) * parts)] for i in range(2)
    )
    reach_refs = refs[2 * blocks + 2 * parts : 2 * blocks + 3 * parts]
    stats_ref, expo_ref, grads_ref, query_held, cot_held = refs[2 * blocks + 3 * parts :]
    rows, width = query_refs[0].shape[0], query_held.shape[1]
    start = position()[0] * width if torus else 0
    columns = pl.ds(pl.multiple_of(start, HEAD_DIM), width)
    for number in range(blocks):
        block = lax.axis_index("blk") ^ number if torus else number
        at = pl.ds(pl.multiple_of(block * rows, rows), rows)
        query_held[at, :] = query_refs[number][:, columns]
        cot_held[at, :] = cot_refs[number][:, columns]
    per, count = chunks(query_held.shape[0])
    width = per * query_held.shape[0]
    start = position()[0] * (HEAD_DIM * stats_ref.shape[1]) if torus else 0
    for group in range(stats_ref.shape[1]):
        columns = pl.ds(pl.multiple_of(start + group * HEAD_DIM, HEAD_DIM), HEAD_DIM)
        for chunk in range(count):
            first = group * REPEAT + chunk * per
            query = heads_of(query_held, first, per)
            cot = heads_of(cot_held, first, per)
            scores, tops = [], []
            for part in range(parts):
                score = lax.dot_general(
                    key_refs[part][:, columns], query, NT_DIMS, preferred_element_type=jnp.float32
                ) * (HEAD_DIM**-0.5)
                key_ids = lax.broadcasted_iota(jnp.int32, score.shape, 0)
                score = jnp.where(key_ids <= reach_refs[part][...], score, neg_large)
                scores.append(score)
                tops.append(jnp.max(score, axis=0, keepdims=True))
            top = functools.reduce(jnp.maximum, tops)
            place = pl.ds(chunk * width, width)
            total, dot = 0.0, 0.0
            for part in range(parts):
                grads = lax.dot_general(
                    value_refs[part][:, columns], cot, NT_DIMS, preferred_element_type=jnp.float32
                )
                expo = jnp.exp(scores[part] - top)
                weights = expo.astype(jnp.bfloat16).astype(jnp.float32)
                total += jnp.sum(expo, axis=0, keepdims=True)
                dot += jnp.sum(weights * grads, axis=0, keepdims=True)
                expo_ref[group, part, :, place] = expo
                grads_ref[group, part, :, place] = grads
            stats_ref[0, group : group + 1, place] = top
            stats_ref[1, group : group + 1, place] = total
            stats_ref[2, group : group + 1, place] = dot


def attention_stats(queries, cots, keys, values, reach, heads, torus):
    blocks, parts = len(queries), len(keys)
    rows = queries[0].shape[0]
    width = heads * REPEAT * HEAD_DIM
    tokens = keys[0].shape[0]
    total = blocks * rows
    saved = shape((heads, parts, tokens, REPEAT * total), jnp.float32)
    held = shape((total, width), jnp.bfloat16)
    outs = [shape((3, heads, REPEAT * total), jnp.float32), saved, saved, held, held]
    return call(
        functools.partial(stats_kernel, torus, blocks, parts),
        outs,
        [VMEM] * (2 * blocks + 3 * parts),
        4 * heads * REPEAT * total * tokens * parts * HEAD_DIM,
    )(*queries, *cots, *keys, *values, *reach)[:4]


def row_scales(group, mine_ref, every_refs):
    at = slice(group, group + 1)
    top = functools.reduce(jnp.maximum, [ref[0, at, :] for ref in every_refs])
    shrink = [jnp.exp(ref[0, at, :] - top) for ref in every_refs]
    total = sum(ref[1, at, :] * factor for ref, factor in zip(every_refs, shrink))
    dot = sum(ref[2, at, :] * factor for ref, factor in zip(every_refs, shrink))
    return jnp.exp(mine_ref[0, at, :] - top) / total, dot / total


def key_gradient(group, stats_refs, expo_ref, grads_ref, query_ref, cosine_ref, sine_ref):
    scale, dot = row_scales(group, stats_refs[0], stats_refs)
    parts, tokens = expo_ref.shape[1:3]
    per, count = chunks(query_ref.shape[0])
    width = per * query_ref.shape[0]
    blocks = []
    for part in range(parts):
        gradient = 0.0
        for chunk in range(count):
            place = slice(chunk * width, (chunk + 1) * width)
            query = heads_of(query_ref, group * REPEAT + chunk * per, per)
            prob = expo_ref[group, part, :, place] * scale[:, place]
            pulled = prob * (grads_ref[group, part, :, place] - dot[:, place])
            gradient += jnp.dot(
                pulled.astype(jnp.bfloat16), query, preferred_element_type=jnp.float32
            )
        gradient = gradient * (HEAD_DIM**-0.5)
        turned = pltpu.roll(gradient, HEAD_DIM // 2, 1)
        at = slice(part * tokens, (part + 1) * tokens)
        blocks.append(
            (gradient * cosine_ref[at, :] + turned * sine_ref[at, :]).astype(jnp.bfloat16)
        )
    return blocks


def grad_kernel(count, *refs):
    stats_refs, out_ref = refs[:count], refs[-1]
    for group in range(stats_refs[0].shape[1]):
        blocks = key_gradient(group, stats_refs, *refs[count:-1])
        out_ref[:, group * HEAD_DIM : (group + 1) * HEAD_DIM] = blocks[0]


def send_kernel(group, *refs):
    stats_refs, saved_refs = refs[:2], refs[2:7]
    own_ref, far_ref, unrot_ref, out_ref = refs[7:]
    own, far = key_gradient(group, stats_refs, *saved_refs)
    unrot_ref[0] = own
    unrot_ref[1] = far
    half = out_ref.shape[0]
    at = pl.ds(pl.multiple_of((1 - first_second()[0]) * half, half), half)
    out_ref[...] = (
        jnp.dot(own_ref[at, :], own, preferred_element_type=jnp.float32)
        + jnp.dot(far_ref[at, :], far, preferred_element_type=jnp.float32)
    ).astype(jnp.bfloat16)


def keep_kernel(own_ref, far_ref, unrot_ref, out_ref):
    half = out_ref.shape[0]
    at = pl.ds(pl.multiple_of(first_second()[0] * half, half), half)
    out_ref[...] = jnp.dot(
        own_ref[at, :], unrot_ref[0], preferred_element_type=jnp.float32
    ) + jnp.dot(far_ref[at, :], unrot_ref[1], preferred_element_type=jnp.float32)


def halve_kernel(*refs):
    keep_refs, come_refs, (send_ref, hold_ref) = refs[:2], refs[2:4], refs[4:]
    half = hold_ref.shape[0]
    second = first_second()[1]
    for place, out_ref in ((1 - second, send_ref), (second, hold_ref)):
        at = pl.ds(pl.multiple_of(place * half, half), half)
        for head in range(2):
            total = keep_refs[head][at, :] + come_refs[head][at, :].astype(jnp.float32)
            out_ref[:, head * HEAD_DIM : (head + 1) * HEAD_DIM] = total.astype(out_ref.dtype)


def quarter_kernel(hold_ref, come_ref, *outs):
    rows = outs[0].shape[0]
    z = position()[3]
    for distance in (2, 3, 1, 0):
        at = pl.ds(pl.multiple_of(((z + distance) & 3) * rows, rows), rows)
        total = hold_ref[at, :] + come_ref[at, :].astype(jnp.float32)
        outs[distance][...] = total.astype(outs[distance].dtype)


def last_kernel(*refs):
    terms, (here_ref, there_ref) = refs[:4], refs[4:]
    rows = here_ref.shape[0]
    core = position()[0]
    for owner, out_ref in ((1 - core, there_ref), (core, here_ref)):
        at = pl.ds(pl.multiple_of(owner * rows, rows), rows)
        out_ref[...] = sum(ref[at, :].astype(jnp.float32) for ref in terms)


def next_kernel(scale, here_ref, there_ref, hessian_ref, out_ref):
    width = here_ref.shape[1]
    core = position()[0]
    for owner, ref in ((core, here_ref), (1 - core, there_ref)):
        columns = pl.ds(pl.multiple_of(owner * width, width), width)
        term = ref[...]
        out_ref[:, columns] = decay_rate * hessian_ref[:, columns] + scale * term * term


def turn_kernel(features_ref, out_ref):
    rows = out_ref.shape[0] // 32
    core = position()[0]
    for x in range(2):
        for c in range(2):
            part = features_ref[:, pl.ds((x * 2 + c) * 8 * rows, 8 * rows)].T
            for z in range(4):
                for y in range(2):
                    pair = jnp.where(core == 0, x * 2 + y, y * 2 + x)
                    at = pl.multiple_of((pair * 8 + z * 2 + c) * rows, rows)
                    out_ref[pl.ds(at, rows), :] = part[
                        (z * 2 + y) * rows : (z * 2 + y + 1) * rows
                    ]


def own_kernel(blocks, *refs):
    sources, (turned_ref, cosine_ref, sine_ref, reach_ref), rest = refs[:8], refs[8:12], refs[12:]
    held, sems = rest[:-1], rest[-1]
    copies = [
        pltpu.make_async_copy(source, target, sems.at[number])
        for number, (source, target) in enumerate(zip(sources, held))
    ]
    for copy in copies:
        copy.start()
    for copy in copies:
        copy.wait()
    keys_ref, (picked_ref, features_ref, coarse_ref, fine_ref) = held[0], held[4:]
    tokens, blk = keys_ref.shape[0], lax.axis_index("blk")
    reach_ref[...] = reach_of(picked_ref[...], blk, reach_ref.shape[1], blocks, tokens)
    starts = blk * tokens, (blk ^ 1) * tokens
    fill_rotation(starts, tokens, coarse_ref, fine_ref, cosine_ref, sine_ref)
    turn_kernel(features_ref, turned_ref)


def far_kernel(blocks, tokens, features_ref, picked_ref, turned_ref, reach_ref):
    here = lax.axis_index("blk") ^ 1
    reach_ref[...] = reach_of(picked_ref[...], here, reach_ref.shape[1], blocks, tokens)
    turn_kernel(features_ref, turned_ref)


def reduced_on_torus(normed, picked, queries, key_states, values, cotangent, hessian):
    tokens = key_states.shape[0]
    out_rows = hessian.shape[0]
    heads = KV_HEADS // 2

    first = swapped(queries, "blk", 2), swapped(cotangent, "blk", 2)
    second = swapped(queries, "blk", 1), swapped(cotangent, "blk", 1)
    third = swapped(first[0], "blk", 1), swapped(first[1], "blk", 1)
    far_keys, far_values = swapped(key_states, "blk", 1), swapped(values, "blk", 1)
    far_normed, far_picked = swapped(normed, "blk", 1), swapped(picked, "blk", 1)

    coarse, fine = rotation_rows(np.arange(0, 4 * tokens, 16)), rotation_rows(np.arange(16))
    turned = shape((normed.shape[1], tokens), jnp.bfloat16)
    table = shape((2 * tokens, HEAD_DIM), jnp.float32)
    last = shape((1, REPEAT * 4 * queries.shape[0]), jnp.int32)
    given = [
        pltpu.with_memory_space_constraint(array, pltpu.HBM)
        for array in (key_states, values, queries, cotangent, picked, normed, coarse, fine)
    ]
    own, cosine, sine, reach, *fetched = call(
        functools.partial(own_kernel, 4),
        [turned, table, table, last] + [shape(array.shape, array.dtype) for array in given[:4]],
        [HBM] * 8,
        1 << 28,
        [pltpu.VMEM(array.shape, array.dtype) for array in given[4:]]
        + [pltpu.SemaphoreType.DMA((8,))],
    )(*given)
    key_states, values, *held = fetched
    held = [held, second, first, third]
    far, far_reach = call(
        functools.partial(far_kernel, 4, tokens), [turned, last], [VMEM] * 2, 1 << 28
    )(far_normed, far_picked)

    stats, expo, grads, query = attention_stats(
        [pair[0] for pair in held],
        [pair[1] for pair in held],
        [key_states, far_keys],
        [values, far_values],
        (reach, far_reach),
        heads,
        True,
    )
    other = swapped(stats, "blk", 2)

    half_rows = normed.shape[1] // 2
    work = 2 * half_rows * 2 * tokens * HEAD_DIM
    route = [(i, i ^ (1 if (i // 8) % 2 else 16)) for i in range(32)]
    route_after = [(i, i ^ (16 if (i // 8) % 2 else 1)) for i in range(32)]
    keeps, come = [], []
    for group in range(heads):
        unrot, send = call(
            functools.partial(send_kernel, group),
            [shape((2, tokens, HEAD_DIM), jnp.bfloat16), shape((half_rows, HEAD_DIM), jnp.bfloat16)],
            [VMEM] * 9,
            work,
        )(stats, other, expo, grads, query, cosine, sine, own, far)
        come.append(lax.ppermute(send, BOTH, route))
        keeps.append(
            call(keep_kernel, shape((half_rows, HEAD_DIM), jnp.float32), [VMEM] * 3, work)(
                own, far, unrot
            )
        )
    block = half_rows // 2, heads * HEAD_DIM
    send, hold = call(
        halve_kernel, [shape(block, jnp.bfloat16), shape(block, jnp.float32)], [VMEM] * 4, 1 << 20
    )(*keeps, *come)
    come = lax.ppermute(send, BOTH, route_after)
    piece = block[0] // 4, block[1]
    mine, *sends = call(
        quarter_kernel,
        [shape(piece, jnp.float32)] + [shape(piece, jnp.bfloat16)] * 3,
        [VMEM] * 2,
        1 << 20,
    )(hold, come)
    arrived = []
    for distance, send in enumerate(sends, 1):
        along = [(i, (i + 2 * distance) % 8) for i in range(8)]
        arrived.append(lax.ppermute(send, "fsdp", along))
    columns = shape((out_rows, block[1]), jnp.float32)
    here, there = call(last_kernel, [columns] * 2, [VMEM] * 4, 1 << 20)(mine, *arrived)
    there = swapped(there, "blk", 1)
    return call(
        functools.partial(next_kernel, (1.0 - decay_rate) / lax.axis_size("fsdp")),
        shape(hessian.shape, jnp.float32),
        [VMEM] * 3,
        1 << 20,
    )(here, there, hessian)


def reduced_anywhere(normed, picked, queries, key_states, values, cotangent):
    rows, tokens = queries.shape[0], key_states.shape[0]
    size, blk = lax.axis_size("blk"), lax.axis_index("blk")
    every_query = lax.all_gather(queries, "blk", axis=0)
    every_cot = lax.all_gather(cotangent, "blk", axis=0)
    order = jnp.arange(size, dtype=jnp.int32)
    ids = order[:, None]
    reach = jnp.where(
        ids == blk, picked, jnp.where(ids > blk, jnp.int32(tokens), jnp.int32(-1))
    ).reshape(1, size * rows)
    reach = jnp.tile(reach, (1, chunks(size * rows)[0]))
    cosine, sine = lax.dynamic_index_in_dim(
        rotation_rows(np.arange(size * tokens)).reshape(2, size, tokens, HEAD_DIM), blk, 1, False
    )
    stats, expo, grads, query = attention_stats(
        [every_query[i] for i in range(size)],
        [every_cot[i] for i in range(size)],
        [key_states],
        [values],
        (reach,),
        KV_HEADS,
        False,
    )
    gathered = lax.all_gather(stats, "blk", axis=0)
    others = [gathered[(blk + i) % size] for i in range(1, size)]
    unrotated = call(
        functools.partial(grad_kernel, size),
        shape((tokens, KV_HEADS * HEAD_DIM), jnp.bfloat16),
        [VMEM] * (size + 5),
        1 << 28,
    )(stats, *others, expo, grads, query, cosine, sine)
    term = lax.dot_general(
        normed, unrotated, (((0,), (0,)), ((), ())), preferred_element_type=jnp.float32
    )
    return lax.psum_scatter(term, BOTH, scatter_dimension=0, tiled=True)


def on_torus(blocks, sequences):
    return blocks == 4 and sequences == 8


def local(normed, picked, queries, key_states, values, cotangent, hessian):
    given = (normed[0], picked, queries[0], key_states[0], values[0], cotangent[0])
    rows, tokens, out_rows = queries.shape[1], key_states.shape[1], hessian.shape[0]
    blocks, sequences = lax.axis_size("blk"), lax.axis_size("fsdp")
    fits = rows & (rows - 1) == 0 and rows <= 16 and tokens % 128 == 0 and out_rows % 16 == 0
    if on_torus(blocks, sequences):
        assert fits
        return reduced_on_torus(*given, hessian)
    summed = reduced_anywhere(*given)
    return decay_rate * hessian + (1.0 - decay_rate) * summed * summed / sequences


def solution(mesh):
    placed = (
        P("fsdp", "blk", None),
        P("fsdp", "blk"),
        P("fsdp", "blk", None),
        P("fsdp", "blk", None),
        P("fsdp", "blk", None),
        P("fsdp", "blk", None),
        P(("blk", "fsdp"), None),
    )
    return jax.shard_map(
        local, mesh=mesh, in_specs=placed, out_specs=P(("blk", "fsdp"), None), check_vma=False
    )
```

time: 54.6 us -> 45.9 us (0.84)
  other arithmetic: 5.25 us -> 0 us
  waiting for transfers between devices: 16.4 us -> 21.4 us
  Pallas kernels: 11.3 us -> 6.47 us
  local copies, waits for them, and re-layouts: 3 us -> 0.01 us
    ppermute x3 -> x6, waiting for transfers between devices: 2.91 us -> 13 us  [the longest x2 5.49 us: reduced_on_torus(): come.append(lax.ppermute(send, BOTH, route))]
    ppermute x14 -> x12, waiting for transfers between devices: 13.5 us -> 8.38 us  [swapped(): return lax.ppermute(block, axis, route)]
    pallas_call x4 -> x11, Pallas kernels: 11.3 us -> 6.47 us  [the longest x1 1.88 us: reduced_on_torus(): call(functools.partial(own_kernel, 4), [turned, table, table, last] + [sh...]
    ppermute x14 -> x12, starting transfers between devices: 12.7 us -> 8.01 us  [swapped(): return lax.ppermute(block, axis, route)]
    ppermute x3 -> x6, starting transfers between devices: 5.57 us -> 9.81 us  [the longest x3 5.82 us: reduced_on_torus(): arrived.append(lax.ppermute(send, 'fsdp', along))]
    unnamed x24 -> x4, local copies, waits for them, and re-layouts: 2.16 us -> 0.01 us
    add x7 -> x0, other arithmetic: 1.99 us -> none  [the longest x1 1.15 us: reduced_by_halves(): a_sum = (a_keep + a_come.astype(jnp.float32)).reshape(2, quarter, left)]
    concatenate x2 -> x0, other arithmetic: 0.88 us -> none  [the longest x1 0.83 us: rotation_tables(): jnp.concatenate([cosine, cosine], -1)]
  transfers between devices with their start and end apart: 17 -> 18, of which waited for: 11 -> 11; matrix products, arithmetic and copies ran while one was open for 10% -> 0% of each run, Pallas kernels for 15% -> 8%
where the time goes in v2:
time: 45.9 us; the launch traced here: 45.8 us
  waiting for transfers between devices  21.4 us (47%)
  starting transfers between devices  17.8 us (39%)
  Pallas kernels  6.47 us (14%)
    ppermute x12, waiting for transfers between devices, swapped(): return lax.ppermute(block, axis, route)  8.38 us
    ppermute x12, starting transfers between devices, swapped(): return lax.ppermute(block, axis, route)  8.01 us
    ppermute x3, starting transfers between devices, reduced_on_torus(): arrived.append(lax.ppermute(send, 'fsdp', along))  5.82 us
    ppermute x2, waiting for transfers between devices, reduced_on_torus(): come.append(lax.ppermute(send, BOTH, route))  5.49 us
    ppermute x1, waiting for transfers between devices, reduced_on_torus(): come = lax.ppermute(send, BOTH, route_after)  4.6 us
    ppermute x3, waiting for transfers between devices, reduced_on_torus(): arrived.append(lax.ppermute(send, 'fsdp', along))  2.92 us
    ppermute x2, starting transfers between devices, reduced_on_torus(): come.append(lax.ppermute(send, BOTH, route))  2.15 us
    pallas_call x1, Pallas kernels, reduced_on_torus(): call(functools.partial(own_kernel, 4), [turned, table, table, last] + [sh...  1.88 us
  transfers between devices with their start and end apart: 18, of which 11 were waited for; matrix products, arithmetic and copies ran while one was open for 0% of the time, Pallas kernels for 8%

profile of v2, /device:TPU:0, one launch (start us, length us, event | category | flops | bytes accessed | tf_op | source)
XLA Modules:
  0.0 45.8 jit_solution(9028211704920478962)
XLA Ops:
  0.0 0.5 %collective-permute-start = (bf16[256,2048]{1,0:T(8,128)(2,1)}, bf16[256,2048]{1,0:T(8,128)(2,1)S(1)}, u32[]{:S(2)}, u32[]{:S(2)}) collective-permute-start(bf16[256,2048]{1,0:T(8,128)(2,1)} %bitcast.5), channel_id=1, source_target_pairs={{0,8},{8,0},{16,24},{24,16},{1,9},{9,1},{17,25},{25,17},{2,10},{10... | collective-permute-start | bytes 3145736 | tf_op jit(solution)/shard_map/ppermute | solution.py:29
  0.5 0.0 collective-permute-start.8
  0.5 0.0 copy-start.1
  0.5 0.5 %collective-permute-start.9 = (bf16[256,512]{1,0:T(8,128)(2,1)}, bf16[256,512]{1,0:T(8,128)(2,1)S(1)}, u32[]{:S(2)}, u32[]{:S(2)}) collective-permute-start(bf16[256,512]{1,0:T(8,128)(2,1)} %bitcast.9), channel_id=1, source_target_pairs={{0,8},{8,0},{16,24},{24,16},{1,9},{9,1},{17,25},{25,17},{2,10},{10... | collective-permute-start | bytes 786440 | tf_op jit(solution)/shard_map/ppermute | solution.py:29
  1.0 2.5 %collective-permute-start.3 = (bf16[16,2048]{1,0:T(8,128)(2,1)}, bf16[16,2048]{1,0:T(8,128)(2,1)S(1)}, u32[]{:S(2)}, u32[]{:S(2)}) collective-permute-start(bf16[16,2048]{1,0:T(8,128)(2,1)} %bitcast.11), channel_id=1, source_target_pairs={{0,16},{8,24},{16,0},{24,8},{1,17},{9,25},{17,1},{25,9},{2,18},{10... | collective-permute-start | bytes 196616 | tf_op jit(solution)/shard_map/ppermute | solution.py:29
  3.5 0.0 copy-done.1
  3.5 0.2 collective-permute-start.1
  3.7 0.9 %collective-permute-done.1.picked_ref = s32[1,16]{1,0:T(1,128)S(1)} collective-permute-done((s32[1,16]{1,0:T(1,128)S(1)}, s32[1,16]{1,0:T(1,128)S(1)}, u32[]{:S(2)}, u32[]{:S(2)}) %collective-permute-start.1) | collective-permute-done | bytes 96 | tf_op jit(solution)/shard_map/ppermute | solution.py:29
  4.7 0.2 collective-permute-start.2
  4.9 1.6 %collective-permute-done.3.refs_2_ = bf16[16,2048]{1,0:T(8,128)(2,1)S(1)} collective-permute-done((bf16[16,2048]{1,0:T(8,128)(2,1)}, bf16[16,2048]{1,0:T(8,128)(2,1)S(1)}, u32[]{:S(2)}, u32[]{:S(2)}) %collective-permute-start.3) | collective-permute-done | bytes 65568 | tf_op jit(solution)/shard_map/ppermute | solution.py:29
  6.5 1.7 %collective-permute-start.6 = (bf16[16,2048]{1,0:T(8,128)(2,1)}, bf16[16,2048]{1,0:T(8,128)(2,1)S(1)}, u32[]{:S(2)}, u32[]{:S(2)}) collective-permute-start(bf16[16,2048]{1,0:T(8,128)(2,1)} %bitcast.14), channel_id=1, source_target_pairs={{0,16},{8,24},{16,0},{24,8},{1,17},{9,25},{17,1},{25,9},{2,18},{10... | collective-permute-start | bytes 196616 | tf_op jit(solution)/shard_map/ppermute | solution.py:29
  8.2 0.0 collective-permute-done.2.refs_1_
  8.2 0.0 collective-permute-start.5
  8.2 2.7 %collective-permute-done.6.refs_6_ = bf16[16,2048]{1,0:T(8,128)(2,1)S(1)} collective-permute-done((bf16[16,2048]{1,0:T(8,128)(2,1)}, bf16[16,2048]{1,0:T(8,128)(2,1)S(1)}, u32[]{:S(2)}, u32[]{:S(2)}) %collective-permute-start.6) | collective-permute-done | bytes 65568 | tf_op jit(solution)/shard_map/ppermute | solution.py:29
  10.9 0.0 collective-permute-start.4
  10.9 0.0 collective-permute-done.features_ref
  10.9 0.5 %collective-permute-start.7 = (bf16[16,2048]{1,0:T(8,128)(2,1)S(1)}, bf16[16,2048]{1,0:T(8,128)(2,1)S(1)}, u32[]{:S(2)}, u32[]{:S(2)}) collective-permute-start(bf16[16,2048]{1,0:T(8,128)(2,1)S(1)} %collective-permute-done.6.refs_6_), channel_id=1, source_target_pairs={{0,8},{8,0},{16,24},{24,16},{1,9},{9,1},{17,25},{25,17},{2,10},{10... | collective-permute-start | bytes 196616 | tf_op jit(solution)/shard_map/ppermute | solution.py:29
  11.4 1.9 %shard_map.91 = (bf16[2048,256]{1,0:T(8,128)(2,1)S(1)}, f32[512,128]{1,0:T(8,128)S(1)}, f32[512,128]{1,0:T(8,128)S(1)}, s32[1,256]{1,0:T(1,128)S(1)}, bf16[256,5...) custom-call(bf16[256,512]{1,0:T(8,128)(2,1)} %bitcast.8, ...), custom_call_target="tpu_custom_call" | custom-call | flops 268435456 | bytes 1048576 | tf_op jit(solution)/shard_map/pallas_call | solution.py:331
  13.3 0.4 shard_map.92
  13.7 0.0 collective-permute-done.5.refs_5_
  13.7 0.0 collective-permute-done.4.refs_3_
  13.7 0.0 collective-permute-done.7.refs_7_
  13.7 0.0 collective-permute-done.8.refs_9_
  13.7 0.0 collective-permute-done.9.refs_11_
  13.8 1.1 %shard_map.93 = (f32[3,2,256]{2,1,0:T(2,128)S(1)}, f32[2,2,256,256]{3,2,1,0:T(8,128)S(1)}, f32[2,2,256,256]{3,2,1,0:T(8,128)S(1)}, bf16[64,1024]{1,0:T(8,128)(2,1)S(1)}, bf16[64,1024]{1,0:T(8,128)(2,1)}) custom-call(bf16[16,2048]{1,0:T(8,128)(2,1)S(1)} %get-tuple-element.33.refs_0_, bf16[16,2048]{1,0:T(8,128)(2,1)S(1)} %collective-permute-done.2.refs_1_, ...), custom_call_target="tpu_custom_call" | custom-call | flops 134217728 | bytes 1048576 | tf_op jit(solution)/shard_map/pallas_call | solution.py:163
  14.8 1.7 %collective-permute-start.10 = (f32[3,2,256]{2,1,0:T(2,128)S(1)}, f32[3,2,256]{2,1,0:T(2,128)S(1)}, u32[]{:S(2)}, u32[]{:S(2)}) collective-permute-start(f32[3,2,256]{2,1,0:T(2,128)S(1)} %get-tuple-element.39.refs_0_), channel_id=1, source_target_pairs={{0,16},{8,24},{16,0},{24,8},{1,17},{9,25},{17,1},{25,9},{2,18},{10... | collective-permute-start | bytes 18440 | tf_op jit(solution)/shard_map/ppermute | solution.py:29
  16.6 1.9 %collective-permute-done.10.refs_1_ = f32[3,2,256]{2,1,0:T(2,128)S(1)} collective-permute-done((f32[3,2,256]{2,1,0:T(2,128)S(1)}, f32[3,2,256]{2,1,0:T(2,128)S(1)}, u32[]{:S(2)}, u32[]{:S(2)}) %collective-permute-start.10) | collective-permute-done | bytes 6176 | tf_op jit(solution)/shard_map/ppermute | solution.py:29
  18.5 0.7 %shard_map.96 = (bf16[2,256,128]{2,1,0:T(8,128)(2,1)S(1)}, bf16[1024,128]{1,0:T(8,128)(2,1)S(1)}) custom-call(f32[3,2,256]{2,1,0:T(2,128)S(1)} %get-tuple-element.39.refs_0_, f32[3,2,256]{2,1,0:T(2,128)S(1)} %collective-permute-done.10.refs_1_, f32[2,2,256,256]{3,2,1,0:T(8,128)S(1)} %get-tuple-element.40.refs_2_, ...), custom_call_target="tpu_custom_call" | custom-call | flops 134217728 | bytes 1048576 | tf_op jit(solution)/shard_map/pallas_call | solution.py:362
  19.2 1.8 %collective-permute-start.12 = (bf16[1024,128]{1,0:T(8,128)(2,1)S(1)}, bf16[1024,128]{1,0:T(8,128)(2,1)S(1)}, u32[]{:S(2)}, u32[]{:S(2)}) collective-permute-start(bf16[1024,128]{1,0:T(8,128)(2,1)S(1)} %get-tuple-element.48), channel_id=1, source_target_pairs={{0,16},{1,17},{2,18},{3,19},{4,20},{5,21},{6,22},{7,23},{8,9},{9,8... | collective-permute-start | bytes 786440 | tf_op jit(solution)/shard_map/ppermute | solution.py:368
  21.0 0.7 %shard_map.94 = (bf16[2,256,128]{2,1,0:T(8,128)(2,1)S(1)}, bf16[1024,128]{1,0:T(8,128)(2,1)S(1)}) custom-call(f32[3,2,256]{2,1,0:T(2,128)S(1)} %get-tuple-element.39.refs_0_, f32[3,2,256]{2,1,0:T(2,128)S(1)} %collective-permute-done.10.refs_1_, f32[2,2,256,256]{3,2,1,0:T(8,128)S(1)} %get-tuple-element.40.refs_2_, ...), custom_call_target="tpu_custom_call" | custom-call | flops 134217728 | bytes 1048576 | tf_op jit(solution)/shard_map/pallas_call | solution.py:362
  21.7 0.3 collective-permute-start.11
  22.1 0.4 shard_map.97.refs_1_
  22.5 0.4 shard_map.95.refs_0_
  22.9 2.7 %collective-permute-done.12.refs_3_ = bf16[1024,128]{1,0:T(8,128)(2,1)S(1)} collective-permute-done((bf16[1024,128]{1,0:T(8,128)(2,1)S(1)}, bf16[1024,128]{1,0:T(8,128)(2,1)S(1)}, u32[]{:S(2)}, u32[]{:S(2)}) %collective-permute-start.12) | collective-permute-done | bytes 262176 | tf_op jit(solution)/shard_map/ppermute | solution.py:368
  25.6 2.8 %collective-permute-done.11.refs_2_ = bf16[1024,128]{1,0:T(8,128)(2,1)S(1)} collective-permute-done((bf16[1024,128]{1,0:T(8,128)(2,1)S(1)}, bf16[1024,128]{1,0:T(8,128)(2,1)S(1)}, u32[]{:S(2)}, u32[]{:S(2)}) %collective-permute-start.11) | collective-permute-done | bytes 262176 | tf_op jit(solution)/shard_map/ppermute | solution.py:368
  28.4 0.1 shard_map.98
  28.5 1.8 %collective-permute-start.13 = (bf16[512,256]{1,0:T(8,128)(2,1)S(1)}, bf16[512,256]{1,0:T(8,128)(2,1)S(1)}, u32[]{:S(2)}, u32[]{:S(2)}) collective-permute-start(bf16[512,256]{1,0:T(8,128)(2,1)S(1)} %get-tuple-element.50), channel_id=1, source_target_pairs={{0,1},{1,0},{2,3},{3,2},{4,5},{5,4},{6,7},{7,6},{8,24},{9,25},{10,... | collective-permute-start | bytes 786440 | tf_op jit(solution)/shard_map/ppermute | solution.py:378
  30.4 4.6 %collective-permute-done.13.come_ref = bf16[512,256]{1,0:T(8,128)(2,1)S(1)} collective-permute-done((bf16[512,256]{1,0:T(8,128)(2,1)S(1)}, bf16[512,256]{1,0:T(8,128)(2,1)S(1)}, u32[]{:S(2)}, u32[]{:S(2)}) %collective-permute-start.13) | collective-permute-done | bytes 262176 | tf_op jit(solution)/shard_map/ppermute | solution.py:378
  35.0 1.9 %collective-permute-start.14 = (bf16[128,256]{1,0:T(8,128)(2,1)S(1)}, bf16[128,256]{1,0:T(8,128)(2,1)S(1)}, u32[]{:S(2)}, u32[]{:S(2)}) collective-permute-start(bf16[128,256]{1,0:T(8,128)(2,1)S(1)} %get-tuple-element.52), channel_id=1, source_target_pairs={{0,2},{1,3},{2,4},{3,5},{4,6},{5,7},{6,0},{7,1},{8,10},{9,11},{10,... | collective-permute-start | bytes 196616 | tf_op jit(solution)/shard_map/ppermute | solution.py:389
  36.9 2.6 %collective-permute-start.15 = (bf16[128,256]{1,0:T(8,128)(2,1)S(1)}, bf16[128,256]{1,0:T(8,128)(2,1)S(1)}, u32[]{:S(2)}, u32[]{:S(2)}) collective-permute-start(bf16[128,256]{1,0:T(8,128)(2,1)S(1)} %get-tuple-element.53), channel_id=1, source_target_pairs={{0,4},{1,5},{2,6},{3,7},{4,0},{5,1},{6,2},{7,3},{8,12},{9,13},{10,... | collective-permute-start | bytes 196616 | tf_op jit(solution)/shard_map/ppermute | solution.py:389
  39.5 1.3 %collective-permute-start.16 = (bf16[128,256]{1,0:T(8,128)(2,1)S(1)}, bf16[128,256]{1,0:T(8,128)(2,1)S(1)}, u32[]{:S(2)}, u32[]{:S(2)}) collective-permute-start(bf16[128,256]{1,0:T(8,128)(2,1)S(1)} %get-tuple-element.54), channel_id=1, source_target_pairs={{0,6},{1,7},{2,0},{3,1},{4,2},{5,3},{6,4},{7,5},{8,14},{9,15},{10,... | collective-permute-start | bytes 196616 | tf_op jit(solution)/shard_map/ppermute | solution.py:389
  40.8 0.3 collective-permute-done.14.refs_1_
  41.2 0.9 %collective-permute-done.15.refs_2_ = bf16[128,256]{1,0:T(8,128)(2,1)S(1)} collective-permute-done((bf16[128,256]{1,0:T(8,128)(2,1)S(1)}, bf16[128,256]{1,0:T(8,128)(2,1)S(1)}, u32[]{:S(2)}, u32[]{:S(2)}) %collective-permute-start.15) | collective-permute-done | bytes 65568 | tf_op jit(solution)/shard_map/ppermute | solution.py:389
  42.1 1.7 %collective-permute-done.16.refs_3_ = bf16[128,256]{1,0:T(8,128)(2,1)S(1)} collective-permute-done((bf16[128,256]{1,0:T(8,128)(2,1)S(1)}, bf16[128,256]{1,0:T(8,128)(2,1)S(1)}, u32[]{:S(2)}, u32[]{:S(2)}) %collective-permute-start.16) | collective-permute-done | bytes 65568 | tf_op jit(solution)/shard_map/ppermute | solution.py:389
  43.8 0.1 collective-permute-start.17
  43.9 1.2 %collective-permute-done.17.there_ref = f32[64,256]{1,0:T(8,128)S(1)} collective-permute-done((f32[64,256]{1,0:T(8,128)S(1)}, f32[64,256]{1,0:T(8,128)S(1)}, u32[]{:S(2)}, u32[]{:S(2)}) %collective-permute-start.17) | collective-permute-done | bytes 65568 | tf_op jit(solution)/shard_map/ppermute | solution.py:29
  45.1 0.0 copy-done
  45.1 0.7 %shard_map.101 = f32[64,512]{1,0:T(8,128)} custom-call(f32[64,256]{1,0:T(8,128)S(1)} %get-tuple-element.55.here_ref, f32[64,256]{1,0:T(8,128)S(1)} %collective-permute-done.17.there_ref, f32[64,512]{1,0:T(8,128)S(1)} %copy-done), custom_call_target="tpu_custom_call" | custom-call | flops 1048576 | bytes 1048576 | tf_op jit(solution)/shard_map/pallas_call | solution.py:393
  (3 shorter events, 0.1 us)
Async XLA Ops:
  0.0 10.9 %collective-permute-start = (bf16[256,2048]{1,0:T(8,128)(2,1)}, bf16[256,2048]{1,0:T(8,128)(2,1)S(1)}, u32[]{:S(2)}, u32[]{:S(2)}) collective-permute-start(bf16[256,2048]{1,0:T(8,128)(2,1)} %bitcast.5), channel_id=1, source_target_pairs={{0,8},{8,0},{16,24},{24,16},{1,9},{9,1},{17,25},{25,17},{2,10},{10... | collective-permute-start | bytes 3145736 | tf_op jit(solution)/shard_map/ppermute | solution.py:29
  0.5 13.2 %collective-permute-start.8 = (bf16[256,512]{1,0:T(8,128)(2,1)}, bf16[256,512]{1,0:T(8,128)(2,1)S(1)}, u32[]{:S(2)}, u32[]{:S(2)}) collective-permute-start(bf16[256,512]{1,0:T(8,128)(2,1)} %bitcast.7), channel_id=1, source_target_pairs={{0,8},{8,0},{16,24},{24,16},{1,9},{9,1},{17,25},{25,17},{2,10},{10... | collective-permute-start | bytes 786440 | tf_op jit(solution)/shard_map/ppermute | solution.py:29
  0.5 3.0 %copy-start.1 = (s32[1,16]{1,0:T(1,128)S(1)}, s32[1,16]{1,0:T(1,128)}, u32[]{:S(2)}) copy-start(s32[1,16]{1,0:T(1,128)} %refs_4_.1) | copy-start | bytes 196
  0.5 13.2 %collective-permute-start.9 = (bf16[256,512]{1,0:T(8,128)(2,1)}, bf16[256,512]{1,0:T(8,128)(2,1)S(1)}, u32[]{:S(2)}, u32[]{:S(2)}) collective-permute-start(bf16[256,512]{1,0:T(8,128)(2,1)} %bitcast.9), channel_id=1, source_target_pairs={{0,8},{8,0},{16,24},{24,16},{1,9},{9,1},{17,25},{25,17},{2,10},{10... | collective-permute-start | bytes 786440 | tf_op jit(solution)/shard_map/ppermute | solution.py:29
  1.0 5.4 %collective-permute-start.3 = (bf16[16,2048]{1,0:T(8,128)(2,1)}, bf16[16,2048]{1,0:T(8,128)(2,1)S(1)}, u32[]{:S(2)}, u32[]{:S(2)}) collective-permute-start(bf16[16,2048]{1,0:T(8,128)(2,1)} %bitcast.11), channel_id=1, source_target_pairs={{0,16},{8,24},{16,0},{24,8},{1,17},{9,25},{17,1},{25,9},{2,18},{10... | collective-permute-start | bytes 196616 | tf_op jit(solution)/shard_map/ppermute | solution.py:29
  3.5 1.2 %collective-permute-start.1 = (s32[1,16]{1,0:T(1,128)S(1)}, s32[1,16]{1,0:T(1,128)S(1)}, u32[]{:S(2)}, u32[]{:S(2)}) collective-permute-start(s32[1,16]{1,0:T(1,128)S(1)} %copy-done.1), channel_id=1, source_target_pairs={{0,8},{8,0},{16,24},{24,16},{1,9},{9,1},{17,25},{25,17},{2,10},{10... | collective-permute-start | bytes 200 | tf_op jit(solution)/shard_map/ppermute | solution.py:29
  4.7 3.6 %collective-permute-start.2 = (bf16[16,2048]{1,0:T(8,128)(2,1)}, bf16[16,2048]{1,0:T(8,128)(2,1)S(1)}, u32[]{:S(2)}, u32[]{:S(2)}) collective-permute-start(bf16[16,2048]{1,0:T(8,128)(2,1)} %bitcast.12), channel_id=1, source_target_pairs={{0,8},{8,0},{16,24},{24,16},{1,9},{9,1},{17,25},{25,17},{2,10},{10... | collective-permute-start | bytes 196616 | tf_op jit(solution)/shard_map/ppermute | solution.py:29
  6.5 4.5 %collective-permute-start.6 = (bf16[16,2048]{1,0:T(8,128)(2,1)}, bf16[16,2048]{1,0:T(8,128)(2,1)S(1)}, u32[]{:S(2)}, u32[]{:S(2)}) collective-permute-start(bf16[16,2048]{1,0:T(8,128)(2,1)} %bitcast.14), channel_id=1, source_target_pairs={{0,16},{8,24},{16,0},{24,8},{1,17},{9,25},{17,1},{25,9},{2,18},{10... | collective-permute-start | bytes 196616 | tf_op jit(solution)/shard_map/ppermute | solution.py:29
  8.2 5.5 %collective-permute-start.5 = (bf16[16,2048]{1,0:T(8,128)(2,1)}, bf16[16,2048]{1,0:T(8,128)(2,1)S(1)}, u32[]{:S(2)}, u32[]{:S(2)}) collective-permute-start(bf16[16,2048]{1,0:T(8,128)(2,1)} %bitcast.15), channel_id=1, source_target_pairs={{0,8},{8,0},{16,24},{24,16},{1,9},{9,1},{17,25},{25,17},{2,10},{10... | collective-permute-start | bytes 196616 | tf_op jit(solution)/shard_map/ppermute | solution.py:29
  10.9 2.8 %collective-permute-start.4 = (bf16[16,2048]{1,0:T(8,128)(2,1)S(1)}, bf16[16,2048]{1,0:T(8,128)(2,1)S(1)}, u32[]{:S(2)}, u32[]{:S(2)}) collective-permute-start(bf16[16,2048]{1,0:T(8,128)(2,1)S(1)} %collective-permute-done.3.refs_2_), channel_id=1, source_target_pairs={{0,8},{8,0},{16,24},{24,16},{1,9},{9,1},{17,25},{25,17},{2,10},{10... | collective-permute-start | bytes 196616 | tf_op jit(solution)/shard_map/ppermute | solution.py:29
  10.9 2.8 %collective-permute-start.7 = (bf16[16,2048]{1,0:T(8,128)(2,1)S(1)}, bf16[16,2048]{1,0:T(8,128)(2,1)S(1)}, u32[]{:S(2)}, u32[]{:S(2)}) collective-permute-start(bf16[16,2048]{1,0:T(8,128)(2,1)S(1)} %collective-permute-done.6.refs_6_), channel_id=1, source_target_pairs={{0,8},{8,0},{16,24},{24,16},{1,9},{9,1},{17,25},{25,17},{2,10},{10... | collective-permute-start | bytes 196616 | tf_op jit(solution)/shard_map/ppermute | solution.py:29
  14.8 3.6 %collective-permute-start.10 = (f32[3,2,256]{2,1,0:T(2,128)S(1)}, f32[3,2,256]{2,1,0:T(2,128)S(1)}, u32[]{:S(2)}, u32[]{:S(2)}) collective-permute-start(f32[3,2,256]{2,1,0:T(2,128)S(1)} %get-tuple-element.39.refs_0_), channel_id=1, source_target_pairs={{0,16},{8,24},{16,0},{24,8},{1,17},{9,25},{17,1},{25,9},{2,18},{10... | collective-permute-start | bytes 18440 | tf_op jit(solution)/shard_map/ppermute | solution.py:29
  19.2 6.4 %collective-permute-start.12 = (bf16[1024,128]{1,0:T(8,128)(2,1)S(1)}, bf16[1024,128]{1,0:T(8,128)(2,1)S(1)}, u32[]{:S(2)}, u32[]{:S(2)}) collective-permute-start(bf16[1024,128]{1,0:T(8,128)(2,1)S(1)} %get-tuple-element.48), channel_id=1, source_target_pairs={{0,16},{1,17},{2,18},{3,19},{4,20},{5,21},{6,22},{7,23},{8,9},{9,8... | collective-permute-start | bytes 786440 | tf_op jit(solution)/shard_map/ppermute | solution.py:368
  21.7 6.7 %collective-permute-start.11 = (bf16[1024,128]{1,0:T(8,128)(2,1)S(1)}, bf16[1024,128]{1,0:T(8,128)(2,1)S(1)}, u32[]{:S(2)}, u32[]{:S(2)}) collective-permute-start(bf16[1024,128]{1,0:T(8,128)(2,1)S(1)} %get-tuple-element.47), channel_id=1, source_target_pairs={{0,16},{1,17},{2,18},{3,19},{4,20},{5,21},{6,22},{7,23},{8,9},{9,8... | collective-permute-start | bytes 786440 | tf_op jit(solution)/shard_map/ppermute | solution.py:368
  28.5 6.4 %collective-permute-start.13 = (bf16[512,256]{1,0:T(8,128)(2,1)S(1)}, bf16[512,256]{1,0:T(8,128)(2,1)S(1)}, u32[]{:S(2)}, u32[]{:S(2)}) collective-permute-start(bf16[512,256]{1,0:T(8,128)(2,1)S(1)} %get-tuple-element.50), channel_id=1, source_target_pairs={{0,1},{1,0},{2,3},{3,2},{4,5},{5,4},{6,7},{7,6},{8,24},{9,25},{10,... | collective-permute-start | bytes 786440 | tf_op jit(solution)/shard_map/ppermute | solution.py:378
  35.0 6.2 %collective-permute-start.14 = (bf16[128,256]{1,0:T(8,128)(2,1)S(1)}, bf16[128,256]{1,0:T(8,128)(2,1)S(1)}, u32[]{:S(2)}, u32[]{:S(2)}) collective-permute-start(bf16[128,256]{1,0:T(8,128)(2,1)S(1)} %get-tuple-element.52), channel_id=1, source_target_pairs={{0,2},{1,3},{2,4},{3,5},{4,6},{5,7},{6,0},{7,1},{8,10},{9,11},{10,... | collective-permute-start | bytes 196616 | tf_op jit(solution)/shard_map/ppermute | solution.py:389
  36.9 5.2 %collective-permute-start.15 = (bf16[128,256]{1,0:T(8,128)(2,1)S(1)}, bf16[128,256]{1,0:T(8,128)(2,1)S(1)}, u32[]{:S(2)}, u32[]{:S(2)}) collective-permute-start(bf16[128,256]{1,0:T(8,128)(2,1)S(1)} %get-tuple-element.53), channel_id=1, source_target_pairs={{0,4},{1,5},{2,6},{3,7},{4,0},{5,1},{6,2},{7,3},{8,12},{9,13},{10,... | collective-permute-start | bytes 196616 | tf_op jit(solution)/shard_map/ppermute | solution.py:389
  39.5 4.3 %collective-permute-start.16 = (bf16[128,256]{1,0:T(8,128)(2,1)S(1)}, bf16[128,256]{1,0:T(8,128)(2,1)S(1)}, u32[]{:S(2)}, u32[]{:S(2)}) collective-permute-start(bf16[128,256]{1,0:T(8,128)(2,1)S(1)} %get-tuple-element.54), channel_id=1, source_target_pairs={{0,6},{1,7},{2,0},{3,1},{4,2},{5,3},{6,4},{7,5},{8,14},{9,15},{10,... | collective-permute-start | bytes 196616 | tf_op jit(solution)/shard_map/ppermute | solution.py:389
  43.8 1.4 %copy-start = (f32[64,512]{1,0:T(8,128)S(1)}, f32[64,512]{1,0:T(8,128)}, u32[]{:S(2)}) copy-start(f32[64,512]{1,0:T(8,128)} %hessian_ref.1) | copy-start | bytes 393220
  43.8 1.3 %collective-permute-start.17 = (f32[64,256]{1,0:T(8,128)S(1)}, f32[64,256]{1,0:T(8,128)S(1)}, u32[]{:S(2)}, u32[]{:S(2)}) collective-permute-start(f32[64,256]{1,0:T(8,128)S(1)} %get-tuple-element.56), channel_id=1, source_target_pairs={{0,8},{8,0},{16,24},{24,16},{1,9},{9,1},{17,25},{25,17},{2,10},{10... | collective-permute-start | bytes 196616 | tf_op jit(solution)/shard_map/ppermute | solution.py:29

commit v3 on v2

--- a/solution.py
+++ b/solution.py
@@ -22,6 +22,7 @@
 HBM = pl.BlockSpec(memory_space=pltpu.HBM)
 NT_DIMS = (((1,), (1,)), ((), ()))
 BOTH = ("blk", "fsdp")
+TRAVEL, STAY, EARLY = ((1, 2), (3, 0)), ((1, 2), (3, 0)), 2
 
 
 def swapped(block, axis, bits):
@@ -209,46 +210,51 @@
         out_ref[:, group * HEAD_DIM : (group + 1) * HEAD_DIM] = blocks[0]
 
 
-def send_kernel(group, *refs):
+def along_z(rows, distance):
+    return pl.multiple_of(((position()[3] + distance) & 3) * rows, rows)
+
+
+def put_product(own_ref, far_ref, unrot_ref, leaves, turns, distances, out_ref):
+    first, second = first_second()
+    size = out_ref.shape[0] // len(distances)
+    quarter = (first ^ leaves) * 2 + (second ^ turns)
+    for number, distance in enumerate(distances):
+        start = pl.multiple_of(quarter * 4 * size, size) + along_z(size, distance)
+        at = pl.ds(pl.multiple_of(start, size), size)
+        total = jnp.dot(
+            own_ref[at, :], unrot_ref[0], preferred_element_type=jnp.float32
+        ) + jnp.dot(far_ref[at, :], unrot_ref[1], preferred_element_type=jnp.float32)
+        out_ref[number * size : (number + 1) * size, :] = total.astype(out_ref.dtype)
+
+
+def send_kernel(chunks_out, *refs):
     stats_refs, saved_refs = refs[:2], refs[2:7]
-    own_ref, far_ref, unrot_ref, out_ref = refs[7:]
-    own, far = key_gradient(group, stats_refs, *saved_refs)
-    unrot_ref[0] = own
-    unrot_ref[1] = far
-    half = out_ref.shape[0]
-    at = pl.ds(pl.multiple_of((1 - first_second()[0]) * half, half), half)
-    out_ref[...] = (
-        jnp.dot(own_ref[at, :], own, preferred_element_type=jnp.float32)
-        + jnp.dot(far_ref[at, :], far, preferred_element_type=jnp.float32)
-    ).astype(jnp.bfloat16)
-
-
-def keep_kernel(own_ref, far_ref, unrot_ref, out_ref):
-    half = out_ref.shape[0]
-    at = pl.ds(pl.multiple_of(first_second()[0] * half, half), half)
-    out_ref[...] = jnp.dot(
-        own_ref[at, :], unrot_ref[0], preferred_element_type=jnp.float32
-    ) + jnp.dot(far_ref[at, :], unrot_ref[1], preferred_element_type=jnp.float32)
-
-
-def halve_kernel(*refs):
-    keep_refs, come_refs, (send_ref, hold_ref) = refs[:2], refs[2:4], refs[4:]
-    half = hold_ref.shape[0]
-    second = first_second()[1]
-    for place, out_ref in ((1 - second, send_ref), (second, hold_ref)):
-        at = pl.ds(pl.multiple_of(place * half, half), half)
-        for head in range(2):
-            total = keep_refs[head][at, :] + come_refs[head][at, :].astype(jnp.float32)
-            out_ref[:, head * HEAD_DIM : (head + 1) * HEAD_DIM] = total.astype(out_ref.dtype)
-
-
-def quarter_kernel(hold_ref, come_ref, *outs):
+    own_ref, far_ref, unrot_ref = refs[7:10]
+    for group in range(stats_refs[0].shape[1]):
+        columns = pl.ds(group * HEAD_DIM, HEAD_DIM)
+        for part, block in enumerate(key_gradient(group, stats_refs, *saved_refs)):
+            unrot_ref[part, :, columns] = block
+    for chunk, out_ref in zip(chunks_out, refs[10:]):
+        put_product(own_ref, far_ref, unrot_ref, *chunk, out_ref)
+
+
+def rest_kernel(chunks_out, own_ref, far_ref, unrot_ref, *outs):
+    for chunk, out_ref in zip(chunks_out, outs):
+        put_product(own_ref, far_ref, unrot_ref, *chunk, out_ref)
+
+
+def add_kernel(start, keep_ref, come_ref, out_ref):
+    at = pl.ds(start, out_ref.shape[0])
+    out_ref[...] = (keep_ref[at, :] + come_ref[...].astype(jnp.float32)).astype(jnp.bfloat16)
+
+
+def total_kernel(keep_start, stay_start, keep_ref, stay_ref, come_ref, *outs):
     rows = outs[0].shape[0]
-    z = position()[3]
-    for distance in (2, 3, 1, 0):
-        at = pl.ds(pl.multiple_of(((z + distance) & 3) * rows, rows), rows)
-        total = hold_ref[at, :] + come_ref[at, :].astype(jnp.float32)
-        outs[distance][...] = total.astype(outs[distance].dtype)
+    for number, out_ref in enumerate(outs):
+        total = keep_ref[pl.ds(keep_start + number * rows, rows), :]
+        total += stay_ref[pl.ds(stay_start + number * rows, rows), :].astype(jnp.float32)
+        total += come_ref[pl.ds(number * rows, rows), :].astype(jnp.float32)
+        out_ref[...] = total.astype(out_ref.dtype)
 
 
 def last_kernel(*refs):
@@ -354,40 +360,62 @@
     other = swapped(stats, "blk", 2)
 
     half_rows = normed.shape[1] // 2
-    work = 2 * half_rows * 2 * tokens * HEAD_DIM
+    work = 2 * half_rows * 2 * tokens * heads * HEAD_DIM
     route = [(i, i ^ (1 if (i // 8) % 2 else 16)) for i in range(32)]
     route_after = [(i, i ^ (16 if (i // 8) % 2 else 1)) for i in range(32)]
-    keeps, come = [], []
-    for group in range(heads):
-        unrot, send = call(
-            functools.partial(send_kernel, group),
-            [shape((2, tokens, HEAD_DIM), jnp.bfloat16), shape((half_rows, HEAD_DIM), jnp.bfloat16)],
-            [VMEM] * 9,
-            work,
-        )(stats, other, expo, grads, query, cosine, sine, own, far)
+    rows, wide = half_rows // 8, heads * HEAD_DIM
+
+    def block(chunk, dtype=jnp.bfloat16):
+        return shape((rows * len(chunk), wide), dtype)
+
+    early = [(1, 1, chunk) for chunk in TRAVEL[:EARLY]]
+    late = [(1, 1, chunk) for chunk in TRAVEL[EARLY:]] + [(1, 0, chunk) for chunk in STAY]
+    unrot, *sends = call(
+        functools.partial(send_kernel, early),
+        [shape((2, tokens, wide), jnp.bfloat16)] + [block(chunk[2]) for chunk in early],
+        [VMEM] * 9,
+        work,
+    )(stats, other, expo, grads, query, cosine, sine, own, far)
+    everywhere = sum(TRAVEL, ())
+    late.append((0, 1, everywhere))
+    *more, turn_keep = call(
+        functools.partial(rest_kernel, late),
+        [block(chunk[2]) for chunk in late[:-1]] + [block(everywhere, jnp.float32)],
+        [VMEM] * 3,
+        work,
+    )(own, far, unrot)
+    sends += more
+    (stay_keep,) = call(
+        functools.partial(rest_kernel, [(0, 0, everywhere)]),
+        [block(everywhere, jnp.float32)],
+        [VMEM] * 3,
+        work,
+    )(own, far, unrot)
+    come = []
+    for send in sends:
         come.append(lax.ppermute(send, BOTH, route))
-        keeps.append(
-            call(keep_kernel, shape((half_rows, HEAD_DIM), jnp.float32), [VMEM] * 3, work)(
-                own, far, unrot
-            )
-        )
-    block = half_rows // 2, heads * HEAD_DIM
-    send, hold = call(
-        halve_kernel, [shape(block, jnp.bfloat16), shape(block, jnp.float32)], [VMEM] * 4, 1 << 20
-    )(*keeps, *come)
-    come = lax.ppermute(send, BOTH, route_after)
-    piece = block[0] // 4, block[1]
-    mine, *sends = call(
-        quarter_kernel,
-        [shape(piece, jnp.float32)] + [shape(piece, jnp.bfloat16)] * 3,
-        [VMEM] * 2,
-        1 << 20,
-    )(hold, come)
+    totals = []
+    for number, chunk in enumerate(TRAVEL):
+        first = everywhere.index(chunk[0])
+        send = call(
+            functools.partial(add_kernel, rows * first), block(chunk), [VMEM] * 2, 1 << 20
+        )(turn_keep, come[number])
+        arrived = lax.ppermute(send, BOTH, route_after)
+        outs = [block((0,), jnp.bfloat16 if distance else jnp.float32) for distance in chunk]
+        source = next(i for i, other in enumerate(STAY) if chunk[0] in other)
+        inside = STAY[source].index(chunk[0])
+        totals += call(
+            functools.partial(total_kernel, rows * first, rows * inside),
+            outs,
+            [VMEM] * 3,
+            1 << 20,
+        )(stay_keep, come[len(TRAVEL) + source], arrived)
+    sends, mine = totals[:3], totals[3]
     arrived = []
-    for distance, send in enumerate(sends, 1):
+    for distance, send in zip(everywhere, sends):
         along = [(i, (i + 2 * distance) % 8) for i in range(8)]
         arrived.append(lax.ppermute(send, "fsdp", along))
-    columns = shape((out_rows, block[1]), jnp.float32)
+    columns = shape((out_rows, wide), jnp.float32)
     here, there = call(last_kernel, [columns] * 2, [VMEM] * 4, 1 << 20)(mine, *arrived)
     there = swapped(there, "blk", 1)
     return call(

time: 45.9 us -> 43.1 us (0.939)
  waiting for transfers between devices: 21.4 us -> 14.2 us
  starting transfers between devices: 17.8 us -> 23 us
  Pallas kernels: 6.47 us -> 5.61 us
    ppermute x1 -> x2, waiting for transfers between devices: 4.6 us -> 0.01 us  [reduced_on_torus(): arrived = lax.ppermute(send, BOTH, route_after)]
    ppermute x2 -> x4, waiting for transfers between devices: 5.49 us -> 1.79 us  [reduced_on_torus(): come.append(lax.ppermute(send, BOTH, route))]
    ppermute x2 -> x4, starting transfers between devices: 2.15 us -> 5.4 us  [reduced_on_torus(): come.append(lax.ppermute(send, BOTH, route))]
    ppermute x1 -> x2, starting transfers between devices: 1.84 us -> 2.92 us  [reduced_on_torus(): arrived = lax.ppermute(send, BOTH, route_after)]
    ppermute x3, waiting for transfers between devices: 2.92 us -> 3.99 us  [reduced_on_torus(): arrived.append(lax.ppermute(send, 'fsdp', along))]
    ppermute x3, starting transfers between devices: 5.82 us -> 6.7 us  [reduced_on_torus(): arrived.append(lax.ppermute(send, 'fsdp', along))]
    pallas_call x6 -> x7, Pallas kernels: 2.45 us -> 1.59 us  [the longest x1 0.72 us: reduced_on_torus(): call(functools.partial(send_kernel, early), [shape((2, tokens, wide), jnp...]
  transfers between devices with their start and end apart: 18 -> 21, of which waited for: 11 -> 9; matrix products, arithmetic and copies ran while one was open for 0% -> 0% of each run, Pallas kernels for 8% -> 7%
where the time goes in v3:
time: 43.1 us; the launch traced here: 42.9 us
  starting transfers between devices  23 us (53%)
  waiting for transfers between devices  14.2 us (33%)
  Pallas kernels  5.61 us (13%)
    ppermute x12, waiting for transfers between devices, swapped(): return lax.ppermute(block, axis, route)  8.38 us
    ppermute x12, starting transfers between devices, swapped(): return lax.ppermute(block, axis, route)  8.01 us
    ppermute x3, starting transfers between devices, reduced_on_torus(): arrived.append(lax.ppermute(send, 'fsdp', along))  6.7 us
    ppermute x4, starting transfers between devices, reduced_on_torus(): come.append(lax.ppermute(send, BOTH, route))  5.4 us
    ppermute x3, waiting for transfers between devices, reduced_on_torus(): arrived.append(lax.ppermute(send, 'fsdp', along))  3.99 us
    ppermute x2, starting transfers between devices, reduced_on_torus(): arrived = lax.ppermute(send, BOTH, route_after)  2.92 us
    pallas_call x1, Pallas kernels, reduced_on_torus(): call(functools.partial(own_kernel, 4), [turned, table, table, last] + [sh...  1.88 us
    ppermute x4, waiting for transfers between devices, reduced_on_torus(): come.append(lax.ppermute(send, BOTH, route))  1.79 us
  transfers between devices with their start and end apart: 21, of which 9 were waited for; matrix products, arithmetic and copies ran while one was open for 0% of the time, Pallas kernels for 7%

profile of v3, /device:TPU:0, one launch (start us, length us, event | category | flops | bytes accessed | tf_op | source)
XLA Modules:
  0.0 42.9 jit_solution(15179377476602039373)
XLA Ops:
  0.0 0.5 %collective-permute-start = (bf16[256,2048]{1,0:T(8,128)(2,1)}, bf16[256,2048]{1,0:T(8,128)(2,1)S(1)}, u32[]{:S(2)}, u32[]{:S(2)}) collective-permute-start(bf16[256,2048]{1,0:T(8,128)(2,1)} %bitcast.5), channel_id=1, source_target_pairs={{0,8},{8,0},{16,24},{24,16},{1,9},{9,1},{17,25},{25,17},{2,10},{10... | collective-permute-start | bytes 3145736 | tf_op jit(solution)/shard_map/ppermute | solution.py:30
  0.5 0.0 collective-permute-start.8
  0.5 0.5 %collective-permute-start.9 = (bf16[256,512]{1,0:T(8,128)(2,1)}, bf16[256,512]{1,0:T(8,128)(2,1)S(1)}, u32[]{:S(2)}, u32[]{:S(2)}) collective-permute-start(bf16[256,512]{1,0:T(8,128)(2,1)} %bitcast.9), channel_id=1, source_target_pairs={{0,8},{8,0},{16,24},{24,16},{1,9},{9,1},{17,25},{25,17},{2,10},{10... | collective-permute-start | bytes 786440 | tf_op jit(solution)/shard_map/ppermute | solution.py:30
  1.0 2.5 %collective-permute-start.3 = (bf16[16,2048]{1,0:T(8,128)(2,1)}, bf16[16,2048]{1,0:T(8,128)(2,1)S(1)}, u32[]{:S(2)}, u32[]{:S(2)}) collective-permute-start(bf16[16,2048]{1,0:T(8,128)(2,1)} %bitcast.11), channel_id=1, source_target_pairs={{0,16},{8,24},{16,0},{24,8},{1,17},{9,25},{17,1},{25,9},{2,18},{10... | collective-permute-start | bytes 196616 | tf_op jit(solution)/shard_map/ppermute | solution.py:30
  3.5 0.2 collective-permute-start.1
  3.7 0.9 %collective-permute-done.1.picked_ref = s32[1,16]{1,0:T(1,128)S(1)} collective-permute-done((s32[1,16]{1,0:T(1,128)S(1)}, s32[1,16]{1,0:T(1,128)S(1)}, u32[]{:S(2)}, u32[]{:S(2)}) %collective-permute-start.1) | collective-permute-done | bytes 96 | tf_op jit(solution)/shard_map/ppermute | solution.py:30
  4.7 0.2 collective-permute-start.2
  4.9 1.6 %collective-permute-done.3.refs_2_ = bf16[16,2048]{1,0:T(8,128)(2,1)S(1)} collective-permute-done((bf16[16,2048]{1,0:T(8,128)(2,1)}, bf16[16,2048]{1,0:T(8,128)(2,1)S(1)}, u32[]{:S(2)}, u32[]{:S(2)}) %collective-permute-start.3) | collective-permute-done | bytes 65568 | tf_op jit(solution)/shard_map/ppermute | solution.py:30
  6.5 1.7 %collective-permute-start.6 = (bf16[16,2048]{1,0:T(8,128)(2,1)}, bf16[16,2048]{1,0:T(8,128)(2,1)S(1)}, u32[]{:S(2)}, u32[]{:S(2)}) collective-permute-start(bf16[16,2048]{1,0:T(8,128)(2,1)} %bitcast.14), channel_id=1, source_target_pairs={{0,16},{8,24},{16,0},{24,8},{1,17},{9,25},{17,1},{25,9},{2,18},{10... | collective-permute-start | bytes 196616 | tf_op jit(solution)/shard_map/ppermute | solution.py:30
  8.2 0.0 collective-permute-done.2.refs_1_
  8.2 0.0 collective-permute-start.5
  8.2 2.7 %collective-permute-done.6.refs_6_ = bf16[16,2048]{1,0:T(8,128)(2,1)S(1)} collective-permute-done((bf16[16,2048]{1,0:T(8,128)(2,1)}, bf16[16,2048]{1,0:T(8,128)(2,1)S(1)}, u32[]{:S(2)}, u32[]{:S(2)}) %collective-permute-start.6) | collective-permute-done | bytes 65568 | tf_op jit(solution)/shard_map/ppermute | solution.py:30
  10.9 0.0 collective-permute-start.4
  10.9 0.0 collective-permute-done.features_ref
  10.9 0.5 %collective-permute-start.7 = (bf16[16,2048]{1,0:T(8,128)(2,1)S(1)}, bf16[16,2048]{1,0:T(8,128)(2,1)S(1)}, u32[]{:S(2)}, u32[]{:S(2)}) collective-permute-start(bf16[16,2048]{1,0:T(8,128)(2,1)S(1)} %collective-permute-done.6.refs_6_), channel_id=1, source_target_pairs={{0,8},{8,0},{16,24},{24,16},{1,9},{9,1},{17,25},{25,17},{2,10},{10... | collective-permute-start | bytes 196616 | tf_op jit(solution)/shard_map/ppermute | solution.py:30
  11.4 1.9 %shard_map.91 = (bf16[2048,256]{1,0:T(8,128)(2,1)S(1)}, f32[512,128]{1,0:T(8,128)S(1)}, f32[512,128]{1,0:T(8,128)S(1)}, s32[1,256]{1,0:T(1,128)S(1)}, bf16[256,5...) custom-call(bf16[256,512]{1,0:T(8,128)(2,1)} %bitcast.8, ...), custom_call_target="tpu_custom_call" | custom-call | flops 268435456 | bytes 1048576 | tf_op jit(solution)/shard_map/pallas_call | solution.py:337
  13.3 0.4 shard_map.92
  13.7 0.0 collective-permute-done.5.refs_5_
  13.7 0.0 collective-permute-done.4.refs_3_
  13.7 0.0 collective-permute-done.7.refs_7_
  13.7 0.0 collective-permute-done.8.refs_9_
  13.7 0.0 collective-permute-done.9.refs_11_
  13.7 1.1 %shard_map.93 = (f32[3,2,256]{2,1,0:T(2,128)S(1)}, f32[2,2,256,256]{3,2,1,0:T(8,128)S(1)}, f32[2,2,256,256]{3,2,1,0:T(8,128)S(1)}, bf16[64,1024]{1,0:T(8,128)(2,1)S(1)}, bf16[64,1024]{1,0:T(8,128)(2,1)}) custom-call(bf16[16,2048]{1,0:T(8,128)(2,1)S(1)} %get-tuple-element.33.refs_0_, bf16[16,2048]{1,0:T(8,128)(2,1)S(1)} %collective-permute-done.2.refs_1_, ...), custom_call_target="tpu_custom_call" | custom-call | flops 134217728 | bytes 1048576 | tf_op jit(solution)/shard_map/pallas_call | solution.py:164
  14.8 1.7 %collective-permute-start.10 = (f32[3,2,256]{2,1,0:T(2,128)S(1)}, f32[3,2,256]{2,1,0:T(2,128)S(1)}, u32[]{:S(2)}, u32[]{:S(2)}) collective-permute-start(f32[3,2,256]{2,1,0:T(2,128)S(1)} %get-tuple-element.39.refs_0_), channel_id=1, source_target_pairs={{0,16},{8,24},{16,0},{24,8},{1,17},{9,25},{17,1},{25,9},{2,18},{10... | collective-permute-start | bytes 18440 | tf_op jit(solution)/shard_map/ppermute | solution.py:30
  16.6 1.9 %collective-permute-done.10.refs_1_ = f32[3,2,256]{2,1,0:T(2,128)S(1)} collective-permute-done((f32[3,2,256]{2,1,0:T(2,128)S(1)}, f32[3,2,256]{2,1,0:T(2,128)S(1)}, u32[]{:S(2)}, u32[]{:S(2)}) %collective-permute-start.10) | collective-permute-done | bytes 6176 | tf_op jit(solution)/shard_map/ppermute | solution.py:30
  18.5 0.7 %shard_map.94 = (bf16[2,256,256]{2,1,0:T(8,128)(2,1)S(1)}, bf16[256,256]{1,0:T(8,128)(2,1)S(1)}, bf16[256,256]{1,0:T(8,128)(2,1)S(1)}) custom-call(f32[3,2,256]{2,1,0:T(2,128)S(1)} %get-tuple-element.39.refs_0_, f32[3,2,256]{2,1,0:T(2,128)S(1)} %collective-permute-done.10.refs_1_, f32[2,2,256,256]{3,2,1,0:T(8,128)S(1)} %get-tuple-element.40.refs_2_, ...), custom_call_target="tpu_custom_call" | custom-call | flops 268435456 | bytes 1048576 | tf_op jit(solution)/shard_map/pallas_call | solution.py:373
  19.2 1.8 %collective-permute-start.12 = (bf16[256,256]{1,0:T(8,128)(2,1)S(1)}, bf16[256,256]{1,0:T(8,128)(2,1)S(1)}, u32[]{:S(2)}, u32[]{:S(2)}) collective-permute-start(bf16[256,256]{1,0:T(8,128)(2,1)S(1)} %get-tuple-element.48), channel_id=1, source_target_pairs={{0,16},{1,17},{2,18},{3,19},{4,20},{5,21},{6,22},{7,23},{8,9},{9,8... | collective-permute-start | bytes 393224 | tf_op jit(solution)/shard_map/ppermute | solution.py:396
  21.0 0.3 collective-permute-start.15
  21.3 0.4 %shard_map.96 = (bf16[256,256]{1,0:T(8,128)(2,1)S(1)}, bf16[256,256]{1,0:T(8,128)(2,1)S(1)}, f32[512,256]{1,0:T(8,128)S(1)}) custom-call(bf16[2048,256]{1,0:T(8,128)(2,1)S(1)} %get-tuple-element.31.refs_7_.own_ref, bf16[2048,256]{1,0:T(8,128)(2,1)S(1)} %get-tuple-element.32.refs_8_.far_ref, bf16[2,256,256]{2,1,0:T(8,128)(2,1)S(1)} %get-tuple-element.45.unrot_ref), custom_call_target="tpu_custom_call" | custom-call | flops 268435456 | bytes 1048576 | tf_op jit(solution)/shard_map/pallas_call | solution.py:381
  21.7 1.8 %collective-permute-start.11 = (bf16[256,256]{1,0:T(8,128)(2,1)S(1)}, bf16[256,256]{1,0:T(8,128)(2,1)S(1)}, u32[]{:S(2)}, u32[]{:S(2)}) collective-permute-start(bf16[256,256]{1,0:T(8,128)(2,1)S(1)} %get-tuple-element.46), channel_id=1, source_target_pairs={{0,16},{1,17},{2,18},{3,19},{4,20},{5,21},{6,22},{7,23},{8,9},{9,8... | collective-permute-start | bytes 393224 | tf_op jit(solution)/shard_map/ppermute | solution.py:396
  23.5 0.7 %collective-permute-done.12.come_ref = bf16[256,256]{1,0:T(8,128)(2,1)S(1)} collective-permute-done((bf16[256,256]{1,0:T(8,128)(2,1)S(1)}, bf16[256,256]{1,0:T(8,128)(2,1)S(1)}, u32[]{:S(2)}, u32[]{:S(2)}) %collective-permute-start.12) | collective-permute-done | bytes 131104 | tf_op jit(solution)/shard_map/ppermute | solution.py:396
  24.3 1.8 %collective-permute-start.13 = (bf16[256,256]{1,0:T(8,128)(2,1)S(1)}, bf16[256,256]{1,0:T(8,128)(2,1)S(1)}, u32[]{:S(2)}, u32[]{:S(2)}) collective-permute-start(bf16[256,256]{1,0:T(8,128)(2,1)S(1)} %shard_map.97), channel_id=1, source_target_pairs={{0,1},{1,0},{2,3},{3,2},{4,5},{5,4},{6,7},{7,6},{8,24},{9,25},{10,... | collective-permute-start | bytes 393224 | tf_op jit(solution)/shard_map/ppermute | solution.py:403
  26.1 1.5 %collective-permute-start.14 = (bf16[256,256]{1,0:T(8,128)(2,1)S(1)}, bf16[256,256]{1,0:T(8,128)(2,1)S(1)}, u32[]{:S(2)}, u32[]{:S(2)}) collective-permute-start(bf16[256,256]{1,0:T(8,128)(2,1)S(1)} %get-tuple-element.50), channel_id=1, source_target_pairs={{0,16},{1,17},{2,18},{3,19},{4,20},{5,21},{6,22},{7,23},{8,9},{9,8... | collective-permute-start | bytes 393224 | tf_op jit(solution)/shard_map/ppermute | solution.py:396
  27.6 0.0 collective-permute-done.15.come_ref
  27.6 1.1 %collective-permute-start.16 = (bf16[256,256]{1,0:T(8,128)(2,1)S(1)}, bf16[256,256]{1,0:T(8,128)(2,1)S(1)}, u32[]{:S(2)}, u32[]{:S(2)}) collective-permute-start(bf16[256,256]{1,0:T(8,128)(2,1)S(1)} %shard_map.99), channel_id=1, source_target_pairs={{0,1},{1,0},{2,3},{3,2},{4,5},{5,4},{6,7},{7,6},{8,24},{9,25},{10,... | collective-permute-start | bytes 393224 | tf_op jit(solution)/shard_map/ppermute | solution.py:403
  28.7 0.3 shard_map.95.keep_ref
  29.0 1.1 %collective-permute-done.11.stay_ref = bf16[256,256]{1,0:T(8,128)(2,1)S(1)} collective-permute-done((bf16[256,256]{1,0:T(8,128)(2,1)S(1)}, bf16[256,256]{1,0:T(8,128)(2,1)S(1)}, u32[]{:S(2)}, u32[]{:S(2)}) %collective-permute-start.11) | collective-permute-done | bytes 131104 | tf_op jit(solution)/shard_map/ppermute | solution.py:396
  30.1 0.0 collective-permute-done.13.come_ref
  30.2 3.4 %collective-permute-start.19 = (bf16[128,256]{1,0:T(8,128)(2,1)S(1)}, bf16[128,256]{1,0:T(8,128)(2,1)S(1)}, u32[]{:S(2)}, u32[]{:S(2)}) collective-permute-start(bf16[128,256]{1,0:T(8,128)(2,1)S(1)} %get-tuple-element.54), channel_id=1, source_target_pairs={{0,6},{1,7},{2,0},{3,1},{4,2},{5,3},{6,4},{7,5},{8,14},{9,15},{10,... | collective-permute-start | bytes 196616 | tf_op jit(solution)/shard_map/ppermute | solution.py:417
  33.6 0.0 collective-permute-done.14.stay_ref
  33.6 0.0 collective-permute-done.16.come_ref
  33.6 0.7 %collective-permute-start.17 = (bf16[128,256]{1,0:T(8,128)(2,1)S(1)}, bf16[128,256]{1,0:T(8,128)(2,1)S(1)}, u32[]{:S(2)}, u32[]{:S(2)}) collective-permute-start(bf16[128,256]{1,0:T(8,128)(2,1)S(1)} %get-tuple-element.52), channel_id=1, source_target_pairs={{0,2},{1,3},{2,4},{3,5},{4,6},{5,7},{6,0},{7,1},{8,10},{9,11},{10,... | collective-permute-start | bytes 196616 | tf_op jit(solution)/shard_map/ppermute | solution.py:417
  34.3 2.6 %collective-permute-start.18 = (bf16[128,256]{1,0:T(8,128)(2,1)S(1)}, bf16[128,256]{1,0:T(8,128)(2,1)S(1)}, u32[]{:S(2)}, u32[]{:S(2)}) collective-permute-start(bf16[128,256]{1,0:T(8,128)(2,1)S(1)} %get-tuple-element.53), channel_id=1, source_target_pairs={{0,4},{1,5},{2,6},{3,7},{4,0},{5,1},{6,2},{7,3},{8,12},{9,13},{10,... | collective-permute-start | bytes 196616 | tf_op jit(solution)/shard_map/ppermute | solution.py:417
  36.9 2.9 %collective-permute-done.17.refs_1_ = bf16[128,256]{1,0:T(8,128)(2,1)S(1)} collective-permute-done((bf16[128,256]{1,0:T(8,128)(2,1)S(1)}, bf16[128,256]{1,0:T(8,128)(2,1)S(1)}, u32[]{:S(2)}, u32[]{:S(2)}) %collective-permute-start.17) | collective-permute-done | bytes 65568 | tf_op jit(solution)/shard_map/ppermute | solution.py:417
  39.8 1.1 %collective-permute-done.18.refs_2_ = bf16[128,256]{1,0:T(8,128)(2,1)S(1)} collective-permute-done((bf16[128,256]{1,0:T(8,128)(2,1)S(1)}, bf16[128,256]{1,0:T(8,128)(2,1)S(1)}, u32[]{:S(2)}, u32[]{:S(2)}) %collective-permute-start.18) | collective-permute-done | bytes 65568 | tf_op jit(solution)/shard_map/ppermute | solution.py:417
  40.9 0.1 collective-permute-start.20
  41.0 1.2 %collective-permute-done.20.there_ref = f32[64,256]{1,0:T(8,128)S(1)} collective-permute-done((f32[64,256]{1,0:T(8,128)S(1)}, f32[64,256]{1,0:T(8,128)S(1)}, u32[]{:S(2)}, u32[]{:S(2)}) %collective-permute-start.20) | collective-permute-done | bytes 65568 | tf_op jit(solution)/shard_map/ppermute | solution.py:30
  42.3 0.7 %shard_map.102 = f32[64,512]{1,0:T(8,128)} custom-call(f32[64,256]{1,0:T(8,128)S(1)} %get-tuple-element.55.here_ref, f32[64,256]{1,0:T(8,128)S(1)} %collective-permute-done.20.there_ref, f32[64,512]{1,0:T(8,128)S(1)} %copy-done), custom_call_target="tpu_custom_call" | custom-call | flops 1048576 | bytes 1048576 | tf_op jit(solution)/shard_map/pallas_call | solution.py:421
  (10 shorter events, 0.2 us)
Async XLA Ops:
  0.0 10.9 %collective-permute-start = (bf16[256,2048]{1,0:T(8,128)(2,1)}, bf16[256,2048]{1,0:T(8,128)(2,1)S(1)}, u32[]{:S(2)}, u32[]{:S(2)}) collective-permute-start(bf16[256,2048]{1,0:T(8,128)(2,1)} %bitcast.5), channel_id=1, source_target_pairs={{0,8},{8,0},{16,24},{24,16},{1,9},{9,1},{17,25},{25,17},{2,10},{10... | collective-permute-start | bytes 3145736 | tf_op jit(solution)/shard_map/ppermute | solution.py:30
  0.5 13.2 %collective-permute-start.8 = (bf16[256,512]{1,0:T(8,128)(2,1)}, bf16[256,512]{1,0:T(8,128)(2,1)S(1)}, u32[]{:S(2)}, u32[]{:S(2)}) collective-permute-start(bf16[256,512]{1,0:T(8,128)(2,1)} %bitcast.7), channel_id=1, source_target_pairs={{0,8},{8,0},{16,24},{24,16},{1,9},{9,1},{17,25},{25,17},{2,10},{10... | collective-permute-start | bytes 786440 | tf_op jit(solution)/shard_map/ppermute | solution.py:30
  0.5 3.0 %copy-start.1 = (s32[1,16]{1,0:T(1,128)S(1)}, s32[1,16]{1,0:T(1,128)}, u32[]{:S(2)}) copy-start(s32[1,16]{1,0:T(1,128)} %refs_4_.1) | copy-start | bytes 196
  0.5 13.2 %collective-permute-start.9 = (bf16[256,512]{1,0:T(8,128)(2,1)}, bf16[256,512]{1,0:T(8,128)(2,1)S(1)}, u32[]{:S(2)}, u32[]{:S(2)}) collective-permute-start(bf16[256,512]{1,0:T(8,128)(2,1)} %bitcast.9), channel_id=1, source_target_pairs={{0,8},{8,0},{16,24},{24,16},{1,9},{9,1},{17,25},{25,17},{2,10},{10... | collective-permute-start | bytes 786440 | tf_op jit(solution)/shard_map/ppermute | solution.py:30
  1.0 5.4 %collective-permute-start.3 = (bf16[16,2048]{1,0:T(8,128)(2,1)}, bf16[16,2048]{1,0:T(8,128)(2,1)S(1)}, u32[]{:S(2)}, u32[]{:S(2)}) collective-permute-start(bf16[16,2048]{1,0:T(8,128)(2,1)} %bitcast.11), channel_id=1, source_target_pairs={{0,16},{8,24},{16,0},{24,8},{1,17},{9,25},{17,1},{25,9},{2,18},{10... | collective-permute-start | bytes 196616 | tf_op jit(solution)/shard_map/ppermute | solution.py:30
  3.5 1.2 %collective-permute-start.1 = (s32[1,16]{1,0:T(1,128)S(1)}, s32[1,16]{1,0:T(1,128)S(1)}, u32[]{:S(2)}, u32[]{:S(2)}) collective-permute-start(s32[1,16]{1,0:T(1,128)S(1)} %copy-done.1), channel_id=1, source_target_pairs={{0,8},{8,0},{16,24},{24,16},{1,9},{9,1},{17,25},{25,17},{2,10},{10... | collective-permute-start | bytes 200 | tf_op jit(solution)/shard_map/ppermute | solution.py:30
  4.7 3.6 %collective-permute-start.2 = (bf16[16,2048]{1,0:T(8,128)(2,1)}, bf16[16,2048]{1,0:T(8,128)(2,1)S(1)}, u32[]{:S(2)}, u32[]{:S(2)}) collective-permute-start(bf16[16,2048]{1,0:T(8,128)(2,1)} %bitcast.12), channel_id=1, source_target_pairs={{0,8},{8,0},{16,24},{24,16},{1,9},{9,1},{17,25},{25,17},{2,10},{10... | collective-permute-start | bytes 196616 | tf_op jit(solution)/shard_map/ppermute | solution.py:30
  6.5 4.5 %collective-permute-start.6 = (bf16[16,2048]{1,0:T(8,128)(2,1)}, bf16[16,2048]{1,0:T(8,128)(2,1)S(1)}, u32[]{:S(2)}, u32[]{:S(2)}) collective-permute-start(bf16[16,2048]{1,0:T(8,128)(2,1)} %bitcast.14), channel_id=1, source_target_pairs={{0,16},{8,24},{16,0},{24,8},{1,17},{9,25},{17,1},{25,9},{2,18},{10... | collective-permute-start | bytes 196616 | tf_op jit(solution)/shard_map/ppermute | solution.py:30
  8.2 5.5 %collective-permute-start.5 = (bf16[16,2048]{1,0:T(8,128)(2,1)}, bf16[16,2048]{1,0:T(8,128)(2,1)S(1)}, u32[]{:S(2)}, u32[]{:S(2)}) collective-permute-start(bf16[16,2048]{1,0:T(8,128)(2,1)} %bitcast.15), channel_id=1, source_target_pairs={{0,8},{8,0},{16,24},{24,16},{1,9},{9,1},{17,25},{25,17},{2,10},{10... | collective-permute-start | bytes 196616 | tf_op jit(solution)/shard_map/ppermute | solution.py:30
  10.9 2.8 %collective-permute-start.4 = (bf16[16,2048]{1,0:T(8,128)(2,1)S(1)}, bf16[16,2048]{1,0:T(8,128)(2,1)S(1)}, u32[]{:S(2)}, u32[]{:S(2)}) collective-permute-start(bf16[16,2048]{1,0:T(8,128)(2,1)S(1)} %collective-permute-done.3.refs_2_), channel_id=1, source_target_pairs={{0,8},{8,0},{16,24},{24,16},{1,9},{9,1},{17,25},{25,17},{2,10},{10... | collective-permute-start | bytes 196616 | tf_op jit(solution)/shard_map/ppermute | solution.py:30
  10.9 2.8 %collective-permute-start.7 = (bf16[16,2048]{1,0:T(8,128)(2,1)S(1)}, bf16[16,2048]{1,0:T(8,128)(2,1)S(1)}, u32[]{:S(2)}, u32[]{:S(2)}) collective-permute-start(bf16[16,2048]{1,0:T(8,128)(2,1)S(1)} %collective-permute-done.6.refs_6_), channel_id=1, source_target_pairs={{0,8},{8,0},{16,24},{24,16},{1,9},{9,1},{17,25},{25,17},{2,10},{10... | collective-permute-start | bytes 196616 | tf_op jit(solution)/shard_map/ppermute | solution.py:30
  14.8 3.6 %collective-permute-start.10 = (f32[3,2,256]{2,1,0:T(2,128)S(1)}, f32[3,2,256]{2,1,0:T(2,128)S(1)}, u32[]{:S(2)}, u32[]{:S(2)}) collective-permute-start(f32[3,2,256]{2,1,0:T(2,128)S(1)} %get-tuple-element.39.refs_0_), channel_id=1, source_target_pairs={{0,16},{8,24},{16,0},{24,8},{1,17},{9,25},{17,1},{25,9},{2,18},{10... | collective-permute-start | bytes 18440 | tf_op jit(solution)/shard_map/ppermute | solution.py:30
  19.2 5.0 %collective-permute-start.12 = (bf16[256,256]{1,0:T(8,128)(2,1)S(1)}, bf16[256,256]{1,0:T(8,128)(2,1)S(1)}, u32[]{:S(2)}, u32[]{:S(2)}) collective-permute-start(bf16[256,256]{1,0:T(8,128)(2,1)S(1)} %get-tuple-element.48), channel_id=1, source_target_pairs={{0,16},{1,17},{2,18},{3,19},{4,20},{5,21},{6,22},{7,23},{8,9},{9,8... | collective-permute-start | bytes 393224 | tf_op jit(solution)/shard_map/ppermute | solution.py:396
  21.0 6.6 %collective-permute-start.15 = (bf16[256,256]{1,0:T(8,128)(2,1)S(1)}, bf16[256,256]{1,0:T(8,128)(2,1)S(1)}, u32[]{:S(2)}, u32[]{:S(2)}) collective-permute-start(bf16[256,256]{1,0:T(8,128)(2,1)S(1)} %get-tuple-element.51), channel_id=1, source_target_pairs={{0,16},{1,17},{2,18},{3,19},{4,20},{5,21},{6,22},{7,23},{8,9},{9,8... | collective-permute-start | bytes 393224 | tf_op jit(solution)/shard_map/ppermute | solution.py:396
  21.7 8.4 %collective-permute-start.11 = (bf16[256,256]{1,0:T(8,128)(2,1)S(1)}, bf16[256,256]{1,0:T(8,128)(2,1)S(1)}, u32[]{:S(2)}, u32[]{:S(2)}) collective-permute-start(bf16[256,256]{1,0:T(8,128)(2,1)S(1)} %get-tuple-element.46), channel_id=1, source_target_pairs={{0,16},{1,17},{2,18},{3,19},{4,20},{5,21},{6,22},{7,23},{8,9},{9,8... | collective-permute-start | bytes 393224 | tf_op jit(solution)/shard_map/ppermute | solution.py:396
  24.3 5.9 %collective-permute-start.13 = (bf16[256,256]{1,0:T(8,128)(2,1)S(1)}, bf16[256,256]{1,0:T(8,128)(2,1)S(1)}, u32[]{:S(2)}, u32[]{:S(2)}) collective-permute-start(bf16[256,256]{1,0:T(8,128)(2,1)S(1)} %shard_map.97), channel_id=1, source_target_pairs={{0,1},{1,0},{2,3},{3,2},{4,5},{5,4},{6,7},{7,6},{8,24},{9,25},{10,... | collective-permute-start | bytes 393224 | tf_op jit(solution)/shard_map/ppermute | solution.py:403
  26.1 7.5 %collective-permute-start.14 = (bf16[256,256]{1,0:T(8,128)(2,1)S(1)}, bf16[256,256]{1,0:T(8,128)(2,1)S(1)}, u32[]{:S(2)}, u32[]{:S(2)}) collective-permute-start(bf16[256,256]{1,0:T(8,128)(2,1)S(1)} %get-tuple-element.50), channel_id=1, source_target_pairs={{0,16},{1,17},{2,18},{3,19},{4,20},{5,21},{6,22},{7,23},{8,9},{9,8... | collective-permute-start | bytes 393224 | tf_op jit(solution)/shard_map/ppermute | solution.py:396
  27.6 6.0 %collective-permute-start.16 = (bf16[256,256]{1,0:T(8,128)(2,1)S(1)}, bf16[256,256]{1,0:T(8,128)(2,1)S(1)}, u32[]{:S(2)}, u32[]{:S(2)}) collective-permute-start(bf16[256,256]{1,0:T(8,128)(2,1)S(1)} %shard_map.99), channel_id=1, source_target_pairs={{0,1},{1,0},{2,3},{3,2},{4,5},{5,4},{6,7},{7,6},{8,24},{9,25},{10,... | collective-permute-start | bytes 393224 | tf_op jit(solution)/shard_map/ppermute | solution.py:403
  30.2 6.8 %collective-permute-start.19 = (bf16[128,256]{1,0:T(8,128)(2,1)S(1)}, bf16[128,256]{1,0:T(8,128)(2,1)S(1)}, u32[]{:S(2)}, u32[]{:S(2)}) collective-permute-start(bf16[128,256]{1,0:T(8,128)(2,1)S(1)} %get-tuple-element.54), channel_id=1, source_target_pairs={{0,6},{1,7},{2,0},{3,1},{4,2},{5,3},{6,4},{7,5},{8,14},{9,15},{10,... | collective-permute-start | bytes 196616 | tf_op jit(solution)/shard_map/ppermute | solution.py:417
  33.6 6.2 %collective-permute-start.17 = (bf16[128,256]{1,0:T(8,128)(2,1)S(1)}, bf16[128,256]{1,0:T(8,128)(2,1)S(1)}, u32[]{:S(2)}, u32[]{:S(2)}) collective-permute-start(bf16[128,256]{1,0:T(8,128)(2,1)S(1)} %get-tuple-element.52), channel_id=1, source_target_pairs={{0,2},{1,3},{2,4},{3,5},{4,6},{5,7},{6,0},{7,1},{8,10},{9,11},{10,... | collective-permute-start | bytes 196616 | tf_op jit(solution)/shard_map/ppermute | solution.py:417
  34.3 6.6 %collective-permute-start.18 = (bf16[128,256]{1,0:T(8,128)(2,1)S(1)}, bf16[128,256]{1,0:T(8,128)(2,1)S(1)}, u32[]{:S(2)}, u32[]{:S(2)}) collective-permute-start(bf16[128,256]{1,0:T(8,128)(2,1)S(1)} %get-tuple-element.53), channel_id=1, source_target_pairs={{0,4},{1,5},{2,6},{3,7},{4,0},{5,1},{6,2},{7,3},{8,12},{9,13},{10,... | collective-permute-start | bytes 196616 | tf_op jit(solution)/shard_map/ppermute | solution.py:417
  40.9 1.4 %copy-start = (f32[64,512]{1,0:T(8,128)S(1)}, f32[64,512]{1,0:T(8,128)}, u32[]{:S(2)}) copy-start(f32[64,512]{1,0:T(8,128)} %hessian_ref.1) | copy-start | bytes 393220
  40.9 1.3 %collective-permute-start.20 = (f32[64,256]{1,0:T(8,128)S(1)}, f32[64,256]{1,0:T(8,128)S(1)}, u32[]{:S(2)}, u32[]{:S(2)}) collective-permute-start(f32[64,256]{1,0:T(8,128)S(1)} %get-tuple-element.56), channel_id=1, source_target_pairs={{0,8},{8,0},{16,24},{24,16},{1,9},{9,1},{17,25},{25,17},{2,10},{10... | collective-permute-start | bytes 196616 | tf_op jit(solution)/shard_map/ppermute | solution.py:30

commit v4 on v3

--- a/solution.py
+++ b/solution.py
@@ -86,7 +86,7 @@
     return parts[0] if count == 1 else jnp.concatenate(parts, axis=0)
 
 
-def reach_of(picked, here, width, blocks, tokens):
+def reach_of(picked, here, width, first_block, blocks, tokens):
     rows = picked.shape[1]
     square = (rows, rows)
     diagonal = lax.broadcasted_iota(jnp.int32, square, 0) == lax.broadcasted_iota(
@@ -97,102 +97,127 @@
     chosen = lax.broadcasted_iota(jnp.int32, (rows, width), 0) == (lane & (rows - 1))
     own = jnp.sum(jnp.where(chosen, column, 0), axis=0, keepdims=True)
     lane = lax.broadcasted_iota(jnp.int32, (1, width), 1)
-    block = (lane >> (rows.bit_length() - 1)) & (blocks - 1)
+    block = first_block + ((lane >> (rows.bit_length() - 1)) & (blocks - 1))
     return jnp.where(block == here, own, jnp.where(block > here, tokens, -1))
 
 
-def stats_kernel(torus, blocks, parts, *refs):
-    query_refs, cot_refs = refs[:blocks], refs[blocks : 2 * blocks]
-    key_refs, value_refs = (
-        refs[(2 * blocks + i * parts) : (2 * blocks + (i + 1) * parts)] for i in range(2)
-    )
-    reach_refs = refs[2 * blocks + 2 * parts : 2 * blocks + 3 * parts]
-    stats_ref, expo_ref, grads_ref, query_held, cot_held = refs[2 * blocks + 3 * parts :]
-    rows, width = query_refs[0].shape[0], query_held.shape[1]
-    start = position()[0] * width if torus else 0
-    columns = pl.ds(pl.multiple_of(start, HEAD_DIM), width)
-    for number in range(blocks):
-        block = lax.axis_index("blk") ^ number if torus else number
-        at = pl.ds(pl.multiple_of(block * rows, rows), rows)
-        query_held[at, :] = query_refs[number][:, columns]
-        cot_held[at, :] = cot_refs[number][:, columns]
+def fill_stats(columns, reaches, key_refs, value_refs, held, outs):
+    query_held, cot_held = held
+    stats, expo_ref, grads_ref = outs
     per, count = chunks(query_held.shape[0])
     width = per * query_held.shape[0]
-    start = position()[0] * (HEAD_DIM * stats_ref.shape[1]) if torus else 0
-    for group in range(stats_ref.shape[1]):
-        columns = pl.ds(pl.multiple_of(start + group * HEAD_DIM, HEAD_DIM), HEAD_DIM)
+    for group in range(expo_ref.shape[0]):
+        at = pl.ds(pl.multiple_of(columns + group * HEAD_DIM, HEAD_DIM), HEAD_DIM)
         for chunk in range(count):
             first = group * REPEAT + chunk * per
             query = heads_of(query_held, first, per)
             cot = heads_of(cot_held, first, per)
             scores, tops = [], []
-            for part in range(parts):
+            for reach, key_ref in zip(reaches, key_refs):
                 score = lax.dot_general(
-                    key_refs[part][:, columns], query, NT_DIMS, preferred_element_type=jnp.float32
+                    key_ref[:, at], query, NT_DIMS, preferred_element_type=jnp.float32
                 ) * (HEAD_DIM**-0.5)
                 key_ids = lax.broadcasted_iota(jnp.int32, score.shape, 0)
-                score = jnp.where(key_ids <= reach_refs[part][...], score, neg_large)
+                score = jnp.where(key_ids <= reach, score, neg_large)
                 scores.append(score)
                 tops.append(jnp.max(score, axis=0, keepdims=True))
             top = functools.reduce(jnp.maximum, tops)
             place = pl.ds(chunk * width, width)
             total, dot = 0.0, 0.0
-            for part in range(parts):
+            for part, (score, value_ref) in enumerate(zip(scores, value_refs)):
                 grads = lax.dot_general(
-                    value_refs[part][:, columns], cot, NT_DIMS, preferred_element_type=jnp.float32
+                    value_ref[:, at], cot, NT_DIMS, preferred_element_type=jnp.float32
                 )
-                expo = jnp.exp(scores[part] - top)
+                expo = jnp.exp(score - top)
                 weights = expo.astype(jnp.bfloat16).astype(jnp.float32)
                 total += jnp.sum(expo, axis=0, keepdims=True)
                 dot += jnp.sum(weights * grads, axis=0, keepdims=True)
                 expo_ref[group, part, :, place] = expo
                 grads_ref[group, part, :, place] = grads
-            stats_ref[0, group : group + 1, place] = top
-            stats_ref[1, group : group + 1, place] = total
-            stats_ref[2, group : group + 1, place] = dot
-
-
-def attention_stats(queries, cots, keys, values, reach, heads, torus):
-    blocks, parts = len(queries), len(keys)
-    rows = queries[0].shape[0]
-    width = heads * REPEAT * HEAD_DIM
-    tokens = keys[0].shape[0]
-    total = blocks * rows
+            for number, value in enumerate((top, total, dot)):
+                stats(number)[group : group + 1, place] = value
+
+
+def hold_rows(places, query_refs, cot_refs, columns, held):
+    for place, query_ref, cot_ref in zip(places, query_refs, cot_refs):
+        rows = query_ref.shape[0]
+        at = pl.ds(pl.multiple_of(place * rows, rows), rows)
+        held[0][at, :] = query_ref[:, columns]
+        held[1][at, :] = cot_ref[:, columns]
+
+
+def any_stats_kernel(blocks, *refs):
+    query_refs, cot_refs = refs[:blocks], refs[blocks : 2 * blocks]
+    key_ref, value_ref, reach_ref, stats_ref, expo_ref, grads_ref, *held = refs[2 * blocks :]
+    hold_rows(range(blocks), query_refs, cot_refs, slice(None), held)
+    outs = (lambda number: stats_ref.at[number]), expo_ref, grads_ref
+    fill_stats(0, [reach_ref[...]], [key_ref], [value_ref], held, outs)
+
+
+def chip_stats_kernel(side, *refs):
+    query_refs, cot_refs, key_refs, value_refs = (refs[2 * i : 2 * i + 2] for i in range(4))
+    rest, (stats_ref, expo_ref, grads_ref, *held) = refs[8:-5], refs[-5:]
+    blk = lax.axis_index("blk")
+    core, chip = blk & 1, blk >> 1
+    tokens, width = key_refs[0].shape[0], held[0].shape[1]
+    if side == 0:
+        lanes = expo_ref.shape[3]
+        reaches = [
+            reach_of(ref[...], blk ^ part, lanes, chip * 2, 2, tokens)
+            for part, ref in enumerate(rest)
+        ]
+        outs = lambda number: stats_ref.at[number]
+    else:
+        reaches = [jnp.where(chip == 0, tokens, -1)] * 2
+        stats_ref[:, 0] = rest[0][...]
+        outs = lambda number: stats_ref.at[number, 1]
+    start = core * width
+    columns = pl.ds(pl.multiple_of(start, HEAD_DIM), width)
+    hold_rows((core, 1 - core), query_refs, cot_refs, columns, held)
+    heads = core * (HEAD_DIM * expo_ref.shape[0])
+    fill_stats(heads, reaches, key_refs, value_refs, held, (outs, expo_ref, grads_ref))
+
+
+def attention_stats(kernel, queries, cots, keys, values, more, heads, sides=()):
+    parts, (rows, tokens) = len(keys), (queries[0].shape[0], keys[0].shape[0])
+    total, width = len(queries) * rows, heads * REPEAT * HEAD_DIM
     saved = shape((heads, parts, tokens, REPEAT * total), jnp.float32)
     held = shape((total, width), jnp.bfloat16)
-    outs = [shape((3, heads, REPEAT * total), jnp.float32), saved, saved, held, held]
-    return call(
-        functools.partial(stats_kernel, torus, blocks, parts),
-        outs,
-        [VMEM] * (2 * blocks + 3 * parts),
-        4 * heads * REPEAT * total * tokens * parts * HEAD_DIM,
-    )(*queries, *cots, *keys, *values, *reach)[:4]
-
-
-def row_scales(group, mine_ref, every_refs):
-    at = slice(group, group + 1)
-    top = functools.reduce(jnp.maximum, [ref[0, at, :] for ref in every_refs])
-    shrink = [jnp.exp(ref[0, at, :] - top) for ref in every_refs]
-    total = sum(ref[1, at, :] * factor for ref, factor in zip(every_refs, shrink))
-    dot = sum(ref[2, at, :] * factor for ref, factor in zip(every_refs, shrink))
-    return jnp.exp(mine_ref[0, at, :] - top) / total, dot / total
-
-
-def key_gradient(group, stats_refs, expo_ref, grads_ref, query_ref, cosine_ref, sine_ref):
-    scale, dot = row_scales(group, stats_refs[0], stats_refs)
-    parts, tokens = expo_ref.shape[1:3]
-    per, count = chunks(query_ref.shape[0])
-    width = per * query_ref.shape[0]
+    outs = [shape((3, *sides, heads, REPEAT * total), jnp.float32), saved, saved, held, held]
+    operands = (*queries, *cots, *keys, *values, *more)
+    flops = 4 * heads * REPEAT * total * tokens * parts * HEAD_DIM
+    return call(kernel, outs, [VMEM] * len(operands), flops)(*operands)[:4]
+
+
+def row_scales(every):
+    tops, totals, dots = zip(*every)
+    top = functools.reduce(jnp.maximum, tops)
+    shrink = [jnp.exp(value - top) for value in tops]
+    total = sum(value * factor for value, factor in zip(totals, shrink))
+    dot = sum(value * factor for value, factor in zip(dots, shrink))
+    return shrink[0] / total, dot / total
+
+
+def key_gradient(group, sets, cosine_ref, sine_ref):
+    scales = [row_scales(rows[0]) for rows in sets]
+    parts, tokens = sets[0][1].shape[1:3]
+    per, count = chunks(sets[0][3].shape[0])
+    width = per * sets[0][3].shape[0]
     blocks = []
     for part in range(parts):
         gradient = 0.0
         for chunk in range(count):
             place = slice(chunk * width, (chunk + 1) * width)
-            query = heads_of(query_ref, group * REPEAT + chunk * per, per)
-            prob = expo_ref[group, part, :, place] * scale[:, place]
-            pulled = prob * (grads_ref[group, part, :, place] - dot[:, place])
+            pulled, queries = [], []
+            for (scale, dot), (_, expo_ref, grads_ref, query_ref) in zip(scales, sets):
+                queries.append(heads_of(query_ref, group * REPEAT + chunk * per, per))
+                prob = expo_ref[group, part, :, place] * scale[:, place]
+                grads = prob * (grads_ref[group, part, :, place] - dot[:, place])
+                pulled.append(grads.astype(jnp.bfloat16))
             gradient += jnp.dot(
-                pulled.astype(jnp.bfloat16), query, preferred_element_type=jnp.float32
+                pulled[0] if len(sets) == 1 else jnp.concatenate(pulled, axis=1),
+                queries[0] if len(sets) == 1 else jnp.concatenate(queries, axis=0),
+                preferred_element_type=jnp.float32,
             )
         gradient = gradient * (HEAD_DIM**-0.5)
         turned = pltpu.roll(gradient, HEAD_DIM // 2, 1)
@@ -204,9 +229,12 @@
 
 
 def grad_kernel(count, *refs):
-    stats_refs, out_ref = refs[:count], refs[-1]
-    for group in range(stats_refs[0].shape[1]):
-        blocks = key_gradient(group, stats_refs, *refs[count:-1])
+    expo_ref, grads_ref, query_ref, cosine_ref, sine_ref, out_ref = refs[count:]
+    for group in range(expo_ref.shape[0]):
+        at = slice(group, group + 1)
+        every = [[ref[number, at, :] for number in range(3)] for ref in refs[:count]]
+        sets = [(every, expo_ref, grads_ref, query_ref)]
+        blocks = key_gradient(group, sets, cosine_ref, sine_ref)
         out_ref[:, group * HEAD_DIM : (group + 1) * HEAD_DIM] = blocks[0]
 
 
@@ -227,14 +255,19 @@
         out_ref[number * size : (number + 1) * size, :] = total.astype(out_ref.dtype)
 
 
-def send_kernel(chunks_out, *refs):
-    stats_refs, saved_refs = refs[:2], refs[2:7]
-    own_ref, far_ref, unrot_ref = refs[7:10]
-    for group in range(stats_refs[0].shape[1]):
+def send_kernel(chunks_out, mine_ref, other_ref, *refs):
+    saved_refs, tables, (own_ref, far_ref, unrot_ref) = refs[:6], refs[6:8], refs[8:11]
+    for group in range(saved_refs[0].shape[0]):
+        at = slice(group, group + 1)
+        sets = []
+        for side in range(2):
+            mine = [mine_ref[number, side, at, :] for number in range(3)]
+            other = [other_ref[number, 1 - side, at, :] for number in range(3)]
+            sets.append(((mine, other), *saved_refs[3 * side : 3 * side + 3]))
         columns = pl.ds(group * HEAD_DIM, HEAD_DIM)
-        for part, block in enumerate(key_gradient(group, stats_refs, *saved_refs)):
+        for part, block in enumerate(key_gradient(group, sets, *tables)):
             unrot_ref[part, :, columns] = block
-    for chunk, out_ref in zip(chunks_out, refs[10:]):
+    for chunk, out_ref in zip(chunks_out, refs[11:]):
         put_product(own_ref, far_ref, unrot_ref, *chunk, out_ref)
 
 
@@ -290,8 +323,8 @@
                     ]
 
 
-def own_kernel(blocks, *refs):
-    sources, (turned_ref, cosine_ref, sine_ref, reach_ref), rest = refs[:8], refs[8:12], refs[12:]
+def own_kernel(*refs):
+    sources, (turned_ref, cosine_ref, sine_ref), rest = refs[:8], refs[8:11], refs[11:]
     held, sems = rest[:-1], rest[-1]
     copies = [
         pltpu.make_async_copy(source, target, sems.at[number])
@@ -301,17 +334,10 @@
         copy.start()
     for copy in copies:
         copy.wait()
-    keys_ref, (picked_ref, features_ref, coarse_ref, fine_ref) = held[0], held[4:]
-    tokens, blk = keys_ref.shape[0], lax.axis_index("blk")
-    reach_ref[...] = reach_of(picked_ref[...], blk, reach_ref.shape[1], blocks, tokens)
+    features_ref, coarse_ref, fine_ref = held[5:]
+    tokens, blk = held[0].shape[0], lax.axis_index("blk")
     starts = blk * tokens, (blk ^ 1) * tokens
     fill_rotation(starts, tokens, coarse_ref, fine_ref, cosine_ref, sine_ref)
-    turn_kernel(features_ref, turned_ref)
-
-
-def far_kernel(blocks, tokens, features_ref, picked_ref, turned_ref, reach_ref):
-    here = lax.axis_index("blk") ^ 1
-    reach_ref[...] = reach_of(picked_ref[...], here, reach_ref.shape[1], blocks, tokens)
     turn_kernel(features_ref, turned_ref)
 
 
@@ -329,33 +355,39 @@
     coarse, fine = rotation_rows(np.arange(0, 4 * tokens, 16)), rotation_rows(np.arange(16))
     turned = shape((normed.shape[1], tokens), jnp.bfloat16)
     table = shape((2 * tokens, HEAD_DIM), jnp.float32)
-    last = shape((1, REPEAT * 4 * queries.shape[0]), jnp.int32)
     given = [
         pltpu.with_memory_space_constraint(array, pltpu.HBM)
         for array in (key_states, values, queries, cotangent, picked, normed, coarse, fine)
     ]
-    own, cosine, sine, reach, *fetched = call(
-        functools.partial(own_kernel, 4),
-        [turned, table, table, last] + [shape(array.shape, array.dtype) for array in given[:4]],
+    own, cosine, sine, key_states, values, queries, cotangent, picked = call(
+        own_kernel,
+        [turned, table, table] + [shape(array.shape, array.dtype) for array in given[:5]],
         [HBM] * 8,
         1 << 28,
-        [pltpu.VMEM(array.shape, array.dtype) for array in given[4:]]
+        [pltpu.VMEM(array.shape, array.dtype) for array in given[5:]]
         + [pltpu.SemaphoreType.DMA((8,))],
     )(*given)
-    key_states, values, *held = fetched
-    held = [held, second, first, third]
-    far, far_reach = call(
-        functools.partial(far_kernel, 4, tokens), [turned, last], [VMEM] * 2, 1 << 28
-    )(far_normed, far_picked)
-
-    stats, expo, grads, query = attention_stats(
-        [pair[0] for pair in held],
-        [pair[1] for pair in held],
-        [key_states, far_keys],
-        [values, far_values],
-        (reach, far_reach),
+    far = call(turn_kernel, turned, [VMEM], 1 << 28)(far_normed)
+
+    keys, values = [key_states, far_keys], [values, far_values]
+    stats, *near = attention_stats(
+        functools.partial(chip_stats_kernel, 0),
+        (queries, second[0]),
+        (cotangent, second[1]),
+        keys,
+        values,
+        (picked, far_picked),
         heads,
-        True,
+    )
+    stats, *across = attention_stats(
+        functools.partial(chip_stats_kernel, 1),
+        (first[0], third[0]),
+        (first[1], third[1]),
+        keys,
+        values,
+        (stats,),
+        heads,
+        (2,),
     )
     other = swapped(stats, "blk", 2)
 
@@ -373,9 +405,9 @@
     unrot, *sends = call(
         functools.partial(send_kernel, early),
         [shape((2, tokens, wide), jnp.bfloat16)] + [block(chunk[2]) for chunk in early],
-        [VMEM] * 9,
+        [VMEM] * 12,
         work,
-    )(stats, other, expo, grads, query, cosine, sine, own, far)
+    )(stats, other, *near, *across, cosine, sine, own, far)
     everywhere = sum(TRAVEL, ())
     late.append((0, 1, everywhere))
     *more, turn_keep = call(
@@ -441,13 +473,13 @@
         rotation_rows(np.arange(size * tokens)).reshape(2, size, tokens, HEAD_DIM), blk, 1, False
     )
     stats, expo, grads, query = attention_stats(
+        functools.partial(any_stats_kernel, size),
         [every_query[i] for i in range(size)],
         [every_cot[i] for i in range(size)],
         [key_states],
         [values],
         (reach,),
         KV_HEADS,
-        False,
     )
     gathered = lax.all_gather(stats, "blk", axis=0)
     others = [gathered[(blk + i) % size] for i in range(1, size)]

time: 43.1 us -> 40.3 us (0.935)
  waiting for transfers between devices: 14.2 us -> 12.3 us
  starting transfers between devices: 23 us -> 21.4 us
  Pallas kernels: 5.61 us -> 6.16 us
    ppermute x3, waiting for transfers between devices: 3.99 us -> 2.01 us  [reduced_on_torus(): arrived.append(lax.ppermute(send, 'fsdp', along))]
    ppermute x2, starting transfers between devices: 2.92 us -> 2.17 us  [reduced_on_torus(): arrived = lax.ppermute(send, BOTH, route_after)]
    ppermute x12, starting transfers between devices: 8.01 us -> 7.4 us  [swapped(): return lax.ppermute(block, axis, route)]
    pallas_call x3 -> x4, Pallas kernels: 3.31 us -> 3.87 us  [the longest x1 1.85 us: reduced_on_torus(): call(own_kernel, [turned, table, table] + [shape(array.shape, array.dtype...]
  transfers between devices with their start and end apart: 21 -> 21, of which waited for: 9 -> 10; matrix products, arithmetic and copies ran while one was open for 0% -> 0% of each run, Pallas kernels for 7% -> 12%
where the time goes in v4:
time: 40.3 us; the launch traced here: 40.1 us
  starting transfers between devices  21.4 us (53%)
  waiting for transfers between devices  12.3 us (31%)
  Pallas kernels  6.16 us (15%)
    ppermute x12, waiting for transfers between devices, swapped(): return lax.ppermute(block, axis, route)  8.29 us
    ppermute x12, starting transfers between devices, swapped(): return lax.ppermute(block, axis, route)  7.4 us
    ppermute x3, starting transfers between devices, reduced_on_torus(): arrived.append(lax.ppermute(send, 'fsdp', along))  6.73 us
    ppermute x4, starting transfers between devices, reduced_on_torus(): come.append(lax.ppermute(send, BOTH, route))  5.14 us
    ppermute x2, starting transfers between devices, reduced_on_torus(): arrived = lax.ppermute(send, BOTH, route_after)  2.17 us
    ppermute x3, waiting for transfers between devices, reduced_on_torus(): arrived.append(lax.ppermute(send, 'fsdp', along))  2.01 us
    pallas_call x1, Pallas kernels, reduced_on_torus(): call(own_kernel, [turned, table, table] + [shape(array.shape, array.dtype...  1.85 us
    ppermute x4, waiting for transfers between devices, reduced_on_torus(): come.append(lax.ppermute(send, BOTH, route))  1.83 us
  transfers between devices with their start and end apart: 21, of which 10 were waited for; matrix products, arithmetic and copies ran while one was open for 0% of the time, Pallas kernels for 12%

profile of v4, /device:TPU:0, one launch (start us, length us, event | category | flops | bytes accessed | tf_op | source)
XLA Modules:
  0.0 40.1 jit_solution(1272286105386330738)
XLA Ops:
  0.0 0.5 %collective-permute-start = (bf16[256,2048]{1,0:T(8,128)(2,1)}, bf16[256,2048]{1,0:T(8,128)(2,1)S(1)}, u32[]{:S(2)}, u32[]{:S(2)}) collective-permute-start(bf16[256,2048]{1,0:T(8,128)(2,1)} %bitcast.5), channel_id=1, source_target_pairs={{0,8},{8,0},{16,24},{24,16},{1,9},{9,1},{17,25},{25,17},{2,10},{10... | collective-permute-start | bytes 3145736 | tf_op jit(solution)/shard_map/ppermute | solution.py:30
  0.5 0.1 collective-permute-start.5
  0.6 0.4 %collective-permute-start.6 = (bf16[256,512]{1,0:T(8,128)(2,1)}, bf16[256,512]{1,0:T(8,128)(2,1)S(1)}, u32[]{:S(2)}, u32[]{:S(2)}) collective-permute-start(bf16[256,512]{1,0:T(8,128)(2,1)} %bitcast.9), channel_id=1, source_target_pairs={{0,8},{8,0},{16,24},{24,16},{1,9},{9,1},{17,25},{25,17},{2,10},{10... | collective-permute-start | bytes 786440 | tf_op jit(solution)/shard_map/ppermute | solution.py:30
  1.0 0.1 copy-done.1
  1.1 0.0 collective-permute-start.9
  1.2 0.5 %collective-permute-start.7 = (bf16[16,2048]{1,0:T(8,128)(2,1)}, bf16[16,2048]{1,0:T(8,128)(2,1)S(1)}, u32[]{:S(2)}, u32[]{:S(2)}) collective-permute-start(bf16[16,2048]{1,0:T(8,128)(2,1)} %bitcast.11), channel_id=1, source_target_pairs={{0,8},{8,0},{16,24},{24,16},{1,9},{9,1},{17,25},{25,17},{2,10},{10... | collective-permute-start | bytes 196616 | tf_op jit(solution)/shard_map/ppermute | solution.py:30
  1.7 2.1 %collective-permute-done.9.refs_9_ = s32[1,16]{1,0:T(1,128)S(1)} collective-permute-done((s32[1,16]{1,0:T(1,128)S(1)}, s32[1,16]{1,0:T(1,128)S(1)}, u32[]{:S(2)}, u32[]{:S(2)}) %collective-permute-start.9) | collective-permute-done | bytes 96 | tf_op jit(solution)/shard_map/ppermute | solution.py:30
  3.7 0.4 collective-permute-start.8
  4.1 0.0 collective-permute-done.7.refs_1_
  4.1 2.6 %collective-permute-start.1 = (bf16[16,2048]{1,0:T(8,128)(2,1)}, bf16[16,2048]{1,0:T(8,128)(2,1)S(1)}, u32[]{:S(2)}, u32[]{:S(2)}) collective-permute-start(bf16[16,2048]{1,0:T(8,128)(2,1)} %bitcast.12), channel_id=1, source_target_pairs={{0,16},{8,24},{16,0},{24,8},{1,17},{9,25},{17,1},{25,9},{2,18},{10... | collective-permute-start | bytes 196616 | tf_op jit(solution)/shard_map/ppermute | solution.py:30
  6.7 0.0 collective-permute-done.8.refs_3_
  6.7 1.3 %collective-permute-start.3 = (bf16[16,2048]{1,0:T(8,128)(2,1)}, bf16[16,2048]{1,0:T(8,128)(2,1)S(1)}, u32[]{:S(2)}, u32[]{:S(2)}) collective-permute-start(bf16[16,2048]{1,0:T(8,128)(2,1)} %bitcast.15), channel_id=1, source_target_pairs={{0,16},{8,24},{16,0},{24,8},{1,17},{9,25},{17,1},{25,9},{2,18},{10... | collective-permute-start | bytes 196616 | tf_op jit(solution)/shard_map/ppermute | solution.py:30
  8.1 1.5 %collective-permute-done.1.refs_0_ = bf16[16,2048]{1,0:T(8,128)(2,1)S(1)} collective-permute-done((bf16[16,2048]{1,0:T(8,128)(2,1)}, bf16[16,2048]{1,0:T(8,128)(2,1)S(1)}, u32[]{:S(2)}, u32[]{:S(2)}) %collective-permute-start.1) | collective-permute-done | bytes 65568 | tf_op jit(solution)/shard_map/ppermute | solution.py:30
  9.6 0.0 collective-permute-start.2
  9.6 1.6 %collective-permute-done.3.refs_2_ = bf16[16,2048]{1,0:T(8,128)(2,1)S(1)} collective-permute-done((bf16[16,2048]{1,0:T(8,128)(2,1)}, bf16[16,2048]{1,0:T(8,128)(2,1)S(1)}, u32[]{:S(2)}, u32[]{:S(2)}) %collective-permute-start.3) | collective-permute-done | bytes 65568 | tf_op jit(solution)/shard_map/ppermute | solution.py:30
  11.2 0.0 collective-permute-start.4
  11.2 1.9 %shard_map.91 = (bf16[2048,256]{1,0:T(8,128)(2,1)S(1)}, f32[512,128]{1,0:T(8,128)S(1)}, f32[512,128]{1,0:T(8,128)S(1)}, bf16[256,512]{1,0:T(8,128)(2,1)S(1)}, bf...) custom-call(bf16[256,512]{1,0:T(8,128)(2,1)} %bitcast.8, ...), custom_call_target="tpu_custom_call" | custom-call | flops 268435456 | bytes 1048576 | tf_op jit(solution)/shard_map/pallas_call | solution.py:362
  13.1 0.0 collective-permute-done.5.refs_5_
  13.1 0.0 collective-permute-done.6.refs_7_
  13.1 0.9 %shard_map.93 = (f32[3,2,128]{2,1,0:T(2,128)S(1)}, f32[2,2,256,128]{3,2,1,0:T(8,128)S(1)}, f32[2,2,256,128]{3,2,1,0:T(8,128)S(1)}, bf16[32,1024]{1,0:T(8,128)(2,1)S(1)}, bf16[32,1024]{1,0:T(8,128)(2,1)}) custom-call(bf16[16,2048]{1,0:T(8,128)(2,1)S(1)} %get-tuple-element.36.refs_0_, bf16[16,2048]{1,0:T(8,128)(2,1)S(1)} %collective-permute-done.7.refs_1_, ...), custom_call_target="tpu_custom_call" | custom-call | flops 67108864 | bytes 1048576 | tf_op jit(solution)/shard_map/pallas_call | solution.py:189
  13.9 0.0 collective-permute-done.2.refs_1_
  14.0 0.0 collective-permute-done.4.refs_3_
  14.0 0.8 %shard_map.94 = (f32[3,2,2,128]{3,2,1,0:T(2,128)S(1)}, f32[2,2,256,128]{3,2,1,0:T(8,128)S(1)}, f32[2,2,256,128]{3,2,1,0:T(8,128)S(1)}, bf16[32,1024]{1,0:T(8,128)(2,1)S(1)}, bf16[32,1024]{1,0:T(8,128)(2,1)}) custom-call(bf16[16,2048]{1,0:T(8,128)(2,1)S(1)} %collective-permute-done.1.refs_0_, bf16[16,2048]{1,0:T(8,128)(2,1)S(1)} %collective-permute-done.2.refs_1_, ...), custom_call_target="tpu_custom_call" | custom-call | flops 67108864 | bytes 1048576 | tf_op jit(solution)/shard_map/pallas_call | solution.py:189
  14.8 1.5 %collective-permute-start.10 = (f32[3,2,2,128]{3,2,1,0:T(2,128)S(1)}, f32[3,2,2,128]{3,2,1,0:T(2,128)S(1)}, u32[]{:S(2)}, u32[]{:S(2)}) collective-permute-start(f32[3,2,2,128]{3,2,1,0:T(2,128)S(1)} %get-tuple-element.40.mine_ref), channel_id=1, source_target_pairs={{0,16},{8,24},{16,0},{24,8},{1,17},{9,25},{17,1},{25,9},{2,18},{10... | collective-permute-start | bytes 18440 | tf_op jit(solution)/shard_map/ppermute | solution.py:30
  16.3 0.0 collective-permute-done.features_ref
  16.3 0.3 shard_map.92.refs_9_.far_ref
  16.6 1.8 %collective-permute-done.10.other_ref = f32[3,2,2,128]{3,2,1,0:T(2,128)S(1)} collective-permute-done((f32[3,2,2,128]{3,2,1,0:T(2,128)S(1)}, f32[3,2,2,128]{3,2,1,0:T(2,128)S(1)}, u32[]{:S(2)}, u32[]{:S(2)}) %collective-permute-start.10) | collective-permute-done | bytes 6176 | tf_op jit(solution)/shard_map/ppermute | solution.py:30
  18.4 0.7 %shard_map.95 = (bf16[2,256,256]{2,1,0:T(8,128)(2,1)S(1)}, bf16[256,256]{1,0:T(8,128)(2,1)S(1)}, bf16[256,256]{1,0:T(8,128)(2,1)S(1)}) custom-call(f32[3,2,2,128]{3,2,1,0:T(2,128)S(1)} %get-tuple-element.40.mine_ref, f32[3,2,2,128]{3,2,1,0:T(2,128)S(1)} %collective-permute-done.10.other_ref, f32[2,2,256,128]{3,2,1,0:T(8,128)S(1)} %get-tuple-element.41.refs_0_, ...), custom_call_target="tpu_custom_call" | custom-call | flops 268435456 | bytes 1048576 | tf_op jit(solution)/shard_map/pallas_call | solution.py:405
  19.2 1.6 %collective-permute-start.15 = (bf16[256,256]{1,0:T(8,128)(2,1)S(1)}, bf16[256,256]{1,0:T(8,128)(2,1)S(1)}, u32[]{:S(2)}, u32[]{:S(2)}) collective-permute-start(bf16[256,256]{1,0:T(8,128)(2,1)S(1)} %get-tuple-element.55), channel_id=1, source_target_pairs={{0,16},{1,17},{2,18},{3,19},{4,20},{5,21},{6,22},{7,23},{8,9},{9,8... | collective-permute-start | bytes 393224 | tf_op jit(solution)/shard_map/ppermute | solution.py:428
  20.7 0.5 %collective-permute-start.12 = (bf16[256,256]{1,0:T(8,128)(2,1)S(1)}, bf16[256,256]{1,0:T(8,128)(2,1)S(1)}, u32[]{:S(2)}, u32[]{:S(2)}) collective-permute-start(bf16[256,256]{1,0:T(8,128)(2,1)S(1)} %get-tuple-element.52), channel_id=1, source_target_pairs={{0,16},{1,17},{2,18},{3,19},{4,20},{5,21},{6,22},{7,23},{8,9},{9,8... | collective-permute-start | bytes 393224 | tf_op jit(solution)/shard_map/ppermute | solution.py:428
  21.2 0.4 %shard_map.97 = (bf16[256,256]{1,0:T(8,128)(2,1)S(1)}, bf16[256,256]{1,0:T(8,128)(2,1)S(1)}, f32[512,256]{1,0:T(8,128)S(1)}) custom-call(bf16[2048,256]{1,0:T(8,128)(2,1)S(1)} %get-tuple-element.33.refs_8_.own_ref, bf16[2048,256]{1,0:T(8,128)(2,1)S(1)} %shard_map.92.refs_9_.far_ref, bf16[2,256,256]{2,1,0:T(8,128)(2,1)S(1)} %get-tuple-element.49.unrot_ref), custom_call_target="tpu_custom_call" | custom-call | flops 268435456 | bytes 1048576 | tf_op jit(solution)/shard_map/pallas_call | solution.py:413
  21.7 1.6 %collective-permute-start.14 = (bf16[256,256]{1,0:T(8,128)(2,1)S(1)}, bf16[256,256]{1,0:T(8,128)(2,1)S(1)}, u32[]{:S(2)}, u32[]{:S(2)}) collective-permute-start(bf16[256,256]{1,0:T(8,128)(2,1)S(1)} %get-tuple-element.54), channel_id=1, source_target_pairs={{0,16},{1,17},{2,18},{3,19},{4,20},{5,21},{6,22},{7,23},{8,9},{9,8... | collective-permute-start | bytes 393224 | tf_op jit(solution)/shard_map/ppermute | solution.py:428
  23.3 0.9 %collective-permute-done.15.come_ref = bf16[256,256]{1,0:T(8,128)(2,1)S(1)} collective-permute-done((bf16[256,256]{1,0:T(8,128)(2,1)S(1)}, bf16[256,256]{1,0:T(8,128)(2,1)S(1)}, u32[]{:S(2)}, u32[]{:S(2)}) %collective-permute-start.15) | collective-permute-done | bytes 131104 | tf_op jit(solution)/shard_map/ppermute | solution.py:428
  24.2 1.6 %collective-permute-start.16 = (bf16[256,256]{1,0:T(8,128)(2,1)S(1)}, bf16[256,256]{1,0:T(8,128)(2,1)S(1)}, u32[]{:S(2)}, u32[]{:S(2)}) collective-permute-start(bf16[256,256]{1,0:T(8,128)(2,1)S(1)} %shard_map.100), channel_id=1, source_target_pairs={{0,1},{1,0},{2,3},{3,2},{4,5},{5,4},{6,7},{7,6},{8,24},{9,25},{10,... | collective-permute-start | bytes 393224 | tf_op jit(solution)/shard_map/ppermute | solution.py:435
  25.8 1.5 %collective-permute-start.11 = (bf16[256,256]{1,0:T(8,128)(2,1)S(1)}, bf16[256,256]{1,0:T(8,128)(2,1)S(1)}, u32[]{:S(2)}, u32[]{:S(2)}) collective-permute-start(bf16[256,256]{1,0:T(8,128)(2,1)S(1)} %get-tuple-element.50), channel_id=1, source_target_pairs={{0,16},{1,17},{2,18},{3,19},{4,20},{5,21},{6,22},{7,23},{8,9},{9,8... | collective-permute-start | bytes 393224 | tf_op jit(solution)/shard_map/ppermute | solution.py:428
  27.3 0.6 %collective-permute-start.13 = (bf16[256,256]{1,0:T(8,128)(2,1)S(1)}, bf16[256,256]{1,0:T(8,128)(2,1)S(1)}, u32[]{:S(2)}, u32[]{:S(2)}) collective-permute-start(bf16[256,256]{1,0:T(8,128)(2,1)S(1)} %shard_map.98), channel_id=1, source_target_pairs={{0,1},{1,0},{2,3},{3,2},{4,5},{5,4},{6,7},{7,6},{8,24},{9,25},{10,... | collective-permute-start | bytes 393224 | tf_op jit(solution)/shard_map/ppermute | solution.py:435
  27.9 0.3 shard_map.96.keep_ref
  28.2 0.9 %collective-permute-done.14.stay_ref = bf16[256,256]{1,0:T(8,128)(2,1)S(1)} collective-permute-done((bf16[256,256]{1,0:T(8,128)(2,1)S(1)}, bf16[256,256]{1,0:T(8,128)(2,1)S(1)}, u32[]{:S(2)}, u32[]{:S(2)}) %collective-permute-start.14) | collective-permute-done | bytes 131104 | tf_op jit(solution)/shard_map/ppermute | solution.py:428
  29.1 0.1 collective-permute-done.16.come_ref
  29.3 1.6 %collective-permute-start.17 = (bf16[128,256]{1,0:T(8,128)(2,1)S(1)}, bf16[128,256]{1,0:T(8,128)(2,1)S(1)}, u32[]{:S(2)}, u32[]{:S(2)}) collective-permute-start(bf16[128,256]{1,0:T(8,128)(2,1)S(1)} %get-tuple-element.56), channel_id=1, source_target_pairs={{0,2},{1,3},{2,4},{3,5},{4,6},{5,7},{6,0},{7,1},{8,10},{9,11},{10,... | collective-permute-start | bytes 196616 | tf_op jit(solution)/shard_map/ppermute | solution.py:449
  30.9 2.6 %collective-permute-start.18 = (bf16[128,256]{1,0:T(8,128)(2,1)S(1)}, bf16[128,256]{1,0:T(8,128)(2,1)S(1)}, u32[]{:S(2)}, u32[]{:S(2)}) collective-permute-start(bf16[128,256]{1,0:T(8,128)(2,1)S(1)} %get-tuple-element.57), channel_id=1, source_target_pairs={{0,4},{1,5},{2,6},{3,7},{4,0},{5,1},{6,2},{7,3},{8,12},{9,13},{10,... | collective-permute-start | bytes 196616 | tf_op jit(solution)/shard_map/ppermute | solution.py:449
  33.5 0.0 collective-permute-done.11.stay_ref
  33.6 2.5 %collective-permute-start.19 = (bf16[128,256]{1,0:T(8,128)(2,1)S(1)}, bf16[128,256]{1,0:T(8,128)(2,1)S(1)}, u32[]{:S(2)}, u32[]{:S(2)}) collective-permute-start(bf16[128,256]{1,0:T(8,128)(2,1)S(1)} %get-tuple-element.58), channel_id=1, source_target_pairs={{0,6},{1,7},{2,0},{3,1},{4,2},{5,3},{6,4},{7,5},{8,14},{9,15},{10,... | collective-permute-start | bytes 196616 | tf_op jit(solution)/shard_map/ppermute | solution.py:449
  36.1 1.5 %collective-permute-done.18.refs_2_ = bf16[128,256]{1,0:T(8,128)(2,1)S(1)} collective-permute-done((bf16[128,256]{1,0:T(8,128)(2,1)S(1)}, bf16[128,256]{1,0:T(8,128)(2,1)S(1)}, u32[]{:S(2)}, u32[]{:S(2)}) %collective-permute-start.18) | collective-permute-done | bytes 65568 | tf_op jit(solution)/shard_map/ppermute | solution.py:449
  37.6 0.5 %collective-permute-done.19.refs_3_ = bf16[128,256]{1,0:T(8,128)(2,1)S(1)} collective-permute-done((bf16[128,256]{1,0:T(8,128)(2,1)S(1)}, bf16[128,256]{1,0:T(8,128)(2,1)S(1)}, u32[]{:S(2)}, u32[]{:S(2)}) %collective-permute-start.19) | collective-permute-done | bytes 65568 | tf_op jit(solution)/shard_map/ppermute | solution.py:449
  38.1 0.1 collective-permute-start.20
  38.2 1.2 %collective-permute-done.20.there_ref = f32[64,256]{1,0:T(8,128)S(1)} collective-permute-done((f32[64,256]{1,0:T(8,128)S(1)}, f32[64,256]{1,0:T(8,128)S(1)}, u32[]{:S(2)}, u32[]{:S(2)}) %collective-permute-start.20) | collective-permute-done | bytes 65568 | tf_op jit(solution)/shard_map/ppermute | solution.py:30
  39.4 0.7 %shard_map.103 = f32[64,512]{1,0:T(8,128)} custom-call(f32[64,256]{1,0:T(8,128)S(1)} %get-tuple-element.59.here_ref, f32[64,256]{1,0:T(8,128)S(1)} %collective-permute-done.20.there_ref, f32[64,512]{1,0:T(8,128)S(1)} %copy-done), custom_call_target="tpu_custom_call" | custom-call | flops 1048576 | bytes 1048576 | tf_op jit(solution)/shard_map/pallas_call | solution.py:453
  (11 shorter events, 0.2 us)
Async XLA Ops:
  0.0 16.3 %collective-permute-start = (bf16[256,2048]{1,0:T(8,128)(2,1)}, bf16[256,2048]{1,0:T(8,128)(2,1)S(1)}, u32[]{:S(2)}, u32[]{:S(2)}) collective-permute-start(bf16[256,2048]{1,0:T(8,128)(2,1)} %bitcast.5), channel_id=1, source_target_pairs={{0,8},{8,0},{16,24},{24,16},{1,9},{9,1},{17,25},{25,17},{2,10},{10... | collective-permute-start | bytes 3145736 | tf_op jit(solution)/shard_map/ppermute | solution.py:30
  0.5 0.7 %copy-start.1 = (s32[1,16]{1,0:T(1,128)S(1)}, s32[1,16]{1,0:T(1,128)}, u32[]{:S(2)}) copy-start(s32[1,16]{1,0:T(1,128)} %refs_4_.1) | copy-start | bytes 196
  0.5 12.6 %collective-permute-start.5 = (bf16[256,512]{1,0:T(8,128)(2,1)}, bf16[256,512]{1,0:T(8,128)(2,1)S(1)}, u32[]{:S(2)}, u32[]{:S(2)}) collective-permute-start(bf16[256,512]{1,0:T(8,128)(2,1)} %bitcast.7), channel_id=1, source_target_pairs={{0,8},{8,0},{16,24},{24,16},{1,9},{9,1},{17,25},{25,17},{2,10},{10... | collective-permute-start | bytes 786440 | tf_op jit(solution)/shard_map/ppermute | solution.py:30
  0.6 12.5 %collective-permute-start.6 = (bf16[256,512]{1,0:T(8,128)(2,1)}, bf16[256,512]{1,0:T(8,128)(2,1)S(1)}, u32[]{:S(2)}, u32[]{:S(2)}) collective-permute-start(bf16[256,512]{1,0:T(8,128)(2,1)} %bitcast.9), channel_id=1, source_target_pairs={{0,8},{8,0},{16,24},{24,16},{1,9},{9,1},{17,25},{25,17},{2,10},{10... | collective-permute-start | bytes 786440 | tf_op jit(solution)/shard_map/ppermute | solution.py:30
  1.1 2.6 %collective-permute-start.9 = (s32[1,16]{1,0:T(1,128)S(1)}, s32[1,16]{1,0:T(1,128)S(1)}, u32[]{:S(2)}, u32[]{:S(2)}) collective-permute-start(s32[1,16]{1,0:T(1,128)S(1)} %copy-done.1), channel_id=1, source_target_pairs={{0,8},{8,0},{16,24},{24,16},{1,9},{9,1},{17,25},{25,17},{2,10},{10... | collective-permute-start | bytes 200 | tf_op jit(solution)/shard_map/ppermute | solution.py:30
  1.2 3.0 %collective-permute-start.7 = (bf16[16,2048]{1,0:T(8,128)(2,1)}, bf16[16,2048]{1,0:T(8,128)(2,1)S(1)}, u32[]{:S(2)}, u32[]{:S(2)}) collective-permute-start(bf16[16,2048]{1,0:T(8,128)(2,1)} %bitcast.11), channel_id=1, source_target_pairs={{0,8},{8,0},{16,24},{24,16},{1,9},{9,1},{17,25},{25,17},{2,10},{10... | collective-permute-start | bytes 196616 | tf_op jit(solution)/shard_map/ppermute | solution.py:30
  3.7 3.0 %collective-permute-start.8 = (bf16[16,2048]{1,0:T(8,128)(2,1)}, bf16[16,2048]{1,0:T(8,128)(2,1)S(1)}, u32[]{:S(2)}, u32[]{:S(2)}) collective-permute-start(bf16[16,2048]{1,0:T(8,128)(2,1)} %bitcast.14), channel_id=1, source_target_pairs={{0,8},{8,0},{16,24},{24,16},{1,9},{9,1},{17,25},{25,17},{2,10},{10... | collective-permute-start | bytes 196616 | tf_op jit(solution)/shard_map/ppermute | solution.py:30
  4.1 5.5 %collective-permute-start.1 = (bf16[16,2048]{1,0:T(8,128)(2,1)}, bf16[16,2048]{1,0:T(8,128)(2,1)S(1)}, u32[]{:S(2)}, u32[]{:S(2)}) collective-permute-start(bf16[16,2048]{1,0:T(8,128)(2,1)} %bitcast.12), channel_id=1, source_target_pairs={{0,16},{8,24},{16,0},{24,8},{1,17},{9,25},{17,1},{25,9},{2,18},{10... | collective-permute-start | bytes 196616 | tf_op jit(solution)/shard_map/ppermute | solution.py:30
  6.7 4.5 %collective-permute-start.3 = (bf16[16,2048]{1,0:T(8,128)(2,1)}, bf16[16,2048]{1,0:T(8,128)(2,1)S(1)}, u32[]{:S(2)}, u32[]{:S(2)}) collective-permute-start(bf16[16,2048]{1,0:T(8,128)(2,1)} %bitcast.15), channel_id=1, source_target_pairs={{0,16},{8,24},{16,0},{24,8},{1,17},{9,25},{17,1},{25,9},{2,18},{10... | collective-permute-start | bytes 196616 | tf_op jit(solution)/shard_map/ppermute | solution.py:30
  9.6 4.4 %collective-permute-start.2 = (bf16[16,2048]{1,0:T(8,128)(2,1)S(1)}, bf16[16,2048]{1,0:T(8,128)(2,1)S(1)}, u32[]{:S(2)}, u32[]{:S(2)}) collective-permute-start(bf16[16,2048]{1,0:T(8,128)(2,1)S(1)} %collective-permute-done.1.refs_0_), channel_id=1, source_target_pairs={{0,8},{8,0},{16,24},{24,16},{1,9},{9,1},{17,25},{25,17},{2,10},{10... | collective-permute-start | bytes 196616 | tf_op jit(solution)/shard_map/ppermute | solution.py:30
  11.2 2.7 %collective-permute-start.4 = (bf16[16,2048]{1,0:T(8,128)(2,1)S(1)}, bf16[16,2048]{1,0:T(8,128)(2,1)S(1)}, u32[]{:S(2)}, u32[]{:S(2)}) collective-permute-start(bf16[16,2048]{1,0:T(8,128)(2,1)S(1)} %collective-permute-done.3.refs_2_), channel_id=1, source_target_pairs={{0,8},{8,0},{16,24},{24,16},{1,9},{9,1},{17,25},{25,17},{2,10},{10... | collective-permute-start | bytes 196616 | tf_op jit(solution)/shard_map/ppermute | solution.py:30
  14.8 3.6 %collective-permute-start.10 = (f32[3,2,2,128]{3,2,1,0:T(2,128)S(1)}, f32[3,2,2,128]{3,2,1,0:T(2,128)S(1)}, u32[]{:S(2)}, u32[]{:S(2)}) collective-permute-start(f32[3,2,2,128]{3,2,1,0:T(2,128)S(1)} %get-tuple-element.40.mine_ref), channel_id=1, source_target_pairs={{0,16},{8,24},{16,0},{24,8},{1,17},{9,25},{17,1},{25,9},{2,18},{10... | collective-permute-start | bytes 18440 | tf_op jit(solution)/shard_map/ppermute | solution.py:30
  19.2 5.0 %collective-permute-start.15 = (bf16[256,256]{1,0:T(8,128)(2,1)S(1)}, bf16[256,256]{1,0:T(8,128)(2,1)S(1)}, u32[]{:S(2)}, u32[]{:S(2)}) collective-permute-start(bf16[256,256]{1,0:T(8,128)(2,1)S(1)} %get-tuple-element.55), channel_id=1, source_target_pairs={{0,16},{1,17},{2,18},{3,19},{4,20},{5,21},{6,22},{7,23},{8,9},{9,8... | collective-permute-start | bytes 393224 | tf_op jit(solution)/shard_map/ppermute | solution.py:428
  20.7 6.6 %collective-permute-start.12 = (bf16[256,256]{1,0:T(8,128)(2,1)S(1)}, bf16[256,256]{1,0:T(8,128)(2,1)S(1)}, u32[]{:S(2)}, u32[]{:S(2)}) collective-permute-start(bf16[256,256]{1,0:T(8,128)(2,1)S(1)} %get-tuple-element.52), channel_id=1, source_target_pairs={{0,16},{1,17},{2,18},{3,19},{4,20},{5,21},{6,22},{7,23},{8,9},{9,8... | collective-permute-start | bytes 393224 | tf_op jit(solution)/shard_map/ppermute | solution.py:428
  21.7 7.4 %collective-permute-start.14 = (bf16[256,256]{1,0:T(8,128)(2,1)S(1)}, bf16[256,256]{1,0:T(8,128)(2,1)S(1)}, u32[]{:S(2)}, u32[]{:S(2)}) collective-permute-start(bf16[256,256]{1,0:T(8,128)(2,1)S(1)} %get-tuple-element.54), channel_id=1, source_target_pairs={{0,16},{1,17},{2,18},{3,19},{4,20},{5,21},{6,22},{7,23},{8,9},{9,8... | collective-permute-start | bytes 393224 | tf_op jit(solution)/shard_map/ppermute | solution.py:428
  24.2 5.0 %collective-permute-start.16 = (bf16[256,256]{1,0:T(8,128)(2,1)S(1)}, bf16[256,256]{1,0:T(8,128)(2,1)S(1)}, u32[]{:S(2)}, u32[]{:S(2)}) collective-permute-start(bf16[256,256]{1,0:T(8,128)(2,1)S(1)} %shard_map.100), channel_id=1, source_target_pairs={{0,1},{1,0},{2,3},{3,2},{4,5},{5,4},{6,7},{7,6},{8,24},{9,25},{10,... | collective-permute-start | bytes 393224 | tf_op jit(solution)/shard_map/ppermute | solution.py:435
  25.8 7.7 %collective-permute-start.11 = (bf16[256,256]{1,0:T(8,128)(2,1)S(1)}, bf16[256,256]{1,0:T(8,128)(2,1)S(1)}, u32[]{:S(2)}, u32[]{:S(2)}) collective-permute-start(bf16[256,256]{1,0:T(8,128)(2,1)S(1)} %get-tuple-element.50), channel_id=1, source_target_pairs={{0,16},{1,17},{2,18},{3,19},{4,20},{5,21},{6,22},{7,23},{8,9},{9,8... | collective-permute-start | bytes 393224 | tf_op jit(solution)/shard_map/ppermute | solution.py:428
  27.3 6.2 %collective-permute-start.13 = (bf16[256,256]{1,0:T(8,128)(2,1)S(1)}, bf16[256,256]{1,0:T(8,128)(2,1)S(1)}, u32[]{:S(2)}, u32[]{:S(2)}) collective-permute-start(bf16[256,256]{1,0:T(8,128)(2,1)S(1)} %shard_map.98), channel_id=1, source_target_pairs={{0,1},{1,0},{2,3},{3,2},{4,5},{5,4},{6,7},{7,6},{8,24},{9,25},{10,... | collective-permute-start | bytes 393224 | tf_op jit(solution)/shard_map/ppermute | solution.py:435
  29.3 6.8 %collective-permute-start.17 = (bf16[128,256]{1,0:T(8,128)(2,1)S(1)}, bf16[128,256]{1,0:T(8,128)(2,1)S(1)}, u32[]{:S(2)}, u32[]{:S(2)}) collective-permute-start(bf16[128,256]{1,0:T(8,128)(2,1)S(1)} %get-tuple-element.56), channel_id=1, source_target_pairs={{0,2},{1,3},{2,4},{3,5},{4,6},{5,7},{6,0},{7,1},{8,10},{9,11},{10,... | collective-permute-start | bytes 196616 | tf_op jit(solution)/shard_map/ppermute | solution.py:449
  30.9 6.7 %collective-permute-start.18 = (bf16[128,256]{1,0:T(8,128)(2,1)S(1)}, bf16[128,256]{1,0:T(8,128)(2,1)S(1)}, u32[]{:S(2)}, u32[]{:S(2)}) collective-permute-start(bf16[128,256]{1,0:T(8,128)(2,1)S(1)} %get-tuple-element.57), channel_id=1, source_target_pairs={{0,4},{1,5},{2,6},{3,7},{4,0},{5,1},{6,2},{7,3},{8,12},{9,13},{10,... | collective-permute-start | bytes 196616 | tf_op jit(solution)/shard_map/ppermute | solution.py:449
  33.6 4.5 %collective-permute-start.19 = (bf16[128,256]{1,0:T(8,128)(2,1)S(1)}, bf16[128,256]{1,0:T(8,128)(2,1)S(1)}, u32[]{:S(2)}, u32[]{:S(2)}) collective-permute-start(bf16[128,256]{1,0:T(8,128)(2,1)S(1)} %get-tuple-element.58), channel_id=1, source_target_pairs={{0,6},{1,7},{2,0},{3,1},{4,2},{5,3},{6,4},{7,5},{8,14},{9,15},{10,... | collective-permute-start | bytes 196616 | tf_op jit(solution)/shard_map/ppermute | solution.py:449
  38.1 1.4 %copy-start = (f32[64,512]{1,0:T(8,128)S(1)}, f32[64,512]{1,0:T(8,128)}, u32[]{:S(2)}) copy-start(f32[64,512]{1,0:T(8,128)} %hessian_ref.1) | copy-start | bytes 393220
  38.1 1.3 %collective-permute-start.20 = (f32[64,256]{1,0:T(8,128)S(1)}, f32[64,256]{1,0:T(8,128)S(1)}, u32[]{:S(2)}, u32[]{:S(2)}) collective-permute-start(f32[64,256]{1,0:T(8,128)S(1)} %get-tuple-element.60), channel_id=1, source_target_pairs={{0,8},{8,0},{16,24},{24,16},{1,9},{9,1},{17,25},{25,17},{2,10},{10... | collective-permute-start | bytes 196616 | tf_op jit(solution)/shard_map/ppermute | solution.py:30

commit v5 on v4

--- a/solution.py
+++ b/solution.py
@@ -290,8 +290,25 @@
         out_ref[...] = total.astype(out_ref.dtype)
 
 
+def last_total_kernel(
+    keep_start, stay_start, keep_ref, stay_ref, come_ref, same_ref, cross_ref, mine_ref
+):
+    half = same_ref.shape[0]
+    core = position()[0]
+    for start, size, out_ref in (
+        (core * half, half, same_ref),
+        ((1 - core) * half, half, cross_ref),
+        (2 * half, 2 * half, mine_ref),
+    ):
+        total = keep_ref[pl.ds(pl.multiple_of(keep_start + start, half), size), :]
+        for first, ref in ((stay_start, stay_ref), (0, come_ref)):
+            at = pl.ds(pl.multiple_of(first + start, half), size)
+            total += ref[at, :].astype(jnp.float32)
+        out_ref[...] = total.astype(out_ref.dtype)
+
+
 def last_kernel(*refs):
-    terms, (here_ref, there_ref) = refs[:4], refs[4:]
+    terms, (here_ref, there_ref) = refs[:-2], refs[-2:]
     rows = here_ref.shape[0]
     core = position()[0]
     for owner, out_ref in ((1 - core, there_ref), (core, here_ref)):
@@ -299,12 +316,12 @@
         out_ref[...] = sum(ref[at, :].astype(jnp.float32) for ref in terms)
 
 
-def next_kernel(scale, here_ref, there_ref, hessian_ref, out_ref):
+def next_kernel(scale, here_ref, same_ref, there_ref, cross_ref, hessian_ref, out_ref):
     width = here_ref.shape[1]
     core = position()[0]
-    for owner, ref in ((core, here_ref), (1 - core, there_ref)):
+    for owner, near, far in ((core, here_ref, same_ref), (1 - core, there_ref, cross_ref)):
         columns = pl.ds(pl.multiple_of(owner * width, width), width)
-        term = ref[...]
+        term = near[...] + far[...].astype(jnp.float32)
         out_ref[:, columns] = decay_rate * hessian_ref[:, columns] + scale * term * term
 
 
@@ -433,29 +450,34 @@
             functools.partial(add_kernel, rows * first), block(chunk), [VMEM] * 2, 1 << 20
         )(turn_keep, come[number])
         arrived = lax.ppermute(send, BOTH, route_after)
-        outs = [block((0,), jnp.bfloat16 if distance else jnp.float32) for distance in chunk]
+        kernel, outs = total_kernel, [block((distance,)) for distance in chunk]
+        if 0 in chunk:
+            split = [shape((out_rows, wide), jnp.bfloat16)] * 2
+            kernel, outs = last_total_kernel, split + [block((0,), jnp.float32)]
         source = next(i for i, other in enumerate(STAY) if chunk[0] in other)
         inside = STAY[source].index(chunk[0])
         totals += call(
-            functools.partial(total_kernel, rows * first, rows * inside),
+            functools.partial(kernel, rows * first, rows * inside),
             outs,
             [VMEM] * 3,
             1 << 20,
         )(stay_keep, come[len(TRAVEL) + source], arrived)
-    sends, mine = totals[:3], totals[3]
+    *sends, cross, mine = totals
     arrived = []
     for distance, send in zip(everywhere, sends):
         along = [(i, (i + 2 * distance) % 8) for i in range(8)]
         arrived.append(lax.ppermute(send, "fsdp", along))
+    across = [(i, (i // 8 ^ 1) * 8 + (i + 6) % 8) for i in range(32)]
+    cross = lax.ppermute(cross, BOTH, across)
     columns = shape((out_rows, wide), jnp.float32)
-    here, there = call(last_kernel, [columns] * 2, [VMEM] * 4, 1 << 20)(mine, *arrived)
+    here, there = call(last_kernel, [columns] * 2, [VMEM] * 3, 1 << 20)(mine, *arrived[:2])
     there = swapped(there, "blk", 1)
     return call(
         functools.partial(next_kernel, (1.0 - decay_rate) / lax.axis_size("fsdp")),
         shape(hessian.shape, jnp.float32),
-        [VMEM] * 3,
+        [VMEM] * 5,
         1 << 20,
-    )(here, there, hessian)
+    )(here, arrived[2], there, cross, hessian)
 
 
 def reduced_anywhere(normed, picked, queries, key_states, values, cotangent):

time: 40.3 us -> 42.9 us (1.065)
  starting transfers between devices: 21.4 us -> 22.8 us
  waiting for transfers between devices: 12.3 us -> 13.5 us
    ppermute x0 -> x1, waiting for transfers between devices: none -> 1.75 us  [reduced_on_torus(): cross = lax.ppermute(cross, BOTH, across)]
    ppermute x0 -> x1, starting transfers between devices: none -> 1.42 us  [reduced_on_torus(): cross = lax.ppermute(cross, BOTH, across)]
    ppermute x12, waiting for transfers between devices: 8.29 us -> 7.05 us  [swapped(): return lax.ppermute(block, axis, route)]
    ppermute x3, waiting for transfers between devices: 2.01 us -> 2.71 us  [reduced_on_torus(): arrived.append(lax.ppermute(send, 'fsdp', along))]
  transfers between devices with their start and end apart: 21 -> 22, of which waited for: 10 -> 11; matrix products, arithmetic and copies ran while one was open for 0% -> 0% of each run, Pallas kernels for 12% -> 11%
where the time goes in v5:
time: 42.9 us; the launch traced here: 42.7 us
  starting transfers between devices  22.8 us (53%)
  waiting for transfers between devices  13.5 us (31%)
  Pallas kernels  6.17 us (14%)
    ppermute x12, starting transfers between devices, swapped(): return lax.ppermute(block, axis, route)  7.4 us
    ppermute x12, waiting for transfers between devices, swapped(): return lax.ppermute(block, axis, route)  7.05 us
    ppermute x3, starting transfers between devices, reduced_on_torus(): arrived.append(lax.ppermute(send, 'fsdp', along))  6.69 us
    ppermute x4, starting transfers between devices, reduced_on_torus(): come.append(lax.ppermute(send, BOTH, route))  5.14 us
    ppermute x3, waiting for transfers between devices, reduced_on_torus(): arrived.append(lax.ppermute(send, 'fsdp', along))  2.71 us
    ppermute x2, starting transfers between devices, reduced_on_torus(): arrived = lax.ppermute(send, BOTH, route_after)  2.17 us
    pallas_call x1, Pallas kernels, reduced_on_torus(): call(own_kernel, [turned, table, table] + [shape(array.shape, array.dtype...  1.85 us
    ppermute x4, waiting for transfers between devices, reduced_on_torus(): come.append(lax.ppermute(send, BOTH, route))  1.83 us
  transfers between devices with their start and end apart: 22, of which 11 were waited for; matrix products, arithmetic and copies ran while one was open for 0% of the time, Pallas kernels for 11%

profile of v5, /device:TPU:0, one launch (start us, length us, event | category | flops | bytes accessed | tf_op | source)
XLA Modules:
  0.0 42.7 jit_solution(11289902867404124901)
XLA Ops:
  0.0 0.5 %collective-permute-start = (bf16[256,2048]{1,0:T(8,128)(2,1)}, bf16[256,2048]{1,0:T(8,128)(2,1)S(1)}, u32[]{:S(2)}, u32[]{:S(2)}) collective-permute-start(bf16[256,2048]{1,0:T(8,128)(2,1)} %bitcast.5), channel_id=1, source_target_pairs={{0,8},{8,0},{16,24},{24,16},{1,9},{9,1},{17,25},{25,17},{2,10},{10... | collective-permute-start | bytes 3145736 | tf_op jit(solution)/shard_map/ppermute | solution.py:30
  0.5 0.1 collective-permute-start.5
  0.6 0.4 %collective-permute-start.6 = (bf16[256,512]{1,0:T(8,128)(2,1)}, bf16[256,512]{1,0:T(8,128)(2,1)S(1)}, u32[]{:S(2)}, u32[]{:S(2)}) collective-permute-start(bf16[256,512]{1,0:T(8,128)(2,1)} %bitcast.9), channel_id=1, source_target_pairs={{0,8},{8,0},{16,24},{24,16},{1,9},{9,1},{17,25},{25,17},{2,10},{10... | collective-permute-start | bytes 786440 | tf_op jit(solution)/shard_map/ppermute | solution.py:30
  1.0 0.1 copy-done.1
  1.1 0.0 collective-permute-start.9
  1.2 0.5 %collective-permute-start.7 = (bf16[16,2048]{1,0:T(8,128)(2,1)}, bf16[16,2048]{1,0:T(8,128)(2,1)S(1)}, u32[]{:S(2)}, u32[]{:S(2)}) collective-permute-start(bf16[16,2048]{1,0:T(8,128)(2,1)} %bitcast.11), channel_id=1, source_target_pairs={{0,8},{8,0},{16,24},{24,16},{1,9},{9,1},{17,25},{25,17},{2,10},{10... | collective-permute-start | bytes 196616 | tf_op jit(solution)/shard_map/ppermute | solution.py:30
  1.7 2.1 %collective-permute-done.9.refs_9_ = s32[1,16]{1,0:T(1,128)S(1)} collective-permute-done((s32[1,16]{1,0:T(1,128)S(1)}, s32[1,16]{1,0:T(1,128)S(1)}, u32[]{:S(2)}, u32[]{:S(2)}) %collective-permute-start.9) | collective-permute-done | bytes 96 | tf_op jit(solution)/shard_map/ppermute | solution.py:30
  3.7 0.4 collective-permute-start.8
  4.1 0.0 collective-permute-done.7.refs_1_
  4.1 2.6 %collective-permute-start.1 = (bf16[16,2048]{1,0:T(8,128)(2,1)}, bf16[16,2048]{1,0:T(8,128)(2,1)S(1)}, u32[]{:S(2)}, u32[]{:S(2)}) collective-permute-start(bf16[16,2048]{1,0:T(8,128)(2,1)} %bitcast.12), channel_id=1, source_target_pairs={{0,16},{8,24},{16,0},{24,8},{1,17},{9,25},{17,1},{25,9},{2,18},{10... | collective-permute-start | bytes 196616 | tf_op jit(solution)/shard_map/ppermute | solution.py:30
  6.7 0.0 collective-permute-done.8.refs_3_
  6.7 1.3 %collective-permute-start.3 = (bf16[16,2048]{1,0:T(8,128)(2,1)}, bf16[16,2048]{1,0:T(8,128)(2,1)S(1)}, u32[]{:S(2)}, u32[]{:S(2)}) collective-permute-start(bf16[16,2048]{1,0:T(8,128)(2,1)} %bitcast.15), channel_id=1, source_target_pairs={{0,16},{8,24},{16,0},{24,8},{1,17},{9,25},{17,1},{25,9},{2,18},{10... | collective-permute-start | bytes 196616 | tf_op jit(solution)/shard_map/ppermute | solution.py:30
  8.1 1.5 %collective-permute-done.1.refs_0_ = bf16[16,2048]{1,0:T(8,128)(2,1)S(1)} collective-permute-done((bf16[16,2048]{1,0:T(8,128)(2,1)}, bf16[16,2048]{1,0:T(8,128)(2,1)S(1)}, u32[]{:S(2)}, u32[]{:S(2)}) %collective-permute-start.1) | collective-permute-done | bytes 65568 | tf_op jit(solution)/shard_map/ppermute | solution.py:30
  9.6 0.0 collective-permute-start.2
  9.6 1.6 %collective-permute-done.3.refs_2_ = bf16[16,2048]{1,0:T(8,128)(2,1)S(1)} collective-permute-done((bf16[16,2048]{1,0:T(8,128)(2,1)}, bf16[16,2048]{1,0:T(8,128)(2,1)S(1)}, u32[]{:S(2)}, u32[]{:S(2)}) %collective-permute-start.3) | collective-permute-done | bytes 65568 | tf_op jit(solution)/shard_map/ppermute | solution.py:30
  11.2 0.0 collective-permute-start.4
  11.2 1.9 %shard_map.91 = (bf16[2048,256]{1,0:T(8,128)(2,1)S(1)}, f32[512,128]{1,0:T(8,128)S(1)}, f32[512,128]{1,0:T(8,128)S(1)}, bf16[256,512]{1,0:T(8,128)(2,1)S(1)}, bf...) custom-call(bf16[256,512]{1,0:T(8,128)(2,1)} %bitcast.8, ...), custom_call_target="tpu_custom_call" | custom-call | flops 268435456 | bytes 1048576 | tf_op jit(solution)/shard_map/pallas_call | solution.py:379
  13.1 0.0 collective-permute-done.5.refs_5_
  13.1 0.0 collective-permute-done.6.refs_7_
  13.1 0.9 %shard_map.93 = (f32[3,2,128]{2,1,0:T(2,128)S(1)}, f32[2,2,256,128]{3,2,1,0:T(8,128)S(1)}, f32[2,2,256,128]{3,2,1,0:T(8,128)S(1)}, bf16[32,1024]{1,0:T(8,128)(2,1)S(1)}, bf16[32,1024]{1,0:T(8,128)(2,1)}) custom-call(bf16[16,2048]{1,0:T(8,128)(2,1)S(1)} %get-tuple-element.37.refs_0_, bf16[16,2048]{1,0:T(8,128)(2,1)S(1)} %collective-permute-done.7.refs_1_, ...), custom_call_target="tpu_custom_call" | custom-call | flops 67108864 | bytes 1048576 | tf_op jit(solution)/shard_map/pallas_call | solution.py:189
  13.9 0.0 collective-permute-done.2.refs_1_
  14.0 0.8 %shard_map.94 = (f32[3,2,2,128]{3,2,1,0:T(2,128)S(1)}, f32[2,2,256,128]{3,2,1,0:T(8,128)S(1)}, f32[2,2,256,128]{3,2,1,0:T(8,128)S(1)}, bf16[32,1024]{1,0:T(8,128)(2,1)S(1)}, bf16[32,1024]{1,0:T(8,128)(2,1)}) custom-call(bf16[16,2048]{1,0:T(8,128)(2,1)S(1)} %collective-permute-done.1.refs_0_, bf16[16,2048]{1,0:T(8,128)(2,1)S(1)} %collective-permute-done.2.refs_1_, ...), custom_call_target="tpu_custom_call" | custom-call | flops 67108864 | bytes 1048576 | tf_op jit(solution)/shard_map/pallas_call | solution.py:189
  14.8 1.5 %collective-permute-start.10 = (f32[3,2,2,128]{3,2,1,0:T(2,128)S(1)}, f32[3,2,2,128]{3,2,1,0:T(2,128)S(1)}, u32[]{:S(2)}, u32[]{:S(2)}) collective-permute-start(f32[3,2,2,128]{3,2,1,0:T(2,128)S(1)} %get-tuple-element.41.mine_ref), channel_id=1, source_target_pairs={{0,16},{8,24},{16,0},{24,8},{1,17},{9,25},{17,1},{25,9},{2,18},{10... | collective-permute-start | bytes 18440 | tf_op jit(solution)/shard_map/ppermute | solution.py:30
  16.3 0.3 shard_map.92.refs_9_.far_ref
  16.6 1.8 %collective-permute-done.10.other_ref = f32[3,2,2,128]{3,2,1,0:T(2,128)S(1)} collective-permute-done((f32[3,2,2,128]{3,2,1,0:T(2,128)S(1)}, f32[3,2,2,128]{3,2,1,0:T(2,128)S(1)}, u32[]{:S(2)}, u32[]{:S(2)}) %collective-permute-start.10) | collective-permute-done | bytes 6176 | tf_op jit(solution)/shard_map/ppermute | solution.py:30
  18.4 0.7 %shard_map.95 = (bf16[2,256,256]{2,1,0:T(8,128)(2,1)S(1)}, bf16[256,256]{1,0:T(8,128)(2,1)S(1)}, bf16[256,256]{1,0:T(8,128)(2,1)S(1)}) custom-call(f32[3,2,2,128]{3,2,1,0:T(2,128)S(1)} %get-tuple-element.41.mine_ref, f32[3,2,2,128]{3,2,1,0:T(2,128)S(1)} %collective-permute-done.10.other_ref, f32[2,2,256,128]{3,2,1,0:T(8,128)S(1)} %get-tuple-element.42.refs_0_, ...), custom_call_target="tpu_custom_call" | custom-call | flops 268435456 | bytes 1048576 | tf_op jit(solution)/shard_map/pallas_call | solution.py:422
  19.2 1.6 %collective-permute-start.15 = (bf16[256,256]{1,0:T(8,128)(2,1)S(1)}, bf16[256,256]{1,0:T(8,128)(2,1)S(1)}, u32[]{:S(2)}, u32[]{:S(2)}) collective-permute-start(bf16[256,256]{1,0:T(8,128)(2,1)S(1)} %get-tuple-element.56), channel_id=1, source_target_pairs={{0,16},{1,17},{2,18},{3,19},{4,20},{5,21},{6,22},{7,23},{8,9},{9,8... | collective-permute-start | bytes 393224 | tf_op jit(solution)/shard_map/ppermute | solution.py:445
  20.7 0.5 %collective-permute-start.12 = (bf16[256,256]{1,0:T(8,128)(2,1)S(1)}, bf16[256,256]{1,0:T(8,128)(2,1)S(1)}, u32[]{:S(2)}, u32[]{:S(2)}) collective-permute-start(bf16[256,256]{1,0:T(8,128)(2,1)S(1)} %get-tuple-element.53), channel_id=1, source_target_pairs={{0,16},{1,17},{2,18},{3,19},{4,20},{5,21},{6,22},{7,23},{8,9},{9,8... | collective-permute-start | bytes 393224 | tf_op jit(solution)/shard_map/ppermute | solution.py:445
  21.2 0.4 %shard_map.97 = (bf16[256,256]{1,0:T(8,128)(2,1)S(1)}, bf16[256,256]{1,0:T(8,128)(2,1)S(1)}, f32[512,256]{1,0:T(8,128)S(1)}) custom-call(bf16[2048,256]{1,0:T(8,128)(2,1)S(1)} %get-tuple-element.34.refs_8_.own_ref, bf16[2048,256]{1,0:T(8,128)(2,1)S(1)} %shard_map.92.refs_9_.far_ref, bf16[2,256,256]{2,1,0:T(8,128)(2,1)S(1)} %get-tuple-element.50.unrot_ref), custom_call_target="tpu_custom_call" | custom-call | flops 268435456 | bytes 1048576 | tf_op jit(solution)/shard_map/pallas_call | solution.py:430
  21.7 1.6 %collective-permute-start.14 = (bf16[256,256]{1,0:T(8,128)(2,1)S(1)}, bf16[256,256]{1,0:T(8,128)(2,1)S(1)}, u32[]{:S(2)}, u32[]{:S(2)}) collective-permute-start(bf16[256,256]{1,0:T(8,128)(2,1)S(1)} %get-tuple-element.55), channel_id=1, source_target_pairs={{0,16},{1,17},{2,18},{3,19},{4,20},{5,21},{6,22},{7,23},{8,9},{9,8... | collective-permute-start | bytes 393224 | tf_op jit(solution)/shard_map/ppermute | solution.py:445
  23.3 0.9 %collective-permute-done.15.come_ref = bf16[256,256]{1,0:T(8,128)(2,1)S(1)} collective-permute-done((bf16[256,256]{1,0:T(8,128)(2,1)S(1)}, bf16[256,256]{1,0:T(8,128)(2,1)S(1)}, u32[]{:S(2)}, u32[]{:S(2)}) %collective-permute-start.15) | collective-permute-done | bytes 131104 | tf_op jit(solution)/shard_map/ppermute | solution.py:445
  24.2 1.6 %collective-permute-start.16 = (bf16[256,256]{1,0:T(8,128)(2,1)S(1)}, bf16[256,256]{1,0:T(8,128)(2,1)S(1)}, u32[]{:S(2)}, u32[]{:S(2)}) collective-permute-start(bf16[256,256]{1,0:T(8,128)(2,1)S(1)} %shard_map.100), channel_id=1, source_target_pairs={{0,1},{1,0},{2,3},{3,2},{4,5},{5,4},{6,7},{7,6},{8,24},{9,25},{10,... | collective-permute-start | bytes 393224 | tf_op jit(solution)/shard_map/ppermute | solution.py:452
  25.8 1.5 %collective-permute-start.11 = (bf16[256,256]{1,0:T(8,128)(2,1)S(1)}, bf16[256,256]{1,0:T(8,128)(2,1)S(1)}, u32[]{:S(2)}, u32[]{:S(2)}) collective-permute-start(bf16[256,256]{1,0:T(8,128)(2,1)S(1)} %get-tuple-element.51), channel_id=1, source_target_pairs={{0,16},{1,17},{2,18},{3,19},{4,20},{5,21},{6,22},{7,23},{8,9},{9,8... | collective-permute-start | bytes 393224 | tf_op jit(solution)/shard_map/ppermute | solution.py:445
  27.3 0.6 %collective-permute-start.13 = (bf16[256,256]{1,0:T(8,128)(2,1)S(1)}, bf16[256,256]{1,0:T(8,128)(2,1)S(1)}, u32[]{:S(2)}, u32[]{:S(2)}) collective-permute-start(bf16[256,256]{1,0:T(8,128)(2,1)S(1)} %shard_map.98), channel_id=1, source_target_pairs={{0,1},{1,0},{2,3},{3,2},{4,5},{5,4},{6,7},{7,6},{8,24},{9,25},{10,... | collective-permute-start | bytes 393224 | tf_op jit(solution)/shard_map/ppermute | solution.py:452
  27.9 0.3 shard_map.96.keep_ref
  28.2 0.9 %collective-permute-done.14.stay_ref = bf16[256,256]{1,0:T(8,128)(2,1)S(1)} collective-permute-done((bf16[256,256]{1,0:T(8,128)(2,1)S(1)}, bf16[256,256]{1,0:T(8,128)(2,1)S(1)}, u32[]{:S(2)}, u32[]{:S(2)}) %collective-permute-start.14) | collective-permute-done | bytes 131104 | tf_op jit(solution)/shard_map/ppermute | solution.py:445
  29.1 0.1 collective-permute-done.16.come_ref
  29.3 1.6 %collective-permute-start.17 = (bf16[128,256]{1,0:T(8,128)(2,1)S(1)}, bf16[128,256]{1,0:T(8,128)(2,1)S(1)}, u32[]{:S(2)}, u32[]{:S(2)}) collective-permute-start(bf16[128,256]{1,0:T(8,128)(2,1)S(1)} %get-tuple-element.57), channel_id=1, source_target_pairs={{0,2},{1,3},{2,4},{3,5},{4,6},{5,7},{6,0},{7,1},{8,10},{9,11},{10,... | collective-permute-start | bytes 196616 | tf_op jit(solution)/shard_map/ppermute | solution.py:469
  30.9 2.6 %collective-permute-start.18 = (bf16[128,256]{1,0:T(8,128)(2,1)S(1)}, bf16[128,256]{1,0:T(8,128)(2,1)S(1)}, u32[]{:S(2)}, u32[]{:S(2)}) collective-permute-start(bf16[128,256]{1,0:T(8,128)(2,1)S(1)} %get-tuple-element.58), channel_id=1, source_target_pairs={{0,4},{1,5},{2,6},{3,7},{4,0},{5,1},{6,2},{7,3},{8,12},{9,13},{10,... | collective-permute-start | bytes 196616 | tf_op jit(solution)/shard_map/ppermute | solution.py:469
  33.5 0.0 collective-permute-done.11.stay_ref
  33.6 1.8 %collective-permute-done.17.refs_1_ = bf16[128,256]{1,0:T(8,128)(2,1)S(1)} collective-permute-done((bf16[128,256]{1,0:T(8,128)(2,1)S(1)}, bf16[128,256]{1,0:T(8,128)(2,1)S(1)}, u32[]{:S(2)}, u32[]{:S(2)}) %collective-permute-start.17) | collective-permute-done | bytes 65568 | tf_op jit(solution)/shard_map/ppermute | solution.py:469
  35.4 0.7 %collective-permute-done.18.refs_2_ = bf16[128,256]{1,0:T(8,128)(2,1)S(1)} collective-permute-done((bf16[128,256]{1,0:T(8,128)(2,1)S(1)}, bf16[128,256]{1,0:T(8,128)(2,1)S(1)}, u32[]{:S(2)}, u32[]{:S(2)}) %collective-permute-start.18) | collective-permute-done | bytes 65568 | tf_op jit(solution)/shard_map/ppermute | solution.py:469
  36.1 0.1 collective-permute-start.20
  36.2 2.5 %collective-permute-start.19 = (bf16[64,256]{1,0:T(8,128)(2,1)S(1)}, bf16[64,256]{1,0:T(8,128)(2,1)S(1)}, u32[]{:S(2)}, u32[]{:S(2)}) collective-permute-start(bf16[64,256]{1,0:T(8,128)(2,1)S(1)} %get-tuple-element.60), channel_id=1, source_target_pairs={{0,6},{1,7},{2,0},{3,1},{4,2},{5,3},{6,4},{7,5},{8,14},{9,15},{10,... | collective-permute-start | bytes 98312 | tf_op jit(solution)/shard_map/ppermute | solution.py:469
  38.7 1.4 %collective-permute-start.21 = (bf16[64,256]{1,0:T(8,128)(2,1)S(1)}, bf16[64,256]{1,0:T(8,128)(2,1)S(1)}, u32[]{:S(2)}, u32[]{:S(2)}) collective-permute-start(bf16[64,256]{1,0:T(8,128)(2,1)S(1)} %get-tuple-element.62), channel_id=1, source_target_pairs={{0,14},{1,15},{2,8},{3,9},{4,10},{5,11},{6,12},{7,13},{8,6},{9,7},... | collective-permute-start | bytes 98312 | tf_op jit(solution)/shard_map/ppermute | solution.py:471
  40.1 0.2 collective-permute-done.19.same_ref
  40.3 1.7 %collective-permute-done.21.cross_ref = bf16[64,256]{1,0:T(8,128)(2,1)S(1)} collective-permute-done((bf16[64,256]{1,0:T(8,128)(2,1)S(1)}, bf16[64,256]{1,0:T(8,128)(2,1)S(1)}, u32[]{:S(2)}, u32[]{:S(2)}) %collective-permute-start.21) | collective-permute-done | bytes 32800 | tf_op jit(solution)/shard_map/ppermute | solution.py:471
  42.0 0.7 %shard_map.103 = f32[64,512]{1,0:T(8,128)} custom-call(f32[64,256]{1,0:T(8,128)S(1)} %get-tuple-element.59.here_ref, bf16[64,256]{1,0:T(8,128)(2,1)S(1)} %collective-permute-done.19.same_ref, f32[64,256]{1,0:T(8,128)S(1)} %collective-permute-done.20.there_ref, bf16[64,256]{1,0:T(8,128)(2,1)S(1)} %collective-permute-done.21.cross_ref, f32[64,512]{1,0:T(8,128)S(1)} %copy-done), custom_call_target="tpu_custom_call" | custom-call | flops 1048576 | bytes 1048576 | tf_op jit(solution)/shard_map/pallas_call | solution.py:475
  (13 shorter events, 0.2 us)
Async XLA Ops:
  0.0 16.3 %collective-permute-start = (bf16[256,2048]{1,0:T(8,128)(2,1)}, bf16[256,2048]{1,0:T(8,128)(2,1)S(1)}, u32[]{:S(2)}, u32[]{:S(2)}) collective-permute-start(bf16[256,2048]{1,0:T(8,128)(2,1)} %bitcast.5), channel_id=1, source_target_pairs={{0,8},{8,0},{16,24},{24,16},{1,9},{9,1},{17,25},{25,17},{2,10},{10... | collective-permute-start | bytes 3145736 | tf_op jit(solution)/shard_map/ppermute | solution.py:30
  0.5 0.7 %copy-start.1 = (s32[1,16]{1,0:T(1,128)S(1)}, s32[1,16]{1,0:T(1,128)}, u32[]{:S(2)}) copy-start(s32[1,16]{1,0:T(1,128)} %refs_4_.1) | copy-start | bytes 196
  0.5 12.6 %collective-permute-start.5 = (bf16[256,512]{1,0:T(8,128)(2,1)}, bf16[256,512]{1,0:T(8,128)(2,1)S(1)}, u32[]{:S(2)}, u32[]{:S(2)}) collective-permute-start(bf16[256,512]{1,0:T(8,128)(2,1)} %bitcast.7), channel_id=1, source_target_pairs={{0,8},{8,0},{16,24},{24,16},{1,9},{9,1},{17,25},{25,17},{2,10},{10... | collective-permute-start | bytes 786440 | tf_op jit(solution)/shard_map/ppermute | solution.py:30
  0.6 12.5 %collective-permute-start.6 = (bf16[256,512]{1,0:T(8,128)(2,1)}, bf16[256,512]{1,0:T(8,128)(2,1)S(1)}, u32[]{:S(2)}, u32[]{:S(2)}) collective-permute-start(bf16[256,512]{1,0:T(8,128)(2,1)} %bitcast.9), channel_id=1, source_target_pairs={{0,8},{8,0},{16,24},{24,16},{1,9},{9,1},{17,25},{25,17},{2,10},{10... | collective-permute-start | bytes 786440 | tf_op jit(solution)/shard_map/ppermute | solution.py:30
  1.1 2.6 %collective-permute-start.9 = (s32[1,16]{1,0:T(1,128)S(1)}, s32[1,16]{1,0:T(1,128)S(1)}, u32[]{:S(2)}, u32[]{:S(2)}) collective-permute-start(s32[1,16]{1,0:T(1,128)S(1)} %copy-done.1), channel_id=1, source_target_pairs={{0,8},{8,0},{16,24},{24,16},{1,9},{9,1},{17,25},{25,17},{2,10},{10... | collective-permute-start | bytes 200 | tf_op jit(solution)/shard_map/ppermute | solution.py:30
  1.2 3.0 %collective-permute-start.7 = (bf16[16,2048]{1,0:T(8,128)(2,1)}, bf16[16,2048]{1,0:T(8,128)(2,1)S(1)}, u32[]{:S(2)}, u32[]{:S(2)}) collective-permute-start(bf16[16,2048]{1,0:T(8,128)(2,1)} %bitcast.11), channel_id=1, source_target_pairs={{0,8},{8,0},{16,24},{24,16},{1,9},{9,1},{17,25},{25,17},{2,10},{10... | collective-permute-start | bytes 196616 | tf_op jit(solution)/shard_map/ppermute | solution.py:30
  3.7 3.0 %collective-permute-start.8 = (bf16[16,2048]{1,0:T(8,128)(2,1)}, bf16[16,2048]{1,0:T(8,128)(2,1)S(1)}, u32[]{:S(2)}, u32[]{:S(2)}) collective-permute-start(bf16[16,2048]{1,0:T(8,128)(2,1)} %bitcast.14), channel_id=1, source_target_pairs={{0,8},{8,0},{16,24},{24,16},{1,9},{9,1},{17,25},{25,17},{2,10},{10... | collective-permute-start | bytes 196616 | tf_op jit(solution)/shard_map/ppermute | solution.py:30
  4.1 5.5 %collective-permute-start.1 = (bf16[16,2048]{1,0:T(8,128)(2,1)}, bf16[16,2048]{1,0:T(8,128)(2,1)S(1)}, u32[]{:S(2)}, u32[]{:S(2)}) collective-permute-start(bf16[16,2048]{1,0:T(8,128)(2,1)} %bitcast.12), channel_id=1, source_target_pairs={{0,16},{8,24},{16,0},{24,8},{1,17},{9,25},{17,1},{25,9},{2,18},{10... | collective-permute-start | bytes 196616 | tf_op jit(solution)/shard_map/ppermute | solution.py:30
  6.7 4.5 %collective-permute-start.3 = (bf16[16,2048]{1,0:T(8,128)(2,1)}, bf16[16,2048]{1,0:T(8,128)(2,1)S(1)}, u32[]{:S(2)}, u32[]{:S(2)}) collective-permute-start(bf16[16,2048]{1,0:T(8,128)(2,1)} %bitcast.15), channel_id=1, source_target_pairs={{0,16},{8,24},{16,0},{24,8},{1,17},{9,25},{17,1},{25,9},{2,18},{10... | collective-permute-start | bytes 196616 | tf_op jit(solution)/shard_map/ppermute | solution.py:30
  9.6 4.4 %collective-permute-start.2 = (bf16[16,2048]{1,0:T(8,128)(2,1)S(1)}, bf16[16,2048]{1,0:T(8,128)(2,1)S(1)}, u32[]{:S(2)}, u32[]{:S(2)}) collective-permute-start(bf16[16,2048]{1,0:T(8,128)(2,1)S(1)} %collective-permute-done.1.refs_0_), channel_id=1, source_target_pairs={{0,8},{8,0},{16,24},{24,16},{1,9},{9,1},{17,25},{25,17},{2,10},{10... | collective-permute-start | bytes 196616 | tf_op jit(solution)/shard_map/ppermute | solution.py:30
  11.2 2.7 %collective-permute-start.4 = (bf16[16,2048]{1,0:T(8,128)(2,1)S(1)}, bf16[16,2048]{1,0:T(8,128)(2,1)S(1)}, u32[]{:S(2)}, u32[]{:S(2)}) collective-permute-start(bf16[16,2048]{1,0:T(8,128)(2,1)S(1)} %collective-permute-done.3.refs_2_), channel_id=1, source_target_pairs={{0,8},{8,0},{16,24},{24,16},{1,9},{9,1},{17,25},{25,17},{2,10},{10... | collective-permute-start | bytes 196616 | tf_op jit(solution)/shard_map/ppermute | solution.py:30
  14.8 3.6 %collective-permute-start.10 = (f32[3,2,2,128]{3,2,1,0:T(2,128)S(1)}, f32[3,2,2,128]{3,2,1,0:T(2,128)S(1)}, u32[]{:S(2)}, u32[]{:S(2)}) collective-permute-start(f32[3,2,2,128]{3,2,1,0:T(2,128)S(1)} %get-tuple-element.41.mine_ref), channel_id=1, source_target_pairs={{0,16},{8,24},{16,0},{24,8},{1,17},{9,25},{17,1},{25,9},{2,18},{10... | collective-permute-start | bytes 18440 | tf_op jit(solution)/shard_map/ppermute | solution.py:30
  19.2 5.0 %collective-permute-start.15 = (bf16[256,256]{1,0:T(8,128)(2,1)S(1)}, bf16[256,256]{1,0:T(8,128)(2,1)S(1)}, u32[]{:S(2)}, u32[]{:S(2)}) collective-permute-start(bf16[256,256]{1,0:T(8,128)(2,1)S(1)} %get-tuple-element.56), channel_id=1, source_target_pairs={{0,16},{1,17},{2,18},{3,19},{4,20},{5,21},{6,22},{7,23},{8,9},{9,8... | collective-permute-start | bytes 393224 | tf_op jit(solution)/shard_map/ppermute | solution.py:445
  20.7 6.6 %collective-permute-start.12 = (bf16[256,256]{1,0:T(8,128)(2,1)S(1)}, bf16[256,256]{1,0:T(8,128)(2,1)S(1)}, u32[]{:S(2)}, u32[]{:S(2)}) collective-permute-start(bf16[256,256]{1,0:T(8,128)(2,1)S(1)} %get-tuple-element.53), channel_id=1, source_target_pairs={{0,16},{1,17},{2,18},{3,19},{4,20},{5,21},{6,22},{7,23},{8,9},{9,8... | collective-permute-start | bytes 393224 | tf_op jit(solution)/shard_map/ppermute | solution.py:445
  21.7 7.4 %collective-permute-start.14 = (bf16[256,256]{1,0:T(8,128)(2,1)S(1)}, bf16[256,256]{1,0:T(8,128)(2,1)S(1)}, u32[]{:S(2)}, u32[]{:S(2)}) collective-permute-start(bf16[256,256]{1,0:T(8,128)(2,1)S(1)} %get-tuple-element.55), channel_id=1, source_target_pairs={{0,16},{1,17},{2,18},{3,19},{4,20},{5,21},{6,22},{7,23},{8,9},{9,8... | collective-permute-start | bytes 393224 | tf_op jit(solution)/shard_map/ppermute | solution.py:445
  24.2 5.0 %collective-permute-start.16 = (bf16[256,256]{1,0:T(8,128)(2,1)S(1)}, bf16[256,256]{1,0:T(8,128)(2,1)S(1)}, u32[]{:S(2)}, u32[]{:S(2)}) collective-permute-start(bf16[256,256]{1,0:T(8,128)(2,1)S(1)} %shard_map.100), channel_id=1, source_target_pairs={{0,1},{1,0},{2,3},{3,2},{4,5},{5,4},{6,7},{7,6},{8,24},{9,25},{10,... | collective-permute-start | bytes 393224 | tf_op jit(solution)/shard_map/ppermute | solution.py:452
  25.8 7.7 %collective-permute-start.11 = (bf16[256,256]{1,0:T(8,128)(2,1)S(1)}, bf16[256,256]{1,0:T(8,128)(2,1)S(1)}, u32[]{:S(2)}, u32[]{:S(2)}) collective-permute-start(bf16[256,256]{1,0:T(8,128)(2,1)S(1)} %get-tuple-element.51), channel_id=1, source_target_pairs={{0,16},{1,17},{2,18},{3,19},{4,20},{5,21},{6,22},{7,23},{8,9},{9,8... | collective-permute-start | bytes 393224 | tf_op jit(solution)/shard_map/ppermute | solution.py:445
  27.3 6.2 %collective-permute-start.13 = (bf16[256,256]{1,0:T(8,128)(2,1)S(1)}, bf16[256,256]{1,0:T(8,128)(2,1)S(1)}, u32[]{:S(2)}, u32[]{:S(2)}) collective-permute-start(bf16[256,256]{1,0:T(8,128)(2,1)S(1)} %shard_map.98), channel_id=1, source_target_pairs={{0,1},{1,0},{2,3},{3,2},{4,5},{5,4},{6,7},{7,6},{8,24},{9,25},{10,... | collective-permute-start | bytes 393224 | tf_op jit(solution)/shard_map/ppermute | solution.py:452
  29.3 6.1 %collective-permute-start.17 = (bf16[128,256]{1,0:T(8,128)(2,1)S(1)}, bf16[128,256]{1,0:T(8,128)(2,1)S(1)}, u32[]{:S(2)}, u32[]{:S(2)}) collective-permute-start(bf16[128,256]{1,0:T(8,128)(2,1)S(1)} %get-tuple-element.57), channel_id=1, source_target_pairs={{0,2},{1,3},{2,4},{3,5},{4,6},{5,7},{6,0},{7,1},{8,10},{9,11},{10,... | collective-permute-start | bytes 196616 | tf_op jit(solution)/shard_map/ppermute | solution.py:469
  30.9 5.2 %collective-permute-start.18 = (bf16[128,256]{1,0:T(8,128)(2,1)S(1)}, bf16[128,256]{1,0:T(8,128)(2,1)S(1)}, u32[]{:S(2)}, u32[]{:S(2)}) collective-permute-start(bf16[128,256]{1,0:T(8,128)(2,1)S(1)} %get-tuple-element.58), channel_id=1, source_target_pairs={{0,4},{1,5},{2,6},{3,7},{4,0},{5,1},{6,2},{7,3},{8,12},{9,13},{10,... | collective-permute-start | bytes 196616 | tf_op jit(solution)/shard_map/ppermute | solution.py:469
  36.1 5.9 %copy-start = (f32[64,512]{1,0:T(8,128)S(1)}, f32[64,512]{1,0:T(8,128)}, u32[]{:S(2)}) copy-start(f32[64,512]{1,0:T(8,128)} %hessian_ref.1) | copy-start | bytes 393220
  36.1 5.9 %collective-permute-start.20 = (f32[64,256]{1,0:T(8,128)S(1)}, f32[64,256]{1,0:T(8,128)S(1)}, u32[]{:S(2)}, u32[]{:S(2)}) collective-permute-start(f32[64,256]{1,0:T(8,128)S(1)} %get-tuple-element.61), channel_id=1, source_target_pairs={{0,8},{8,0},{16,24},{24,16},{1,9},{9,1},{17,25},{25,17},{2,10},{10... | collective-permute-start | bytes 196616 | tf_op jit(solution)/shard_map/ppermute | solution.py:30
  36.2 4.0 %collective-permute-start.19 = (bf16[64,256]{1,0:T(8,128)(2,1)S(1)}, bf16[64,256]{1,0:T(8,128)(2,1)S(1)}, u32[]{:S(2)}, u32[]{:S(2)}) collective-permute-start(bf16[64,256]{1,0:T(8,128)(2,1)S(1)} %get-tuple-element.60), channel_id=1, source_target_pairs={{0,6},{1,7},{2,0},{3,1},{4,2},{5,3},{6,4},{7,5},{8,14},{9,15},{10,... | collective-permute-start | bytes 98312 | tf_op jit(solution)/shard_map/ppermute | solution.py:469
  38.7 3.3 %collective-permute-start.21 = (bf16[64,256]{1,0:T(8,128)(2,1)S(1)}, bf16[64,256]{1,0:T(8,128)(2,1)S(1)}, u32[]{:S(2)}, u32[]{:S(2)}) collective-permute-start(bf16[64,256]{1,0:T(8,128)(2,1)S(1)} %get-tuple-element.62), channel_id=1, source_target_pairs={{0,14},{1,15},{2,8},{3,9},{4,10},{5,11},{6,12},{7,13},{8,6},{9,7},... | collective-permute-start | bytes 98312 | tf_op jit(solution)/shard_map/ppermute | solution.py:471
